TPU v7x, 32 devices: a whole 2x2x4 slice. The times are simulated.
32 devices in a mesh: layer: 4 (over y, x), row: 2 (over core), col: 4 (over z).
Axes of the slice: x: 2, y: 2, z: 4, core: 2. Of those that a mesh axis runs over, the one named last changes fastest.
Arguments:
- block_values: bfloat16 [4, 2, 4, 32, 256, 256], P('layer', 'row', 'col'), may hold values from 0 to 3
- block_rows: int32 [4, 2, 4, 32], P('layer', 'row', 'col'), may hold values from 0 to 255
- block_cols: int32 [4, 2, 4, 32], P('layer', 'row', 'col'), may hold values from 0 to 127
- block_count: int32 [4, 2, 4], P('layer', 'row', 'col'), may hold values from 1 to 32, as said below
- dangling: int32 [4, 2, 4, 16384], P('layer', 'row', 'col'), may hold values 0 or 1
- start_ranks: float32 [4, 2, 4, 16384], P('layer', 'row', 'col'), may hold values from 0.2 to 5
Outputs:
- ranks: float32 [4, 2, 4, 16384], P('layer', 'row', 'col')
- residuals: float32 [3, 4], P(None, 'layer')
Inputs may be any that keep to these rules, and one draw needn't show every extreme that they name: `block_count`: live slots of a tile; in every layer some tile has all 32 slots live. `block_rows`: slots at or past a tile's count carry no edges; coordinates may repeat within a tile, and repeated blocks add.
All inputs are finite; a program needn't handle non-finite values. No bound on the sum of `dangling` on one device may be relied on, other than what follows from the above.
Results may differ from a plain program's by a relative error of at most 0.0012.
Values may be sent and summed in bfloat16 or wider, within the bound.
No kernel may reach another device: no remote copies, remote signals or barrier semaphores. Data moves between devices by JAX's collectives and lax.ppermute only.
A program may use at most 64 MiB of HBM per device.

v0:
```python
import functools
import jax
import jax.numpy as jnp
from jax import lax
from jax.experimental import pallas as pl
from jax.experimental.pallas import tpu as pltpu
from jax.sharding import PartitionSpec as P

ITERS = 3
damping = 0.85
coupling = 0.3

F32 = jnp.float32
BF16 = jnp.bfloat16
VMEM = pl.BlockSpec(memory_space=pltpu.VMEM)
HBM = pl.BlockSpec(memory_space=pltpu.HBM)
META = 8
CHUNKS = 4


def call(body, outs, specs, scratch=(), aliases={}):
    return pl.pallas_call(
        body,
        out_shape=outs,
        in_specs=specs,
        out_specs=(VMEM,) * len(outs) if isinstance(outs, tuple) else VMEM,
        scratch_shapes=scratch,
        input_output_aliases=aliases,
        compiler_params=pltpu.CompilerParams(vmem_limit_bytes=24 * 1024 * 1024),
    )


def two_terms(x):
    hi = x.astype(BF16)
    return hi, (x - hi.astype(F32)).astype(BF16)


def place(onehot, rows):
    hi, lo = two_terms(rows)
    return jnp.dot(onehot, hi, preferred_element_type=F32) + jnp.dot(
        onehot, lo, preferred_element_type=F32
    )


def to_blocks(ref, edge):
    wide = edge // 128
    count = ref.shape[0] // wide
    return jnp.concatenate([ref[pl.ds(w, count, wide), :] for w in range(wide)], axis=1)


def opening(values_h, cols_h, rows_h, count_h, x_h, dangling_h, packed, turned, pick, marks,
            values, cols, rows, count, x, dangling, sems):
    slots, edge, _ = values.shape
    blocks = x.shape[0] * 128 // edge
    step = slots // CHUNKS
    large = [
        pltpu.make_async_copy(
            values_h.at[pl.ds(k * step, step)], values.at[pl.ds(k * step, step)], sems.at[k]
        )
        for k in range(CHUNKS)
    ]
    pairs = ((cols_h, cols), (rows_h, rows), (count_h, count), (x_h, x), (dangling_h, dangling))
    small = [
        pltpu.make_async_copy(source, target, sems.at[CHUNKS + k])
        for k, (source, target) in enumerate(pairs)
    ]
    for copy in small + large:
        copy.start()
    for copy in small:
        copy.wait()
    live = lax.broadcasted_iota(jnp.int32, (1, slots), 1) < count[...]
    packed[0, slots : slots + META, :] = jnp.zeros((META, edge), F32)
    packed[0, slots : slots + 1, 0:slots] = jnp.where(live, cols[...], -1).astype(F32)
    marks[...] = jnp.zeros((META, edge), F32)
    marks[0:1, 0:slots] = jnp.where(live, rows[...], -1).astype(F32)
    source_ids = lax.broadcasted_iota(jnp.int32, (pick.shape[1], slots), 0)
    pick[...] = (source_ids == cols[...]).astype(F32).T.astype(BF16)
    at = slots + META
    packed[0, at : at + blocks, :] = to_blocks(x, edge)
    packed[0, at + blocks : at + 2 * blocks, :] = 1.0 - to_blocks(dangling, edge).astype(F32)
    ones = jnp.ones((16, edge), BF16)
    for k in range(CHUNKS):
        large[k].wait()
        for s in range(k * step, (k + 1) * step):
            block = values[s]
            turned[s] = block.T
            got = jnp.dot(ones, block, preferred_element_type=F32)
            packed[0, s : s + 1, :] = got[0:1, :]


def send_out(layers, pair_rows, x, inv, kinv, turned, pick, marks, payload, spill, xcur):
    slots = turned.shape[0]
    scaled = (x * kinv).astype(BF16)
    picked = jnp.dot(pick[...], scaled, preferred_element_type=F32).astype(BF16)
    group = 16
    for g in range(slots // group):
        lhs = picked[g * group : (g + 1) * group, :]
        for k in range(group):
            s = g * group + k
            got = jnp.dot(lhs, turned[s], preferred_element_type=F32)
            payload[s : s + 1, :] = got[k : k + 1, :]
    payload[slots : slots + META, :] = marks[...]
    payload[slots + 1 : slots + 2, :] = jnp.sum(x * inv, axis=0, keepdims=True)
    layer = lax.axis_index("layer")
    spread = jnp.where((layer == 0) | (layer == layers - 1), 1.0, 0.5).astype(F32) * coupling
    if x.shape[0] == pair_rows:
        own = x
    else:
        first_row = pl.multiple_of((lax.axis_index("row") // 2) * pair_rows, pair_rows)
        own = xcur[pl.ds(first_row, pair_rows), :]
    spill[...] = (own * spread).astype(BF16)


def first(layers, turned, pick, marks, *rest):
    shared, (payload, spill, xcur, inv_o, kinv_o) = rest[:-5], rest[-5:]
    slots = turned.shape[0]
    at = slots + META
    blocks = (shared[0].shape[1] - at) // 2
    if len(shared) == 1:
        parts = [(shared[0].at[r], r * blocks) for r in range(shared[0].shape[0])]
    else:
        row = lax.axis_index("row")
        starts = (row * blocks, (1 - row) * blocks)
        parts = [(ref.at[0], pl.multiple_of(at, blocks)) for ref, at in zip(shared, starts)]
    degree = None
    block_ids = lax.broadcasted_iota(jnp.int32, (xcur.shape[0], slots), 0).astype(F32)
    for ref, start in parts:
        onehot = (block_ids == ref[slots : slots + 1, 0:slots]).astype(BF16)
        part = place(onehot, ref[0:slots, :])
        degree = part if degree is None else degree + part
        mine = pl.ds(start, blocks)
        xcur[mine, :] = ref[at : at + blocks, :]
        kinv_o[mine, :] = ref[at + blocks : at + 2 * blocks, :]
    x, keep = xcur[...], kinv_o[...]
    inv = 1.0 / (keep * degree + 1.0)
    kinv = keep * inv
    inv_o[...] = inv
    kinv_o[...] = kinv
    send_out(layers, 2 * blocks, x, inv, kinv, turned, pick, marks, payload, spill, xcur)


def joined(parts):
    parts = [ref[k] for ref in parts for k in range(ref.shape[0])]
    pairs = [parts[2 * k] + parts[2 * k + 1] for k in range(len(parts) // 2)]
    return pairs[0] if len(pairs) == 1 else jnp.concatenate(pairs, axis=0)


def lane_change(x, xold):
    return jnp.sum(jnp.abs(x - xold[...]), axis=0, keepdims=True)


def middle(layers, turned, pick, marks, inv_i, kinv_i, xold, *rest):
    shared, (payload, spill, xcur) = rest[:-3], rest[-3:]
    slots = turned.shape[0]
    x = joined(shared)
    xcur[...] = x
    send_out(layers, shared[0].shape[1], x, inv_i[...], kinv_i[...], turned, pick, marks, payload,
             spill, xcur)
    payload[slots + 2 : slots + 3, :] = lane_change(x, xold)


def partial(layers, node_total, early, spill, *rest):
    pays, outs = (rest[:-1], rest[-1:]) if early else (rest[:-2], rest[-2:])
    part = outs[0]
    slots = pays[0].shape[0] - META
    blocks = part.shape[1] // 2
    odd = lax.axis_index("row") % 2
    first_block = (lax.axis_index("col") * blocks).astype(F32)
    block_ids = lax.broadcasted_iota(jnp.int32, (blocks, slots), 0).astype(F32) + first_block
    walks, sums = [], None
    for pay in pays:
        onehot = (block_ids == pay[slots : slots + 1, 0:slots]).astype(BF16)
        walks.append(place(onehot, pay[0:slots, :]))
        meta = pay[slots : slots + META, :]
        sums = meta if sums is None else sums + meta
    mass = jnp.sum(sums[1:2, :], axis=1, keepdims=True)
    if not early:
        outs[1][...] = sums
    end = jnp.where(odd == 0, layers - 1, 0)
    arrive = jnp.where(lax.axis_index("layer") == end, 0.0, damping * spill[...].astype(F32))
    walk = damping * (1.0 - coupling)
    own = walk * (walks[0] + mass / node_total) + (1.0 - damping)
    peer = walk * sum(walks[1:])
    part[0, 0:blocks, :] = arrive[0:blocks] + jnp.where(odd == 0, own, peer)
    part[0, blocks:, :] = arrive[blocks:] + jnp.where(odd == 0, peer, own)


def closing(xold, *rest):
    shared, (xnew, change) = rest[:-2], rest[-2:]
    x = joined(shared)
    xnew[...] = x
    change[...] = jnp.broadcast_to(lane_change(x, xold), change.shape)


def flatten(xnew, ranks):
    wide = xnew.shape[1] // 128
    blocks = ranks.shape[0] // wide
    start = pl.multiple_of(lax.axis_index("row") * blocks, blocks)
    own = xnew[pl.ds(start, blocks), :]
    for w in range(wide):
        ranks[pl.ds(w, blocks, wide), :] = own[:, w * 128 : (w + 1) * 128]


def totals(*refs):
    early, late, out = refs[: ITERS - 1], refs[ITERS - 1 : -1], refs[-1]
    rows = [ref[2:3, :] for ref in early] + [sum(ref[0:1, :] for ref in late)]
    for t, row in enumerate(rows):
        out[0:1, t : t + 1] = jnp.sum(row, axis=1, keepdims=True)


def to_others(x):
    rows, cols = lax.axis_size("row"), lax.axis_size("col")
    got = []
    for step in range(1, cols):
        pairs = []
        for row in range(rows):
            for col in range(cols):
                other = (col + step) % cols if cols & (cols - 1) else col ^ step
                pairs.append((row * cols + col, (row ^ 1) * cols + other))
        got.append(lax.ppermute(x, ("row", "col"), pairs))
    return got


def to_rows(x):
    rows = lax.axis_size("row")
    if rows == 2:
        return x, lax.ppermute(x, "row", [(0, 1), (1, 0)])
    return (lax.all_gather(x, "row", axis=0, tiled=True),)


def to_layers(spill):
    layers, rows = lax.axis_size("layer"), lax.axis_size("row")
    pairs = []
    for layer in range(layers):
        for row in range(rows):
            other = (layer + 1) % layers if row % 2 == 0 else (layer - 1) % layers
            pairs.append((layer * rows + row, other * rows + (row ^ 1)))
    return lax.ppermute(spill, ("layer", "row"), pairs)


def local(block_values, block_rows, block_cols, block_count, dangling, start_ranks):
    slots, edge = block_values.shape[3], block_values.shape[-1]
    span = start_ranks.shape[-1]
    row_devices = lax.axis_size("row")
    layers = lax.axis_size("layer")
    node_total = row_devices * lax.axis_size("col") * span
    blocks = span // edge
    col_blk = row_devices * blocks
    flat = (span // 128, 128)
    arguments = [
        block_values.reshape(slots, edge, edge), block_cols.reshape(1, slots),
        block_rows.reshape(1, slots), block_count.reshape(1, 1), start_ranks.reshape(flat),
        dangling.reshape(flat),
    ]
    arguments = [
        x if x.size == 1 else pltpu.with_memory_space_constraint(x, pltpu.HBM) for x in arguments
    ]

    def shape(n, dtype=F32):
        return jax.ShapeDtypeStruct((n, edge), dtype)

    def lead(n):
        return jax.ShapeDtypeStruct((1, n, edge), F32)

    packed, turned, pick, marks = call(
        opening,
        (lead(slots + META + 2 * blocks), pltpu.VMEM((slots, edge, edge), BF16),
         pltpu.VMEM((slots, col_blk), BF16), pltpu.VMEM((META, edge), F32)),
        (HBM, HBM, HBM, pl.BlockSpec(memory_space=pl.ANY), HBM, HBM),
        [pltpu.VMEM((slots, edge, edge), BF16), pltpu.VMEM((1, slots), jnp.int32),
         pltpu.VMEM((1, slots), jnp.int32), pltpu.VMEM((1, 1), jnp.int32), pltpu.VMEM(flat, F32),
         pltpu.VMEM(flat, jnp.int32), pltpu.SemaphoreType.DMA((5 + CHUNKS,))],
    )(*arguments)
    shared = to_rows(packed)
    sent = (shape(slots + META), shape(2 * blocks, BF16), shape(col_blk))
    payload, spill, x, inv, kinv = call(
        functools.partial(first, layers), sent + (shape(col_blk), shape(col_blk)),
        (VMEM,) * (3 + len(shared)),
    )(turned, pick, marks, *shared)
    changes = []
    for t in range(ITERS):
        if t:
            payload, spill, x = call(
                functools.partial(middle, layers), sent, (VMEM,) * (6 + len(shared)),
            )(turned, pick, marks, inv, kinv, x, *shared)
        arriving = to_layers(spill)
        others = to_others(payload)
        part, *change = call(
            functools.partial(partial, layers, node_total, t == 0),
            (lead(2 * blocks), shape(META))[: 1 + (t > 0)], (VMEM,) * (2 + len(others)),
        )(arriving, payload, *others)
        changes += change
        shared = to_rows(part)
    xnew, last = call(
        closing, (shape(col_blk), shape(META)), (VMEM,) * (1 + len(shared))
    )(x, *shared)
    lates = [last] + to_others(last)
    ranks = call(flatten, jax.ShapeDtypeStruct(flat, F32), (VMEM,))(xnew)
    residuals = call(
        totals, jax.ShapeDtypeStruct((1, ITERS), F32),
        (VMEM,) * (ITERS - 1 + len(lates)),
    )(*changes, *lates)
    return ranks.reshape(start_ranks.shape), residuals.reshape(ITERS, 1)


def solution(mesh):
    placed = (
        P("layer", "row", "col", None, None, None),
        P("layer", "row", "col", None),
        P("layer", "row", "col", None),
        P("layer", "row", "col"),
        P("layer", "row", "col", None),
        P("layer", "row", "col", None),
    )
    return jax.shard_map(
        local,
        mesh=mesh,
        in_specs=placed,
        out_specs=(P("layer", "row", "col", None), P(None, "layer")),
        check_vma=False,
    )
```

profile of v0, /device:TPU:1, one launch (start us, length us, event | category | flops | bytes accessed | tf_op | source)
XLA Modules:
  0.0 48.0 jit_solution(1985849025935746132)
XLA Ops:
  1.3 2.7 %shard_map.77 = (f32[1,168,256]{2,1,0:T(8,128)S(1)}, bf16[32,256,256]{2,1,0:T(8,128)(2,1)S(1)}, bf16[32,128]{1,0:T(8,128)(2,1)S(1)}, f32[8,256]{1,0:T(8,128)S(1)}) custom-call(bf16[32,256,256]{2,1,0:T(8,128)(2,1)} %bitcast.9, s32[1,32]{1,0:T(1,128)} %bitcast.13, s32[1,32]{1,0:T(1,128)} %bitcast.14, s32[1,1]{1,0:T(1,128)} %bitcast.8.count_h, ...), custom_call_target="tpu_custom_call" | custom-call | tf_op jit(solution)/shard_map/pallas_call | solution.py:265
  4.1 1.4 %collective-permute-done.rest_1_ = f32[1,168,256]{2,1,0:T(8,128)S(1)} collective-permute-done((f32[1,168,256]{2,1,0:T(8,128)S(1)}, f32[1,168,256]{2,1,0:T(8,128)S(1)}, u32[]{:S(2)}, u32[]{:S(2)}) %collective-permute-start) | collective-permute-done | bytes 172064 | tf_op jit(solution)/shard_map/ppermute | solution.py:227
  5.5 1.0 %shard_map.78 = (f32[40,256]{1,0:T(8,128)S(1)}, bf16[128,256]{1,0:T(8,128)(2,1)S(1)}, f32[128,256]{1,0:T(8,128)S(1)}, f32[128,256]{1,0:T(8,128)S(1)}, f32[128,256]{1,0:T(8,128)S(1)}) custom-call(bf16[32,256,256]{2,1,0:T(8,128)(2,1)S(1)} %get-tuple-element.23.turned, bf16[32,128]{1,0:T(8,128)(2,1)S(1)} %get-tuple-element.24.pick, ...), custom_call_target="tpu_custom_call" | custom-call | tf_op jit(solution)/shard_map/pallas_call | solution.py:276
  6.5 3.6 %collective-permute-start.1 = (bf16[128,256]{1,0:T(8,128)(2,1)S(1)}, bf16[128,256]{1,0:T(8,128)(2,1)S(1)}, u32[]{:S(2)}, u32[]{:S(2)}) collective-permute-start(bf16[128,256]{1,0:T(8,128)(2,1)S(1)} %get-tuple-element.30), channel_id=1, source_target_pairs={{0,12},{4,24},{8,20},{12,0},{16,28},{20,8},{24,4},{28,16},{1,13},{... | collective-permute-start | bytes 196616 | tf_op jit(solution)/shard_map/ppermute | solution.py:238
  10.1 2.4 %collective-permute-start.4 = (f32[40,256]{1,0:T(8,128)S(1)}, f32[40,256]{1,0:T(8,128)S(1)}, u32[]{:S(2)}, u32[]{:S(2)}) collective-permute-start(f32[40,256]{1,0:T(8,128)S(1)} %get-tuple-element.31.rest_0_), channel_id=1, source_target_pairs={{0,7},{1,6},{2,5},{3,4},{4,3},{5,2},{6,1},{7,0},{8,15},{9,14},{10,... | collective-permute-start | bytes 122888 | tf_op jit(solution)/shard_map/ppermute | solution.py:220
  12.5 0.4 collective-permute-start.3
  12.9 1.1 %collective-permute-start.2 = (f32[40,256]{1,0:T(8,128)S(1)}, f32[40,256]{1,0:T(8,128)S(1)}, u32[]{:S(2)}, u32[]{:S(2)}) collective-permute-start(f32[40,256]{1,0:T(8,128)S(1)} %get-tuple-element.31.rest_0_), channel_id=1, source_target_pairs={{0,5},{1,4},{2,7},{3,6},{4,1},{5,0},{6,3},{7,2},{8,13},{9,12},{10,... | collective-permute-start | bytes 122888 | tf_op jit(solution)/shard_map/ppermute | solution.py:220
  14.0 1.4 %collective-permute-done.4.rest_3_ = f32[40,256]{1,0:T(8,128)S(1)} collective-permute-done((f32[40,256]{1,0:T(8,128)S(1)}, f32[40,256]{1,0:T(8,128)S(1)}, u32[]{:S(2)}, u32[]{:S(2)}) %collective-permute-start.4) | collective-permute-done | bytes 40992 | tf_op jit(solution)/shard_map/ppermute | solution.py:220
  15.3 1.6 %collective-permute-done.3.rest_2_ = f32[40,256]{1,0:T(8,128)S(1)} collective-permute-done((f32[40,256]{1,0:T(8,128)S(1)}, f32[40,256]{1,0:T(8,128)S(1)}, u32[]{:S(2)}, u32[]{:S(2)}) %collective-permute-start.3) | collective-permute-done | bytes 40992 | tf_op jit(solution)/shard_map/ppermute | solution.py:220
  17.2 1.4 %collective-permute-start.5 = (f32[1,128,256]{2,1,0:T(8,128)S(1)}, f32[1,128,256]{2,1,0:T(8,128)S(1)}, u32[]{:S(2)}, u32[]{:S(2)}) collective-permute-start(f32[1,128,256]{2,1,0:T(8,128)S(1)} %shard_map.79.rest_0_), channel_id=1, source_target_pairs={{0,4},{4,0},{1,5},{5,1},{2,6},{6,2},{3,7},{7,3},{8,12},{12,8},{9,1... | collective-permute-start | bytes 393224 | tf_op jit(solution)/shard_map/ppermute | solution.py:227
  18.6 1.0 %collective-permute-done.5.rest_1_ = f32[1,128,256]{2,1,0:T(8,128)S(1)} collective-permute-done((f32[1,128,256]{2,1,0:T(8,128)S(1)}, f32[1,128,256]{2,1,0:T(8,128)S(1)}, u32[]{:S(2)}, u32[]{:S(2)}) %collective-permute-start.5) | collective-permute-done | bytes 131104 | tf_op jit(solution)/shard_map/ppermute | solution.py:227
  19.6 0.8 %shard_map.80 = (f32[40,256]{1,0:T(8,128)S(1)}, bf16[128,256]{1,0:T(8,128)(2,1)S(1)}, f32[128,256]{1,0:T(8,128)S(1)}) custom-call(bf16[32,256,256]{2,1,0:T(8,128)(2,1)S(1)} %get-tuple-element.23.turned, bf16[32,128]{1,0:T(8,128)(2,1)S(1)} %get-tuple-element.24.pick, f32[8,256]{1,0:T(8,128)S(1)} %get-tuple-element.25.marks, ...), custom_call_target="tpu_custom_call" | custom-call | tf_op jit(solution)/shard_map/pallas_call | solution.py:283
  20.3 0.6 %collective-permute-start.6 = (bf16[128,256]{1,0:T(8,128)(2,1)S(1)}, bf16[128,256]{1,0:T(8,128)(2,1)S(1)}, u32[]{:S(2)}, u32[]{:S(2)}) collective-permute-start(bf16[128,256]{1,0:T(8,128)(2,1)S(1)} %get-tuple-element.33), channel_id=1, source_target_pairs={{0,12},{4,24},{8,20},{12,0},{16,28},{20,8},{24,4},{28,16},{1,13},{... | collective-permute-start | bytes 196616 | tf_op jit(solution)/shard_map/ppermute | solution.py:238
  20.9 2.0 %collective-permute-start.9 = (f32[40,256]{1,0:T(8,128)S(1)}, f32[40,256]{1,0:T(8,128)S(1)}, u32[]{:S(2)}, u32[]{:S(2)}) collective-permute-start(f32[40,256]{1,0:T(8,128)S(1)} %get-tuple-element.34.rest_0_), channel_id=1, source_target_pairs={{0,7},{1,6},{2,5},{3,4},{4,3},{5,2},{6,1},{7,0},{8,15},{9,14},{10,... | collective-permute-start | bytes 122888 | tf_op jit(solution)/shard_map/ppermute | solution.py:220
  22.9 1.7 %collective-permute-start.7 = (f32[40,256]{1,0:T(8,128)S(1)}, f32[40,256]{1,0:T(8,128)S(1)}, u32[]{:S(2)}, u32[]{:S(2)}) collective-permute-start(f32[40,256]{1,0:T(8,128)S(1)} %get-tuple-element.34.rest_0_), channel_id=1, source_target_pairs={{0,5},{1,4},{2,7},{3,6},{4,1},{5,0},{6,3},{7,2},{8,13},{9,12},{10,... | collective-permute-start | bytes 122888 | tf_op jit(solution)/shard_map/ppermute | solution.py:220
  24.6 1.9 %collective-permute-done.9.rest_3_ = f32[40,256]{1,0:T(8,128)S(1)} collective-permute-done((f32[40,256]{1,0:T(8,128)S(1)}, f32[40,256]{1,0:T(8,128)S(1)}, u32[]{:S(2)}, u32[]{:S(2)}) %collective-permute-start.9) | collective-permute-done | bytes 40992 | tf_op jit(solution)/shard_map/ppermute | solution.py:220
  26.5 1.7 %collective-permute-done.8.rest_2_ = f32[40,256]{1,0:T(8,128)S(1)} collective-permute-done((f32[40,256]{1,0:T(8,128)S(1)}, f32[40,256]{1,0:T(8,128)S(1)}, u32[]{:S(2)}, u32[]{:S(2)}) %collective-permute-start.8) | collective-permute-done | bytes 40992 | tf_op jit(solution)/shard_map/ppermute | solution.py:220
  28.4 0.5 collective-permute-start.10
  28.9 1.0 %collective-permute-done.10.rest_1_ = f32[1,128,256]{2,1,0:T(8,128)S(1)} collective-permute-done((f32[1,128,256]{2,1,0:T(8,128)S(1)}, f32[1,128,256]{2,1,0:T(8,128)S(1)}, u32[]{:S(2)}, u32[]{:S(2)}) %collective-permute-start.10) | collective-permute-done | bytes 131104 | tf_op jit(solution)/shard_map/ppermute | solution.py:227
  29.9 0.8 %shard_map.82 = (f32[40,256]{1,0:T(8,128)S(1)}, bf16[128,256]{1,0:T(8,128)(2,1)S(1)}, f32[128,256]{1,0:T(8,128)S(1)}) custom-call(bf16[32,256,256]{2,1,0:T(8,128)(2,1)S(1)} %get-tuple-element.23.turned, bf16[32,128]{1,0:T(8,128)(2,1)S(1)} %get-tuple-element.24.pick, f32[8,256]{1,0:T(8,128)S(1)} %get-tuple-element.25.marks, ...), custom_call_target="tpu_custom_call" | custom-call | tf_op jit(solution)/shard_map/pallas_call | solution.py:283
  30.6 1.5 %collective-permute-start.11 = (bf16[128,256]{1,0:T(8,128)(2,1)S(1)}, bf16[128,256]{1,0:T(8,128)(2,1)S(1)}, u32[]{:S(2)}, u32[]{:S(2)}) collective-permute-start(bf16[128,256]{1,0:T(8,128)(2,1)S(1)} %get-tuple-element.37), channel_id=1, source_target_pairs={{0,12},{4,24},{8,20},{12,0},{16,28},{20,8},{24,4},{28,16},{1,13},{... | collective-permute-start | bytes 196616 | tf_op jit(solution)/shard_map/ppermute | solution.py:238
  32.1 2.2 %collective-permute-start.14 = (f32[40,256]{1,0:T(8,128)S(1)}, f32[40,256]{1,0:T(8,128)S(1)}, u32[]{:S(2)}, u32[]{:S(2)}) collective-permute-start(f32[40,256]{1,0:T(8,128)S(1)} %get-tuple-element.38.rest_0_), channel_id=1, source_target_pairs={{0,7},{1,6},{2,5},{3,4},{4,3},{5,2},{6,1},{7,0},{8,15},{9,14},{10,... | collective-permute-start | bytes 122888 | tf_op jit(solution)/shard_map/ppermute | solution.py:220
  34.3 1.8 %collective-permute-start.12 = (f32[40,256]{1,0:T(8,128)S(1)}, f32[40,256]{1,0:T(8,128)S(1)}, u32[]{:S(2)}, u32[]{:S(2)}) collective-permute-start(f32[40,256]{1,0:T(8,128)S(1)} %get-tuple-element.38.rest_0_), channel_id=1, source_target_pairs={{0,5},{1,4},{2,7},{3,6},{4,1},{5,0},{6,3},{7,2},{8,13},{9,12},{10,... | collective-permute-start | bytes 122888 | tf_op jit(solution)/shard_map/ppermute | solution.py:220
  36.0 1.4 %collective-permute-done.14.rest_3_ = f32[40,256]{1,0:T(8,128)S(1)} collective-permute-done((f32[40,256]{1,0:T(8,128)S(1)}, f32[40,256]{1,0:T(8,128)S(1)}, u32[]{:S(2)}, u32[]{:S(2)}) %collective-permute-start.14) | collective-permute-done | bytes 40992 | tf_op jit(solution)/shard_map/ppermute | solution.py:220
  37.4 1.9 %collective-permute-done.13.rest_2_ = f32[40,256]{1,0:T(8,128)S(1)} collective-permute-done((f32[40,256]{1,0:T(8,128)S(1)}, f32[40,256]{1,0:T(8,128)S(1)}, u32[]{:S(2)}, u32[]{:S(2)}) %collective-permute-start.13) | collective-permute-done | bytes 40992 | tf_op jit(solution)/shard_map/ppermute | solution.py:220
  39.6 0.5 collective-permute-start.15
  40.1 1.0 %collective-permute-done.15.rest_1_ = f32[1,128,256]{2,1,0:T(8,128)S(1)} collective-permute-done((f32[1,128,256]{2,1,0:T(8,128)S(1)}, f32[1,128,256]{2,1,0:T(8,128)S(1)}, u32[]{:S(2)}, u32[]{:S(2)}) %collective-permute-start.15) | collective-permute-done | bytes 131104 | tf_op jit(solution)/shard_map/ppermute | solution.py:227
  41.1 2.3 %collective-permute-start.18 = (f32[8,256]{1,0:T(8,128)S(1)}, f32[8,256]{1,0:T(8,128)S(1)}, u32[]{:S(2)}, u32[]{:S(2)}) collective-permute-start(f32[8,256]{1,0:T(8,128)S(1)} %get-tuple-element.43.refs_2_), channel_id=1, source_target_pairs={{0,7},{1,6},{2,5},{3,4},{4,3},{5,2},{6,1},{7,0},{8,15},{9,14},{10,... | collective-permute-start | bytes 24584 | tf_op jit(solution)/shard_map/ppermute | solution.py:220
  43.4 1.8 %collective-permute-start.16 = (f32[8,256]{1,0:T(8,128)S(1)}, f32[8,256]{1,0:T(8,128)S(1)}, u32[]{:S(2)}, u32[]{:S(2)}) collective-permute-start(f32[8,256]{1,0:T(8,128)S(1)} %get-tuple-element.43.refs_2_), channel_id=1, source_target_pairs={{0,5},{1,4},{2,7},{3,6},{4,1},{5,0},{6,3},{7,2},{8,13},{9,12},{10,... | collective-permute-start | bytes 24584 | tf_op jit(solution)/shard_map/ppermute | solution.py:220
  45.2 0.6 %shard_map.85 = f32[128,128]{1,0:T(8,128)} custom-call(f32[128,256]{1,0:T(8,128)S(1)} %get-tuple-element.40.xnew), custom_call_target="tpu_custom_call" | custom-call | tf_op jit(solution)/shard_map/pallas_call | solution.py:298
  46.1 1.3 %collective-permute-done.17.refs_4_ = f32[8,256]{1,0:T(8,128)S(1)} collective-permute-done((f32[8,256]{1,0:T(8,128)S(1)}, f32[8,256]{1,0:T(8,128)S(1)}, u32[]{:S(2)}, u32[]{:S(2)}) %collective-permute-start.17) | collective-permute-done | bytes 8224 | tf_op jit(solution)/shard_map/ppermute | solution.py:220
  47.4 0.6 %shard_map.86 = f32[1,3]{1,0:T(1,128)} custom-call(f32[8,256]{1,0:T(8,128)S(1)} %get-tuple-element.41.refs_0_, f32[8,256]{1,0:T(8,128)S(1)} %get-tuple-element.42.refs_1_, f32[8,256]{1,0:T(8,128)S(1)} %get-tuple-element.43.refs_2_, f32[8,256]{1,0:T(8,128)S(1)} %collective-permute-done.16.refs_3_, f32[8,256]{1,0:T(8,128)S(1)} %collective-permute-done.17.refs_4_, ...), custom_call_target="tpu_custom_call" | custom-call | tf_op jit(solution)/shard_map/pallas_call | solution.py:299
  (16 shorter events, 1.0 us)
Async XLA Ops:
  4.0 1.5 %collective-permute-start = (f32[1,168,256]{2,1,0:T(8,128)S(1)}, f32[1,168,256]{2,1,0:T(8,128)S(1)}, u32[]{:S(2)}, u32[]{:S(2)}) collective-permute-start(f32[1,168,256]{2,1,0:T(8,128)S(1)} %get-tuple-element.26.rest_0_), channel_id=1, source_target_pairs={{0,4},{4,0},{1,5},{5,1},{2,6},{6,2},{3,7},{7,3},{8,12},{12,8},{9,1... | collective-permute-start | bytes 516104 | tf_op jit(solution)/shard_map/ppermute | solution.py:227
  6.5 10.5 %collective-permute-start.1 = (bf16[128,256]{1,0:T(8,128)(2,1)S(1)}, bf16[128,256]{1,0:T(8,128)(2,1)S(1)}, u32[]{:S(2)}, u32[]{:S(2)}) collective-permute-start(bf16[128,256]{1,0:T(8,128)(2,1)S(1)} %get-tuple-element.30), channel_id=1, source_target_pairs={{0,12},{4,24},{8,20},{12,0},{16,28},{20,8},{24,4},{28,16},{1,13},{... | collective-permute-start | bytes 196616 | tf_op jit(solution)/shard_map/ppermute | solution.py:238
  10.1 5.3 %collective-permute-start.4 = (f32[40,256]{1,0:T(8,128)S(1)}, f32[40,256]{1,0:T(8,128)S(1)}, u32[]{:S(2)}, u32[]{:S(2)}) collective-permute-start(f32[40,256]{1,0:T(8,128)S(1)} %get-tuple-element.31.rest_0_), channel_id=1, source_target_pairs={{0,7},{1,6},{2,5},{3,4},{4,3},{5,2},{6,1},{7,0},{8,15},{9,14},{10,... | collective-permute-start | bytes 122888 | tf_op jit(solution)/shard_map/ppermute | solution.py:220
  12.5 4.5 %collective-permute-start.3 = (f32[40,256]{1,0:T(8,128)S(1)}, f32[40,256]{1,0:T(8,128)S(1)}, u32[]{:S(2)}, u32[]{:S(2)}) collective-permute-start(f32[40,256]{1,0:T(8,128)S(1)} %get-tuple-element.31.rest_0_), channel_id=1, source_target_pairs={{0,6},{1,7},{2,4},{3,5},{4,2},{5,3},{6,0},{7,1},{8,14},{9,15},{10,... | collective-permute-start | bytes 122888 | tf_op jit(solution)/shard_map/ppermute | solution.py:220
  12.9 4.1 %collective-permute-start.2 = (f32[40,256]{1,0:T(8,128)S(1)}, f32[40,256]{1,0:T(8,128)S(1)}, u32[]{:S(2)}, u32[]{:S(2)}) collective-permute-start(f32[40,256]{1,0:T(8,128)S(1)} %get-tuple-element.31.rest_0_), channel_id=1, source_target_pairs={{0,5},{1,4},{2,7},{3,6},{4,1},{5,0},{6,3},{7,2},{8,13},{9,12},{10,... | collective-permute-start | bytes 122888 | tf_op jit(solution)/shard_map/ppermute | solution.py:220
  17.2 2.4 %collective-permute-start.5 = (f32[1,128,256]{2,1,0:T(8,128)S(1)}, f32[1,128,256]{2,1,0:T(8,128)S(1)}, u32[]{:S(2)}, u32[]{:S(2)}) collective-permute-start(f32[1,128,256]{2,1,0:T(8,128)S(1)} %shard_map.79.rest_0_), channel_id=1, source_target_pairs={{0,4},{4,0},{1,5},{5,1},{2,6},{6,2},{3,7},{7,3},{8,12},{12,8},{9,1... | collective-permute-start | bytes 393224 | tf_op jit(solution)/shard_map/ppermute | solution.py:227
  20.3 7.8 %collective-permute-start.6 = (bf16[128,256]{1,0:T(8,128)(2,1)S(1)}, bf16[128,256]{1,0:T(8,128)(2,1)S(1)}, u32[]{:S(2)}, u32[]{:S(2)}) collective-permute-start(bf16[128,256]{1,0:T(8,128)(2,1)S(1)} %get-tuple-element.33), channel_id=1, source_target_pairs={{0,12},{4,24},{8,20},{12,0},{16,28},{20,8},{24,4},{28,16},{1,13},{... | collective-permute-start | bytes 196616 | tf_op jit(solution)/shard_map/ppermute | solution.py:238
  20.9 5.5 %collective-permute-start.9 = (f32[40,256]{1,0:T(8,128)S(1)}, f32[40,256]{1,0:T(8,128)S(1)}, u32[]{:S(2)}, u32[]{:S(2)}) collective-permute-start(f32[40,256]{1,0:T(8,128)S(1)} %get-tuple-element.34.rest_0_), channel_id=1, source_target_pairs={{0,7},{1,6},{2,5},{3,4},{4,3},{5,2},{6,1},{7,0},{8,15},{9,14},{10,... | collective-permute-start | bytes 122888 | tf_op jit(solution)/shard_map/ppermute | solution.py:220
  22.9 5.2 %collective-permute-start.8 = (f32[40,256]{1,0:T(8,128)S(1)}, f32[40,256]{1,0:T(8,128)S(1)}, u32[]{:S(2)}, u32[]{:S(2)}) collective-permute-start(f32[40,256]{1,0:T(8,128)S(1)} %get-tuple-element.34.rest_0_), channel_id=1, source_target_pairs={{0,6},{1,7},{2,4},{3,5},{4,2},{5,3},{6,0},{7,1},{8,14},{9,15},{10,... | collective-permute-start | bytes 122888 | tf_op jit(solution)/shard_map/ppermute | solution.py:220
  22.9 5.2 %collective-permute-start.7 = (f32[40,256]{1,0:T(8,128)S(1)}, f32[40,256]{1,0:T(8,128)S(1)}, u32[]{:S(2)}, u32[]{:S(2)}) collective-permute-start(f32[40,256]{1,0:T(8,128)S(1)} %get-tuple-element.34.rest_0_), channel_id=1, source_target_pairs={{0,5},{1,4},{2,7},{3,6},{4,1},{5,0},{6,3},{7,2},{8,13},{9,12},{10,... | collective-permute-start | bytes 122888 | tf_op jit(solution)/shard_map/ppermute | solution.py:220
  28.4 1.4 %collective-permute-start.10 = (f32[1,128,256]{2,1,0:T(8,128)S(1)}, f32[1,128,256]{2,1,0:T(8,128)S(1)}, u32[]{:S(2)}, u32[]{:S(2)}) collective-permute-start(f32[1,128,256]{2,1,0:T(8,128)S(1)} %get-tuple-element.35.rest_0_), channel_id=1, source_target_pairs={{0,4},{4,0},{1,5},{5,1},{2,6},{6,2},{3,7},{7,3},{8,12},{12,8},{9,1... | collective-permute-start | bytes 393224 | tf_op jit(solution)/shard_map/ppermute | solution.py:227
  30.6 8.7 %collective-permute-start.11 = (bf16[128,256]{1,0:T(8,128)(2,1)S(1)}, bf16[128,256]{1,0:T(8,128)(2,1)S(1)}, u32[]{:S(2)}, u32[]{:S(2)}) collective-permute-start(bf16[128,256]{1,0:T(8,128)(2,1)S(1)} %get-tuple-element.37), channel_id=1, source_target_pairs={{0,12},{4,24},{8,20},{12,0},{16,28},{20,8},{24,4},{28,16},{1,13},{... | collective-permute-start | bytes 196616 | tf_op jit(solution)/shard_map/ppermute | solution.py:238
  32.1 5.3 %collective-permute-start.14 = (f32[40,256]{1,0:T(8,128)S(1)}, f32[40,256]{1,0:T(8,128)S(1)}, u32[]{:S(2)}, u32[]{:S(2)}) collective-permute-start(f32[40,256]{1,0:T(8,128)S(1)} %get-tuple-element.38.rest_0_), channel_id=1, source_target_pairs={{0,7},{1,6},{2,5},{3,4},{4,3},{5,2},{6,1},{7,0},{8,15},{9,14},{10,... | collective-permute-start | bytes 122888 | tf_op jit(solution)/shard_map/ppermute | solution.py:220
  34.3 5.1 %collective-permute-start.13 = (f32[40,256]{1,0:T(8,128)S(1)}, f32[40,256]{1,0:T(8,128)S(1)}, u32[]{:S(2)}, u32[]{:S(2)}) collective-permute-start(f32[40,256]{1,0:T(8,128)S(1)} %get-tuple-element.38.rest_0_), channel_id=1, source_target_pairs={{0,6},{1,7},{2,4},{3,5},{4,2},{5,3},{6,0},{7,1},{8,14},{9,15},{10,... | collective-permute-start | bytes 122888 | tf_op jit(solution)/shard_map/ppermute | solution.py:220
  34.3 5.1 %collective-permute-start.12 = (f32[40,256]{1,0:T(8,128)S(1)}, f32[40,256]{1,0:T(8,128)S(1)}, u32[]{:S(2)}, u32[]{:S(2)}) collective-permute-start(f32[40,256]{1,0:T(8,128)S(1)} %get-tuple-element.38.rest_0_), channel_id=1, source_target_pairs={{0,5},{1,4},{2,7},{3,6},{4,1},{5,0},{6,3},{7,2},{8,13},{9,12},{10,... | collective-permute-start | bytes 122888 | tf_op jit(solution)/shard_map/ppermute | solution.py:220
  39.6 1.4 %collective-permute-start.15 = (f32[1,128,256]{2,1,0:T(8,128)S(1)}, f32[1,128,256]{2,1,0:T(8,128)S(1)}, u32[]{:S(2)}, u32[]{:S(2)}) collective-permute-start(f32[1,128,256]{2,1,0:T(8,128)S(1)} %get-tuple-element.39.rest_0_), channel_id=1, source_target_pairs={{0,4},{4,0},{1,5},{5,1},{2,6},{6,2},{3,7},{7,3},{8,12},{12,8},{9,1... | collective-permute-start | bytes 393224 | tf_op jit(solution)/shard_map/ppermute | solution.py:227
  41.1 5.0 %collective-permute-start.18 = (f32[8,256]{1,0:T(8,128)S(1)}, f32[8,256]{1,0:T(8,128)S(1)}, u32[]{:S(2)}, u32[]{:S(2)}) collective-permute-start(f32[8,256]{1,0:T(8,128)S(1)} %get-tuple-element.43.refs_2_), channel_id=1, source_target_pairs={{0,7},{1,6},{2,5},{3,4},{4,3},{5,2},{6,1},{7,0},{8,15},{9,14},{10,... | collective-permute-start | bytes 24584 | tf_op jit(solution)/shard_map/ppermute | solution.py:220
  43.4 4.0 %collective-permute-start.17 = (f32[8,256]{1,0:T(8,128)S(1)}, f32[8,256]{1,0:T(8,128)S(1)}, u32[]{:S(2)}, u32[]{:S(2)}) collective-permute-start(f32[8,256]{1,0:T(8,128)S(1)} %get-tuple-element.43.refs_2_), channel_id=1, source_target_pairs={{0,6},{1,7},{2,4},{3,5},{4,2},{5,3},{6,0},{7,1},{8,14},{9,15},{10,... | collective-permute-start | bytes 24584 | tf_op jit(solution)/shard_map/ppermute | solution.py:220
  43.4 4.0 %collective-permute-start.16 = (f32[8,256]{1,0:T(8,128)S(1)}, f32[8,256]{1,0:T(8,128)S(1)}, u32[]{:S(2)}, u32[]{:S(2)}) collective-permute-start(f32[8,256]{1,0:T(8,128)S(1)} %get-tuple-element.43.refs_2_), channel_id=1, source_target_pairs={{0,5},{1,4},{2,7},{3,6},{4,1},{5,0},{6,3},{7,2},{8,13},{9,12},{10,... | collective-permute-start | bytes 24584 | tf_op jit(solution)/shard_map/ppermute | solution.py:220
where the time goes:
time: 48.3 us; the launch traced here: 48 us
  starting transfers between devices  23.7 us (49%)
  waiting for transfers between devices  15.8 us (33%)
  Pallas kernels  7.17 us (15%)
  between operations  1.35 us (3%)
    ppermute x12, starting transfers between devices, to_others(): got.append(lax.ppermute(x, ('row', 'col'), pairs))  15.6 us
    ppermute x12, waiting for transfers between devices, to_others(): got.append(lax.ppermute(x, ('row', 'col'), pairs))  11.4 us
    ppermute x3, starting transfers between devices, to_layers(): return lax.ppermute(spill, ('layer', 'row'), pairs)  5.7 us
    ppermute x4, waiting for transfers between devices, to_rows(): return (x, lax.ppermute(x, 'row', [(0, 1), (1, 0)]))  4.35 us
    pallas_call x1, Pallas kernels, local(): call(opening, (lead(slots + META + 2 * blocks), pltpu.VMEM((slots, edge,...  2.72 us
    ppermute x4, starting transfers between devices, to_rows(): return (x, lax.ppermute(x, 'row', [(0, 1), (1, 0)]))  2.37 us
    pallas_call x2, Pallas kernels, local(): call(functools.partial(middle, layers), sent, (VMEM,) * (6 + len(shared)))  1.53 us
    pallas_call x1, Pallas kernels, local(): call(functools.partial(first, layers), sent + (shape(col_blk), shape(col_...  0.99 us
  transfers between devices with their start and end apart: 19, of which 12 were waited for; matrix products, arithmetic and copies ran while one was open for 0% of the time, Pallas kernels for 1%

commit v1 on v0

--- a/solution.py
+++ b/solution.py
@@ -15,6 +15,7 @@
 VMEM = pl.BlockSpec(memory_space=pltpu.VMEM)
 HBM = pl.BlockSpec(memory_space=pltpu.HBM)
 META = 8
+LANES = 128
 CHUNKS = 4
 
 
@@ -71,7 +72,7 @@
     live = lax.broadcasted_iota(jnp.int32, (1, slots), 1) < count[...]
     packed[0, slots : slots + META, :] = jnp.zeros((META, edge), F32)
     packed[0, slots : slots + 1, 0:slots] = jnp.where(live, cols[...], -1).astype(F32)
-    marks[...] = jnp.zeros((META, edge), F32)
+    marks[...] = jnp.zeros((META, LANES), F32)
     marks[0:1, 0:slots] = jnp.where(live, rows[...], -1).astype(F32)
     source_ids = lax.broadcasted_iota(jnp.int32, (pick.shape[1], slots), 0)
     pick[...] = (source_ids == cols[...]).astype(F32).T.astype(BF16)
@@ -89,7 +90,7 @@
 
 
 def send_out(layers, pair_rows, x, inv, kinv, turned, pick, marks, payload, spill, xcur):
-    slots = turned.shape[0]
+    slots, wide = turned.shape[0], turned.shape[1] // LANES
     scaled = (x * kinv).astype(BF16)
     picked = jnp.dot(pick[...], scaled, preferred_element_type=F32).astype(BF16)
     group = 16
@@ -98,9 +99,12 @@
         for k in range(group):
             s = g * group + k
             got = jnp.dot(lhs, turned[s], preferred_element_type=F32)
-            payload[s : s + 1, :] = got[k : k + 1, :]
-    payload[slots : slots + META, :] = marks[...]
-    payload[slots + 1 : slots + 2, :] = jnp.sum(x * inv, axis=0, keepdims=True)
+            for w in range(wide):
+                at = w * slots + s
+                payload[at : at + 1, :] = got[k : k + 1, w * LANES : (w + 1) * LANES]
+    meta = wide * slots
+    payload[meta : meta + META, :] = marks[...]
+    payload[meta + 1 : meta + 2, :] = lane_sum(x * inv)
     layer = lax.axis_index("layer")
     spread = jnp.where((layer == 0) | (layer == layers - 1), 1.0, 0.5).astype(F32) * coupling
     if x.shape[0] == pair_rows:
@@ -145,34 +149,37 @@
     return pairs[0] if len(pairs) == 1 else jnp.concatenate(pairs, axis=0)
 
 
-def lane_change(x, xold):
-    return jnp.sum(jnp.abs(x - xold[...]), axis=0, keepdims=True)
+def lane_sum(x):
+    row = jnp.sum(x, axis=0, keepdims=True)
+    return sum(row[:, w : w + LANES] for w in range(0, row.shape[1], LANES))
 
 
 def middle(layers, turned, pick, marks, inv_i, kinv_i, xold, *rest):
     shared, (payload, spill, xcur) = rest[:-3], rest[-3:]
-    slots = turned.shape[0]
     x = joined(shared)
     xcur[...] = x
     send_out(layers, shared[0].shape[1], x, inv_i[...], kinv_i[...], turned, pick, marks, payload,
              spill, xcur)
-    payload[slots + 2 : slots + 3, :] = lane_change(x, xold)
+    meta = payload.shape[0] - META
+    payload[meta + 2 : meta + 3, :] = lane_sum(jnp.abs(x - xold[...]))
 
 
 def partial(layers, node_total, early, spill, *rest):
     pays, outs = (rest[:-1], rest[-1:]) if early else (rest[:-2], rest[-2:])
     part = outs[0]
-    slots = pays[0].shape[0] - META
+    meta, wide = pays[0].shape[0] - META, part.shape[2] // LANES
+    slots = meta // wide
     blocks = part.shape[1] // 2
     odd = lax.axis_index("row") % 2
     first_block = (lax.axis_index("col") * blocks).astype(F32)
     block_ids = lax.broadcasted_iota(jnp.int32, (blocks, slots), 0).astype(F32) + first_block
     walks, sums = [], None
     for pay in pays:
-        onehot = (block_ids == pay[slots : slots + 1, 0:slots]).astype(BF16)
-        walks.append(place(onehot, pay[0:slots, :]))
-        meta = pay[slots : slots + META, :]
-        sums = meta if sums is None else sums + meta
+        onehot = (block_ids == pay[meta : meta + 1, 0:slots]).astype(BF16)
+        terms = [pay[w * slots : (w + 1) * slots, :] for w in range(wide)]
+        walks.append(place(onehot, jnp.concatenate(terms, axis=1)))
+        extra = pay[meta : meta + META, :]
+        sums = extra if sums is None else sums + extra
     mass = jnp.sum(sums[1:2, :], axis=1, keepdims=True)
     if not early:
         outs[1][...] = sums
@@ -189,7 +196,7 @@
     shared, (xnew, change) = rest[:-2], rest[-2:]
     x = joined(shared)
     xnew[...] = x
-    change[...] = jnp.broadcast_to(lane_change(x, xold), change.shape)
+    change[...] = jnp.broadcast_to(lane_sum(jnp.abs(x - xold[...])), change.shape)
 
 
 def flatten(xnew, ranks):
@@ -233,8 +240,9 @@
     pairs = []
     for layer in range(layers):
         for row in range(rows):
-            other = (layer + 1) % layers if row % 2 == 0 else (layer - 1) % layers
-            pairs.append((layer * rows + row, other * rows + (row ^ 1)))
+            other = layer + 1 if row % 2 == 1 else layer - 1
+            here = layer * rows + row
+            pairs.append((here, other * rows + row if 0 <= other < layers else layer * rows + (row ^ 1)))
     return lax.ppermute(spill, ("layer", "row"), pairs)
 
 
@@ -265,14 +273,16 @@
     packed, turned, pick, marks = call(
         opening,
         (lead(slots + META + 2 * blocks), pltpu.VMEM((slots, edge, edge), BF16),
-         pltpu.VMEM((slots, col_blk), BF16), pltpu.VMEM((META, edge), F32)),
+         pltpu.VMEM((slots, col_blk), BF16), pltpu.VMEM((META, LANES), F32)),
         (HBM, HBM, HBM, pl.BlockSpec(memory_space=pl.ANY), HBM, HBM),
         [pltpu.VMEM((slots, edge, edge), BF16), pltpu.VMEM((1, slots), jnp.int32),
          pltpu.VMEM((1, slots), jnp.int32), pltpu.VMEM((1, 1), jnp.int32), pltpu.VMEM(flat, F32),
          pltpu.VMEM(flat, jnp.int32), pltpu.SemaphoreType.DMA((5 + CHUNKS,))],
     )(*arguments)
     shared = to_rows(packed)
-    sent = (shape(slots + META), shape(2 * blocks, BF16), shape(col_blk))
+    lanes = jax.ShapeDtypeStruct((META, LANES), F32)
+    products = jax.ShapeDtypeStruct((slots * edge // LANES + META, LANES), F32)
+    sent = (products, shape(2 * blocks, BF16), shape(col_blk))
     payload, spill, x, inv, kinv = call(
         functools.partial(first, layers), sent + (shape(col_blk), shape(col_blk)),
         (VMEM,) * (3 + len(shared)),
@@ -287,13 +297,11 @@
         others = to_others(payload)
         part, *change = call(
             functools.partial(partial, layers, node_total, t == 0),
-            (lead(2 * blocks), shape(META))[: 1 + (t > 0)], (VMEM,) * (2 + len(others)),
+            (lead(2 * blocks), lanes)[: 1 + (t > 0)], (VMEM,) * (2 + len(others)),
         )(arriving, payload, *others)
         changes += change
         shared = to_rows(part)
-    xnew, last = call(
-        closing, (shape(col_blk), shape(META)), (VMEM,) * (1 + len(shared))
-    )(x, *shared)
+    xnew, last = call(closing, (shape(col_blk), lanes), (VMEM,) * (1 + len(shared)))(x, *shared)
     lates = [last] + to_others(last)
     ranks = call(flatten, jax.ShapeDtypeStruct(flat, F32), (VMEM,))(xnew)
     residuals = call(

time: 48.3 us -> 46.7 us (0.967)
  starting transfers between devices: 23.7 us -> 21.5 us
  waiting for transfers between devices: 15.8 us -> 16.5 us
    ppermute x12, starting transfers between devices: 15.6 us -> 13.6 us  [to_others(): got.append(lax.ppermute(x, ('row', 'col'), pairs))]
    ppermute x12, waiting for transfers between devices: 11.4 us -> 12.1 us  [to_others(): got.append(lax.ppermute(x, ('row', 'col'), pairs))]
  transfers between devices with their start and end apart: 19 -> 19, of which waited for: 12 -> 13; matrix products, arithmetic and copies ran while one was open for 0% -> 0% of each run, Pallas kernels for 1% -> 1%
where the time goes in v1:
time: 46.7 us; the launch traced here: 46.4 us
  starting transfers between devices  21.5 us (46%)
  waiting for transfers between devices  16.5 us (35%)
  Pallas kernels  7 us (15%)
  between operations  1.4 us (3%)
    ppermute x12, starting transfers between devices, to_others(): got.append(lax.ppermute(x, ('row', 'col'), pairs))  13.6 us
    ppermute x12, waiting for transfers between devices, to_others(): got.append(lax.ppermute(x, ('row', 'col'), pairs))  12.1 us
    ppermute x3, starting transfers between devices, to_layers(): return lax.ppermute(spill, ('layer', 'row'), pairs)  5.41 us
    ppermute x4, waiting for transfers between devices, to_rows(): return (x, lax.ppermute(x, 'row', [(0, 1), (1, 0)]))  4.35 us
    pallas_call x1, Pallas kernels, local(): call(opening, (lead(slots + META + 2 * blocks), pltpu.VMEM((slots, edge,...  2.72 us
    ppermute x4, starting transfers between devices, to_rows(): return (x, lax.ppermute(x, 'row', [(0, 1), (1, 0)]))  2.45 us
    pallas_call x2, Pallas kernels, local(): call(functools.partial(middle, layers), sent, (VMEM,) * (6 + len(shared)))  1.41 us
    pallas_call x1, Pallas kernels, local(): call(functools.partial(first, layers), sent + (shape(col_blk), shape(col_...  0.94 us
  transfers between devices with their start and end apart: 19, of which 13 were waited for; matrix products, arithmetic and copies ran while one was open for 0% of the time, Pallas kernels for 1%

profile of v1, /device:TPU:1, one launch (start us, length us, event | category | flops | bytes accessed | tf_op | source)
XLA Modules:
  0.0 46.4 jit_solution(2166954426126883513)
XLA Ops:
  1.3 2.7 %shard_map.77 = (f32[1,168,256]{2,1,0:T(8,128)S(1)}, bf16[32,256,256]{2,1,0:T(8,128)(2,1)S(1)}, bf16[32,128]{1,0:T(8,128)(2,1)S(1)}, f32[8,128]{1,0:T(8,128)S(1)}) custom-call(bf16[32,256,256]{2,1,0:T(8,128)(2,1)} %bitcast.9, s32[1,32]{1,0:T(1,128)} %bitcast.13, s32[1,32]{1,0:T(1,128)} %bitcast.14, s32[1,1]{1,0:T(1,128)} %bitcast.8.count_h, ...), custom_call_target="tpu_custom_call" | custom-call | tf_op jit(solution)/shard_map/pallas_call | solution.py:273
  4.1 1.4 %collective-permute-done.rest_1_ = f32[1,168,256]{2,1,0:T(8,128)S(1)} collective-permute-done((f32[1,168,256]{2,1,0:T(8,128)S(1)}, f32[1,168,256]{2,1,0:T(8,128)S(1)}, u32[]{:S(2)}, u32[]{:S(2)}) %collective-permute-start) | collective-permute-done | bytes 172064 | tf_op jit(solution)/shard_map/ppermute | solution.py:234
  5.5 0.9 %shard_map.78 = (f32[72,128]{1,0:T(8,128)S(1)}, bf16[128,256]{1,0:T(8,128)(2,1)S(1)}, f32[128,256]{1,0:T(8,128)S(1)}, f32[128,256]{1,0:T(8,128)S(1)}, f32[128,256]{1,0:T(8,128)S(1)}) custom-call(bf16[32,256,256]{2,1,0:T(8,128)(2,1)S(1)} %get-tuple-element.23.turned, bf16[32,128]{1,0:T(8,128)(2,1)S(1)} %get-tuple-element.24.pick, ...), custom_call_target="tpu_custom_call" | custom-call | tf_op jit(solution)/shard_map/pallas_call | solution.py:286
  6.4 2.4 %collective-permute-start.1 = (bf16[128,256]{1,0:T(8,128)(2,1)S(1)}, bf16[128,256]{1,0:T(8,128)(2,1)S(1)}, u32[]{:S(2)}, u32[]{:S(2)}) collective-permute-start(bf16[128,256]{1,0:T(8,128)(2,1)S(1)} %get-tuple-element.30), channel_id=1, source_target_pairs={{0,4},{4,12},{8,0},{12,20},{16,8},{20,28},{24,16},{28,24},{1,5},{5... | collective-permute-start | bytes 196616 | tf_op jit(solution)/shard_map/ppermute | solution.py:246
  8.9 2.5 %collective-permute-start.4 = (f32[72,128]{1,0:T(8,128)S(1)}, f32[72,128]{1,0:T(8,128)S(1)}, u32[]{:S(2)}, u32[]{:S(2)}) collective-permute-start(f32[72,128]{1,0:T(8,128)S(1)} %get-tuple-element.31.rest_0_), channel_id=1, source_target_pairs={{0,7},{1,6},{2,5},{3,4},{4,3},{5,2},{6,1},{7,0},{8,15},{9,14},{10,... | collective-permute-start | bytes 110600 | tf_op jit(solution)/shard_map/ppermute | solution.py:227
  11.6 1.1 %collective-permute-start.2 = (f32[72,128]{1,0:T(8,128)S(1)}, f32[72,128]{1,0:T(8,128)S(1)}, u32[]{:S(2)}, u32[]{:S(2)}) collective-permute-start(f32[72,128]{1,0:T(8,128)S(1)} %get-tuple-element.31.rest_0_), channel_id=1, source_target_pairs={{0,5},{1,4},{2,7},{3,6},{4,1},{5,0},{6,3},{7,2},{8,13},{9,12},{10,... | collective-permute-start | bytes 110600 | tf_op jit(solution)/shard_map/ppermute | solution.py:227
  12.7 1.3 %collective-permute-done.4.rest_3_ = f32[72,128]{1,0:T(8,128)S(1)} collective-permute-done((f32[72,128]{1,0:T(8,128)S(1)}, f32[72,128]{1,0:T(8,128)S(1)}, u32[]{:S(2)}, u32[]{:S(2)}) %collective-permute-start.4) | collective-permute-done | bytes 36896 | tf_op jit(solution)/shard_map/ppermute | solution.py:227
  14.0 1.7 %collective-permute-done.3.rest_2_ = f32[72,128]{1,0:T(8,128)S(1)} collective-permute-done((f32[72,128]{1,0:T(8,128)S(1)}, f32[72,128]{1,0:T(8,128)S(1)}, u32[]{:S(2)}, u32[]{:S(2)}) %collective-permute-start.3) | collective-permute-done | bytes 36896 | tf_op jit(solution)/shard_map/ppermute | solution.py:227
  16.0 1.2 %collective-permute-start.5 = (f32[1,128,256]{2,1,0:T(8,128)S(1)}, f32[1,128,256]{2,1,0:T(8,128)S(1)}, u32[]{:S(2)}, u32[]{:S(2)}) collective-permute-start(f32[1,128,256]{2,1,0:T(8,128)S(1)} %shard_map.79.rest_0_), channel_id=1, source_target_pairs={{0,4},{4,0},{1,5},{5,1},{2,6},{6,2},{3,7},{7,3},{8,12},{12,8},{9,1... | collective-permute-start | bytes 393224 | tf_op jit(solution)/shard_map/ppermute | solution.py:234
  17.2 1.0 %collective-permute-done.5.rest_1_ = f32[1,128,256]{2,1,0:T(8,128)S(1)} collective-permute-done((f32[1,128,256]{2,1,0:T(8,128)S(1)}, f32[1,128,256]{2,1,0:T(8,128)S(1)}, u32[]{:S(2)}, u32[]{:S(2)}) %collective-permute-start.5) | collective-permute-done | bytes 131104 | tf_op jit(solution)/shard_map/ppermute | solution.py:234
  18.2 0.7 %shard_map.80 = (f32[72,128]{1,0:T(8,128)S(1)}, bf16[128,256]{1,0:T(8,128)(2,1)S(1)}, f32[128,256]{1,0:T(8,128)S(1)}) custom-call(bf16[32,256,256]{2,1,0:T(8,128)(2,1)S(1)} %get-tuple-element.23.turned, bf16[32,128]{1,0:T(8,128)(2,1)S(1)} %get-tuple-element.24.pick, f32[8,128]{1,0:T(8,128)S(1)} %get-tuple-element.25.marks, ...), custom_call_target="tpu_custom_call" | custom-call | tf_op jit(solution)/shard_map/pallas_call | solution.py:293
  18.9 1.5 %collective-permute-start.6 = (bf16[128,256]{1,0:T(8,128)(2,1)S(1)}, bf16[128,256]{1,0:T(8,128)(2,1)S(1)}, u32[]{:S(2)}, u32[]{:S(2)}) collective-permute-start(bf16[128,256]{1,0:T(8,128)(2,1)S(1)} %get-tuple-element.33), channel_id=1, source_target_pairs={{0,4},{4,12},{8,0},{12,20},{16,8},{20,28},{24,16},{28,24},{1,5},{5... | collective-permute-start | bytes 196616 | tf_op jit(solution)/shard_map/ppermute | solution.py:246
  20.4 1.1 %collective-permute-start.9 = (f32[72,128]{1,0:T(8,128)S(1)}, f32[72,128]{1,0:T(8,128)S(1)}, u32[]{:S(2)}, u32[]{:S(2)}) collective-permute-start(f32[72,128]{1,0:T(8,128)S(1)} %get-tuple-element.34.rest_0_), channel_id=1, source_target_pairs={{0,7},{1,6},{2,5},{3,4},{4,3},{5,2},{6,1},{7,0},{8,15},{9,14},{10,... | collective-permute-start | bytes 110600 | tf_op jit(solution)/shard_map/ppermute | solution.py:227
  21.9 1.3 %collective-permute-start.7 = (f32[72,128]{1,0:T(8,128)S(1)}, f32[72,128]{1,0:T(8,128)S(1)}, u32[]{:S(2)}, u32[]{:S(2)}) collective-permute-start(f32[72,128]{1,0:T(8,128)S(1)} %get-tuple-element.34.rest_0_), channel_id=1, source_target_pairs={{0,5},{1,4},{2,7},{3,6},{4,1},{5,0},{6,3},{7,2},{8,13},{9,12},{10,... | collective-permute-start | bytes 110600 | tf_op jit(solution)/shard_map/ppermute | solution.py:227
  23.2 2.6 %collective-permute-done.9.rest_3_ = f32[72,128]{1,0:T(8,128)S(1)} collective-permute-done((f32[72,128]{1,0:T(8,128)S(1)}, f32[72,128]{1,0:T(8,128)S(1)}, u32[]{:S(2)}, u32[]{:S(2)}) %collective-permute-start.9) | collective-permute-done | bytes 36896 | tf_op jit(solution)/shard_map/ppermute | solution.py:227
  25.8 1.6 %collective-permute-done.8.rest_2_ = f32[72,128]{1,0:T(8,128)S(1)} collective-permute-done((f32[72,128]{1,0:T(8,128)S(1)}, f32[72,128]{1,0:T(8,128)S(1)}, u32[]{:S(2)}, u32[]{:S(2)}) %collective-permute-start.8) | collective-permute-done | bytes 36896 | tf_op jit(solution)/shard_map/ppermute | solution.py:227
  27.7 0.5 %collective-permute-start.10 = (f32[1,128,256]{2,1,0:T(8,128)S(1)}, f32[1,128,256]{2,1,0:T(8,128)S(1)}, u32[]{:S(2)}, u32[]{:S(2)}) collective-permute-start(f32[1,128,256]{2,1,0:T(8,128)S(1)} %get-tuple-element.35.rest_0_), channel_id=1, source_target_pairs={{0,4},{4,0},{1,5},{5,1},{2,6},{6,2},{3,7},{7,3},{8,12},{12,8},{9,1... | collective-permute-start | bytes 393224 | tf_op jit(solution)/shard_map/ppermute | solution.py:234
  28.2 1.0 %collective-permute-done.10.rest_1_ = f32[1,128,256]{2,1,0:T(8,128)S(1)} collective-permute-done((f32[1,128,256]{2,1,0:T(8,128)S(1)}, f32[1,128,256]{2,1,0:T(8,128)S(1)}, u32[]{:S(2)}, u32[]{:S(2)}) %collective-permute-start.10) | collective-permute-done | bytes 131104 | tf_op jit(solution)/shard_map/ppermute | solution.py:234
  29.2 0.7 %shard_map.82 = (f32[72,128]{1,0:T(8,128)S(1)}, bf16[128,256]{1,0:T(8,128)(2,1)S(1)}, f32[128,256]{1,0:T(8,128)S(1)}) custom-call(bf16[32,256,256]{2,1,0:T(8,128)(2,1)S(1)} %get-tuple-element.23.turned, bf16[32,128]{1,0:T(8,128)(2,1)S(1)} %get-tuple-element.24.pick, f32[8,128]{1,0:T(8,128)S(1)} %get-tuple-element.25.marks, ...), custom_call_target="tpu_custom_call" | custom-call | tf_op jit(solution)/shard_map/pallas_call | solution.py:293
  29.9 1.5 %collective-permute-start.11 = (bf16[128,256]{1,0:T(8,128)(2,1)S(1)}, bf16[128,256]{1,0:T(8,128)(2,1)S(1)}, u32[]{:S(2)}, u32[]{:S(2)}) collective-permute-start(bf16[128,256]{1,0:T(8,128)(2,1)S(1)} %get-tuple-element.37), channel_id=1, source_target_pairs={{0,4},{4,12},{8,0},{12,20},{16,8},{20,28},{24,16},{28,24},{1,5},{5... | collective-permute-start | bytes 196616 | tf_op jit(solution)/shard_map/ppermute | solution.py:246
  31.4 0.7 %collective-permute-start.14 = (f32[72,128]{1,0:T(8,128)S(1)}, f32[72,128]{1,0:T(8,128)S(1)}, u32[]{:S(2)}, u32[]{:S(2)}) collective-permute-start(f32[72,128]{1,0:T(8,128)S(1)} %get-tuple-element.38.rest_0_), channel_id=1, source_target_pairs={{0,7},{1,6},{2,5},{3,4},{4,3},{5,2},{6,1},{7,0},{8,15},{9,14},{10,... | collective-permute-start | bytes 110600 | tf_op jit(solution)/shard_map/ppermute | solution.py:227
  32.0 0.9 %collective-permute-start.13 = (f32[72,128]{1,0:T(8,128)S(1)}, f32[72,128]{1,0:T(8,128)S(1)}, u32[]{:S(2)}, u32[]{:S(2)}) collective-permute-start(f32[72,128]{1,0:T(8,128)S(1)} %get-tuple-element.38.rest_0_), channel_id=1, source_target_pairs={{0,6},{1,7},{2,4},{3,5},{4,2},{5,3},{6,0},{7,1},{8,14},{9,15},{10,... | collective-permute-start | bytes 110600 | tf_op jit(solution)/shard_map/ppermute | solution.py:227
  32.9 1.3 %collective-permute-start.12 = (f32[72,128]{1,0:T(8,128)S(1)}, f32[72,128]{1,0:T(8,128)S(1)}, u32[]{:S(2)}, u32[]{:S(2)}) collective-permute-start(f32[72,128]{1,0:T(8,128)S(1)} %get-tuple-element.38.rest_0_), channel_id=1, source_target_pairs={{0,5},{1,4},{2,7},{3,6},{4,1},{5,0},{6,3},{7,2},{8,13},{9,12},{10,... | collective-permute-start | bytes 110600 | tf_op jit(solution)/shard_map/ppermute | solution.py:227
  34.2 2.5 %collective-permute-done.14.rest_3_ = f32[72,128]{1,0:T(8,128)S(1)} collective-permute-done((f32[72,128]{1,0:T(8,128)S(1)}, f32[72,128]{1,0:T(8,128)S(1)}, u32[]{:S(2)}, u32[]{:S(2)}) %collective-permute-start.14) | collective-permute-done | bytes 36896 | tf_op jit(solution)/shard_map/ppermute | solution.py:227
  36.6 1.2 %collective-permute-done.13.rest_2_ = f32[72,128]{1,0:T(8,128)S(1)} collective-permute-done((f32[72,128]{1,0:T(8,128)S(1)}, f32[72,128]{1,0:T(8,128)S(1)}, u32[]{:S(2)}, u32[]{:S(2)}) %collective-permute-start.13) | collective-permute-done | bytes 36896 | tf_op jit(solution)/shard_map/ppermute | solution.py:227
  38.3 0.6 %collective-permute-start.15 = (f32[1,128,256]{2,1,0:T(8,128)S(1)}, f32[1,128,256]{2,1,0:T(8,128)S(1)}, u32[]{:S(2)}, u32[]{:S(2)}) collective-permute-start(f32[1,128,256]{2,1,0:T(8,128)S(1)} %get-tuple-element.39.rest_0_), channel_id=1, source_target_pairs={{0,4},{4,0},{1,5},{5,1},{2,6},{6,2},{3,7},{7,3},{8,12},{12,8},{9,1... | collective-permute-start | bytes 393224 | tf_op jit(solution)/shard_map/ppermute | solution.py:234
  38.9 1.0 %collective-permute-done.15.rest_1_ = f32[1,128,256]{2,1,0:T(8,128)S(1)} collective-permute-done((f32[1,128,256]{2,1,0:T(8,128)S(1)}, f32[1,128,256]{2,1,0:T(8,128)S(1)}, u32[]{:S(2)}, u32[]{:S(2)}) %collective-permute-start.15) | collective-permute-done | bytes 131104 | tf_op jit(solution)/shard_map/ppermute | solution.py:234
  39.9 1.9 %collective-permute-start.18 = (f32[8,128]{1,0:T(8,128)S(1)}, f32[8,128]{1,0:T(8,128)S(1)}, u32[]{:S(2)}, u32[]{:S(2)}) collective-permute-start(f32[8,128]{1,0:T(8,128)S(1)} %get-tuple-element.43.refs_2_), channel_id=1, source_target_pairs={{0,7},{1,6},{2,5},{3,4},{4,3},{5,2},{6,1},{7,0},{8,15},{9,14},{10,... | collective-permute-start | bytes 12296 | tf_op jit(solution)/shard_map/ppermute | solution.py:227
  41.8 2.2 %collective-permute-start.16 = (f32[8,128]{1,0:T(8,128)S(1)}, f32[8,128]{1,0:T(8,128)S(1)}, u32[]{:S(2)}, u32[]{:S(2)}) collective-permute-start(f32[8,128]{1,0:T(8,128)S(1)} %get-tuple-element.43.refs_2_), channel_id=1, source_target_pairs={{0,5},{1,4},{2,7},{3,6},{4,1},{5,0},{6,3},{7,2},{8,13},{9,12},{10,... | collective-permute-start | bytes 12296 | tf_op jit(solution)/shard_map/ppermute | solution.py:227
  44.1 0.6 %shard_map.85 = f32[128,128]{1,0:T(8,128)} custom-call(f32[128,256]{1,0:T(8,128)S(1)} %get-tuple-element.40.xnew), custom_call_target="tpu_custom_call" | custom-call | tf_op jit(solution)/shard_map/pallas_call | solution.py:306
  44.9 0.9 %collective-permute-done.17.refs_4_ = f32[8,128]{1,0:T(8,128)S(1)} collective-permute-done((f32[8,128]{1,0:T(8,128)S(1)}, f32[8,128]{1,0:T(8,128)S(1)}, u32[]{:S(2)}, u32[]{:S(2)}) %collective-permute-start.17) | collective-permute-done | bytes 4128 | tf_op jit(solution)/shard_map/ppermute | solution.py:227
  45.8 0.6 %shard_map.86 = f32[1,3]{1,0:T(1,128)} custom-call(f32[8,128]{1,0:T(8,128)S(1)} %get-tuple-element.41.refs_0_, f32[8,128]{1,0:T(8,128)S(1)} %get-tuple-element.42.refs_1_, f32[8,128]{1,0:T(8,128)S(1)} %get-tuple-element.43.refs_2_, f32[8,128]{1,0:T(8,128)S(1)} %collective-permute-done.16.refs_3_, f32[8,128]{1,0:T(8,128)S(1)} %collective-permute-done.17.refs_4_, ...), custom_call_target="tpu_custom_call" | custom-call | tf_op jit(solution)/shard_map/pallas_call | solution.py:307
  (16 shorter events, 1.8 us)
Async XLA Ops:
  4.0 1.5 %collective-permute-start = (f32[1,168,256]{2,1,0:T(8,128)S(1)}, f32[1,168,256]{2,1,0:T(8,128)S(1)}, u32[]{:S(2)}, u32[]{:S(2)}) collective-permute-start(f32[1,168,256]{2,1,0:T(8,128)S(1)} %get-tuple-element.26.rest_0_), channel_id=1, source_target_pairs={{0,4},{4,0},{1,5},{5,1},{2,6},{6,2},{3,7},{7,3},{8,12},{12,8},{9,1... | collective-permute-start | bytes 516104 | tf_op jit(solution)/shard_map/ppermute | solution.py:234
  6.4 9.3 %collective-permute-start.1 = (bf16[128,256]{1,0:T(8,128)(2,1)S(1)}, bf16[128,256]{1,0:T(8,128)(2,1)S(1)}, u32[]{:S(2)}, u32[]{:S(2)}) collective-permute-start(bf16[128,256]{1,0:T(8,128)(2,1)S(1)} %get-tuple-element.30), channel_id=1, source_target_pairs={{0,4},{4,12},{8,0},{12,20},{16,8},{20,28},{24,16},{28,24},{1,5},{5... | collective-permute-start | bytes 196616 | tf_op jit(solution)/shard_map/ppermute | solution.py:246
  8.9 5.2 %collective-permute-start.4 = (f32[72,128]{1,0:T(8,128)S(1)}, f32[72,128]{1,0:T(8,128)S(1)}, u32[]{:S(2)}, u32[]{:S(2)}) collective-permute-start(f32[72,128]{1,0:T(8,128)S(1)} %get-tuple-element.31.rest_0_), channel_id=1, source_target_pairs={{0,7},{1,6},{2,5},{3,4},{4,3},{5,2},{6,1},{7,0},{8,15},{9,14},{10,... | collective-permute-start | bytes 110600 | tf_op jit(solution)/shard_map/ppermute | solution.py:227
  11.4 4.4 %collective-permute-start.3 = (f32[72,128]{1,0:T(8,128)S(1)}, f32[72,128]{1,0:T(8,128)S(1)}, u32[]{:S(2)}, u32[]{:S(2)}) collective-permute-start(f32[72,128]{1,0:T(8,128)S(1)} %get-tuple-element.31.rest_0_), channel_id=1, source_target_pairs={{0,6},{1,7},{2,4},{3,5},{4,2},{5,3},{6,0},{7,1},{8,14},{9,15},{10,... | collective-permute-start | bytes 110600 | tf_op jit(solution)/shard_map/ppermute | solution.py:227
  11.6 4.1 %collective-permute-start.2 = (f32[72,128]{1,0:T(8,128)S(1)}, f32[72,128]{1,0:T(8,128)S(1)}, u32[]{:S(2)}, u32[]{:S(2)}) collective-permute-start(f32[72,128]{1,0:T(8,128)S(1)} %get-tuple-element.31.rest_0_), channel_id=1, source_target_pairs={{0,5},{1,4},{2,7},{3,6},{4,1},{5,0},{6,3},{7,2},{8,13},{9,12},{10,... | collective-permute-start | bytes 110600 | tf_op jit(solution)/shard_map/ppermute | solution.py:227
  16.0 2.2 %collective-permute-start.5 = (f32[1,128,256]{2,1,0:T(8,128)S(1)}, f32[1,128,256]{2,1,0:T(8,128)S(1)}, u32[]{:S(2)}, u32[]{:S(2)}) collective-permute-start(f32[1,128,256]{2,1,0:T(8,128)S(1)} %shard_map.79.rest_0_), channel_id=1, source_target_pairs={{0,4},{4,0},{1,5},{5,1},{2,6},{6,2},{3,7},{7,3},{8,12},{12,8},{9,1... | collective-permute-start | bytes 393224 | tf_op jit(solution)/shard_map/ppermute | solution.py:234
  18.9 8.5 %collective-permute-start.6 = (bf16[128,256]{1,0:T(8,128)(2,1)S(1)}, bf16[128,256]{1,0:T(8,128)(2,1)S(1)}, u32[]{:S(2)}, u32[]{:S(2)}) collective-permute-start(bf16[128,256]{1,0:T(8,128)(2,1)S(1)} %get-tuple-element.33), channel_id=1, source_target_pairs={{0,4},{4,12},{8,0},{12,20},{16,8},{20,28},{24,16},{28,24},{1,5},{5... | collective-permute-start | bytes 196616 | tf_op jit(solution)/shard_map/ppermute | solution.py:246
  20.4 5.4 %collective-permute-start.9 = (f32[72,128]{1,0:T(8,128)S(1)}, f32[72,128]{1,0:T(8,128)S(1)}, u32[]{:S(2)}, u32[]{:S(2)}) collective-permute-start(f32[72,128]{1,0:T(8,128)S(1)} %get-tuple-element.34.rest_0_), channel_id=1, source_target_pairs={{0,7},{1,6},{2,5},{3,4},{4,3},{5,2},{6,1},{7,0},{8,15},{9,14},{10,... | collective-permute-start | bytes 110600 | tf_op jit(solution)/shard_map/ppermute | solution.py:227
  21.5 5.9 %collective-permute-start.8 = (f32[72,128]{1,0:T(8,128)S(1)}, f32[72,128]{1,0:T(8,128)S(1)}, u32[]{:S(2)}, u32[]{:S(2)}) collective-permute-start(f32[72,128]{1,0:T(8,128)S(1)} %get-tuple-element.34.rest_0_), channel_id=1, source_target_pairs={{0,6},{1,7},{2,4},{3,5},{4,2},{5,3},{6,0},{7,1},{8,14},{9,15},{10,... | collective-permute-start | bytes 110600 | tf_op jit(solution)/shard_map/ppermute | solution.py:227
  21.9 5.6 %collective-permute-start.7 = (f32[72,128]{1,0:T(8,128)S(1)}, f32[72,128]{1,0:T(8,128)S(1)}, u32[]{:S(2)}, u32[]{:S(2)}) collective-permute-start(f32[72,128]{1,0:T(8,128)S(1)} %get-tuple-element.34.rest_0_), channel_id=1, source_target_pairs={{0,5},{1,4},{2,7},{3,6},{4,1},{5,0},{6,3},{7,2},{8,13},{9,12},{10,... | collective-permute-start | bytes 110600 | tf_op jit(solution)/shard_map/ppermute | solution.py:227
  27.7 1.5 %collective-permute-start.10 = (f32[1,128,256]{2,1,0:T(8,128)S(1)}, f32[1,128,256]{2,1,0:T(8,128)S(1)}, u32[]{:S(2)}, u32[]{:S(2)}) collective-permute-start(f32[1,128,256]{2,1,0:T(8,128)S(1)} %get-tuple-element.35.rest_0_), channel_id=1, source_target_pairs={{0,4},{4,0},{1,5},{5,1},{2,6},{6,2},{3,7},{7,3},{8,12},{12,8},{9,1... | collective-permute-start | bytes 393224 | tf_op jit(solution)/shard_map/ppermute | solution.py:234
  29.9 8.1 %collective-permute-start.11 = (bf16[128,256]{1,0:T(8,128)(2,1)S(1)}, bf16[128,256]{1,0:T(8,128)(2,1)S(1)}, u32[]{:S(2)}, u32[]{:S(2)}) collective-permute-start(bf16[128,256]{1,0:T(8,128)(2,1)S(1)} %get-tuple-element.37), channel_id=1, source_target_pairs={{0,4},{4,12},{8,0},{12,20},{16,8},{20,28},{24,16},{28,24},{1,5},{5... | collective-permute-start | bytes 196616 | tf_op jit(solution)/shard_map/ppermute | solution.py:246
  31.4 5.3 %collective-permute-start.14 = (f32[72,128]{1,0:T(8,128)S(1)}, f32[72,128]{1,0:T(8,128)S(1)}, u32[]{:S(2)}, u32[]{:S(2)}) collective-permute-start(f32[72,128]{1,0:T(8,128)S(1)} %get-tuple-element.38.rest_0_), channel_id=1, source_target_pairs={{0,7},{1,6},{2,5},{3,4},{4,3},{5,2},{6,1},{7,0},{8,15},{9,14},{10,... | collective-permute-start | bytes 110600 | tf_op jit(solution)/shard_map/ppermute | solution.py:227
  32.0 5.8 %collective-permute-start.13 = (f32[72,128]{1,0:T(8,128)S(1)}, f32[72,128]{1,0:T(8,128)S(1)}, u32[]{:S(2)}, u32[]{:S(2)}) collective-permute-start(f32[72,128]{1,0:T(8,128)S(1)} %get-tuple-element.38.rest_0_), channel_id=1, source_target_pairs={{0,6},{1,7},{2,4},{3,5},{4,2},{5,3},{6,0},{7,1},{8,14},{9,15},{10,... | collective-permute-start | bytes 110600 | tf_op jit(solution)/shard_map/ppermute | solution.py:227
  32.9 5.1 %collective-permute-start.12 = (f32[72,128]{1,0:T(8,128)S(1)}, f32[72,128]{1,0:T(8,128)S(1)}, u32[]{:S(2)}, u32[]{:S(2)}) collective-permute-start(f32[72,128]{1,0:T(8,128)S(1)} %get-tuple-element.38.rest_0_), channel_id=1, source_target_pairs={{0,5},{1,4},{2,7},{3,6},{4,1},{5,0},{6,3},{7,2},{8,13},{9,12},{10,... | collective-permute-start | bytes 110600 | tf_op jit(solution)/shard_map/ppermute | solution.py:227
  38.3 1.6 %collective-permute-start.15 = (f32[1,128,256]{2,1,0:T(8,128)S(1)}, f32[1,128,256]{2,1,0:T(8,128)S(1)}, u32[]{:S(2)}, u32[]{:S(2)}) collective-permute-start(f32[1,128,256]{2,1,0:T(8,128)S(1)} %get-tuple-element.39.rest_0_), channel_id=1, source_target_pairs={{0,4},{4,0},{1,5},{5,1},{2,6},{6,2},{3,7},{7,3},{8,12},{12,8},{9,1... | collective-permute-start | bytes 393224 | tf_op jit(solution)/shard_map/ppermute | solution.py:234
  39.9 4.9 %collective-permute-start.18 = (f32[8,128]{1,0:T(8,128)S(1)}, f32[8,128]{1,0:T(8,128)S(1)}, u32[]{:S(2)}, u32[]{:S(2)}) collective-permute-start(f32[8,128]{1,0:T(8,128)S(1)} %get-tuple-element.43.refs_2_), channel_id=1, source_target_pairs={{0,7},{1,6},{2,5},{3,4},{4,3},{5,2},{6,1},{7,0},{8,15},{9,14},{10,... | collective-permute-start | bytes 12296 | tf_op jit(solution)/shard_map/ppermute | solution.py:227
  41.8 3.9 %collective-permute-start.17 = (f32[8,128]{1,0:T(8,128)S(1)}, f32[8,128]{1,0:T(8,128)S(1)}, u32[]{:S(2)}, u32[]{:S(2)}) collective-permute-start(f32[8,128]{1,0:T(8,128)S(1)} %get-tuple-element.43.refs_2_), channel_id=1, source_target_pairs={{0,6},{1,7},{2,4},{3,5},{4,2},{5,3},{6,0},{7,1},{8,14},{9,15},{10,... | collective-permute-start | bytes 12296 | tf_op jit(solution)/shard_map/ppermute | solution.py:227
  41.8 3.9 %collective-permute-start.16 = (f32[8,128]{1,0:T(8,128)S(1)}, f32[8,128]{1,0:T(8,128)S(1)}, u32[]{:S(2)}, u32[]{:S(2)}) collective-permute-start(f32[8,128]{1,0:T(8,128)S(1)} %get-tuple-element.43.refs_2_), channel_id=1, source_target_pairs={{0,5},{1,4},{2,7},{3,6},{4,1},{5,0},{6,3},{7,2},{8,13},{9,12},{10,... | collective-permute-start | bytes 12296 | tf_op jit(solution)/shard_map/ppermute | solution.py:227

commit v2 on v1

--- a/solution.py
+++ b/solution.py
@@ -186,8 +186,8 @@
     end = jnp.where(odd == 0, layers - 1, 0)
     arrive = jnp.where(lax.axis_index("layer") == end, 0.0, damping * spill[...].astype(F32))
     walk = damping * (1.0 - coupling)
-    own = walk * (walks[0] + mass / node_total) + (1.0 - damping)
-    peer = walk * sum(walks[1:])
+    own = walk * (sum(walks[:2]) + mass / node_total) + (1.0 - damping)
+    peer = walk * sum(walks[2:])
     part[0, 0:blocks, :] = arrive[0:blocks] + jnp.where(odd == 0, own, peer)
     part[0, blocks:, :] = arrive[blocks:] + jnp.where(odd == 0, peer, own)
 
@@ -223,7 +223,7 @@
         for row in range(rows):
             for col in range(cols):
                 other = (col + step) % cols if cols & (cols - 1) else col ^ step
-                pairs.append((row * cols + col, (row ^ 1) * cols + other))
+                pairs.append((row * cols + col, (row ^ (step > 1)) * cols + other))
         got.append(lax.ppermute(x, ("row", "col"), pairs))
     return got
 

time: 46.7 us -> 47 us (level)
  starting transfers between devices: 21.5 us -> 23.4 us
  waiting for transfers between devices: 16.5 us -> 14.7 us
    ppermute x12, waiting for transfers between devices: 12.1 us -> 10.3 us  [to_others(): got.append(lax.ppermute(x, ('row', 'col'), pairs))]
    ppermute x12, starting transfers between devices: 13.6 us -> 15.4 us  [to_others(): got.append(lax.ppermute(x, ('row', 'col'), pairs))]
where the time goes in v2:
time: 47 us; the launch traced here: 46.5 us
  starting transfers between devices  23.4 us (50%)
  waiting for transfers between devices  14.7 us (31%)
  Pallas kernels  7 us (15%)
  between operations  1.4 us (3%)
    ppermute x12, starting transfers between devices, to_others(): got.append(lax.ppermute(x, ('row', 'col'), pairs))  15.4 us
    ppermute x12, waiting for transfers between devices, to_others(): got.append(lax.ppermute(x, ('row', 'col'), pairs))  10.3 us
    ppermute x3, starting transfers between devices, to_layers(): return lax.ppermute(spill, ('layer', 'row'), pairs)  5.22 us
    ppermute x4, waiting for transfers between devices, to_rows(): return (x, lax.ppermute(x, 'row', [(0, 1), (1, 0)]))  4.35 us
    ppermute x4, starting transfers between devices, to_rows(): return (x, lax.ppermute(x, 'row', [(0, 1), (1, 0)]))  2.83 us
    pallas_call x1, Pallas kernels, local(): call(opening, (lead(slots + META + 2 * blocks), pltpu.VMEM((slots, edge,...  2.72 us
    pallas_call x2, Pallas kernels, local(): call(functools.partial(middle, layers), sent, (VMEM,) * (6 + len(shared)))  1.41 us
    pallas_call x1, Pallas kernels, local(): call(functools.partial(first, layers), sent + (shape(col_blk), shape(col_...  0.94 us
  transfers between devices with their start and end apart: 19, of which 13 were waited for; matrix products, arithmetic and copies ran while one was open for 0% of the time, Pallas kernels for 1%

profile of v2, /device:TPU:1, one launch (start us, length us, event | category | flops | bytes accessed | tf_op | source)
XLA Modules:
  0.0 46.5 jit_solution(6344769493591034355)
XLA Ops:
  1.3 2.7 %shard_map.77 = (f32[1,168,256]{2,1,0:T(8,128)S(1)}, bf16[32,256,256]{2,1,0:T(8,128)(2,1)S(1)}, bf16[32,128]{1,0:T(8,128)(2,1)S(1)}, f32[8,128]{1,0:T(8,128)S(1)}) custom-call(bf16[32,256,256]{2,1,0:T(8,128)(2,1)} %bitcast.9, s32[1,32]{1,0:T(1,128)} %bitcast.13, s32[1,32]{1,0:T(1,128)} %bitcast.14, s32[1,1]{1,0:T(1,128)} %bitcast.8.count_h, ...), custom_call_target="tpu_custom_call" | custom-call | tf_op jit(solution)/shard_map/pallas_call | solution.py:273
  4.1 1.4 %collective-permute-done.rest_1_ = f32[1,168,256]{2,1,0:T(8,128)S(1)} collective-permute-done((f32[1,168,256]{2,1,0:T(8,128)S(1)}, f32[1,168,256]{2,1,0:T(8,128)S(1)}, u32[]{:S(2)}, u32[]{:S(2)}) %collective-permute-start) | collective-permute-done | bytes 172064 | tf_op jit(solution)/shard_map/ppermute | solution.py:234
  5.5 0.9 %shard_map.78 = (f32[72,128]{1,0:T(8,128)S(1)}, bf16[128,256]{1,0:T(8,128)(2,1)S(1)}, f32[128,256]{1,0:T(8,128)S(1)}, f32[128,256]{1,0:T(8,128)S(1)}, f32[128,256]{1,0:T(8,128)S(1)}) custom-call(bf16[32,256,256]{2,1,0:T(8,128)(2,1)S(1)} %get-tuple-element.23.turned, bf16[32,128]{1,0:T(8,128)(2,1)S(1)} %get-tuple-element.24.pick, ...), custom_call_target="tpu_custom_call" | custom-call | tf_op jit(solution)/shard_map/pallas_call | solution.py:286
  6.4 2.4 %collective-permute-start.1 = (bf16[128,256]{1,0:T(8,128)(2,1)S(1)}, bf16[128,256]{1,0:T(8,128)(2,1)S(1)}, u32[]{:S(2)}, u32[]{:S(2)}) collective-permute-start(bf16[128,256]{1,0:T(8,128)(2,1)S(1)} %get-tuple-element.30), channel_id=1, source_target_pairs={{0,4},{4,12},{8,0},{12,20},{16,8},{20,28},{24,16},{28,24},{1,5},{5... | collective-permute-start | bytes 196616 | tf_op jit(solution)/shard_map/ppermute | solution.py:246
  8.9 2.5 %collective-permute-start.4 = (f32[72,128]{1,0:T(8,128)S(1)}, f32[72,128]{1,0:T(8,128)S(1)}, u32[]{:S(2)}, u32[]{:S(2)}) collective-permute-start(f32[72,128]{1,0:T(8,128)S(1)} %get-tuple-element.31.rest_0_), channel_id=1, source_target_pairs={{0,7},{1,6},{2,5},{3,4},{4,3},{5,2},{6,1},{7,0},{8,15},{9,14},{10,... | collective-permute-start | bytes 110600 | tf_op jit(solution)/shard_map/ppermute | solution.py:227
  11.6 1.1 %collective-permute-start.2 = (f32[72,128]{1,0:T(8,128)S(1)}, f32[72,128]{1,0:T(8,128)S(1)}, u32[]{:S(2)}, u32[]{:S(2)}) collective-permute-start(f32[72,128]{1,0:T(8,128)S(1)} %get-tuple-element.31.rest_0_), channel_id=1, source_target_pairs={{0,1},{1,0},{2,3},{3,2},{4,5},{5,4},{6,7},{7,6},{8,9},{9,8},{10,11... | collective-permute-start | bytes 110600 | tf_op jit(solution)/shard_map/ppermute | solution.py:227
  12.7 1.4 %collective-permute-done.4.rest_3_ = f32[72,128]{1,0:T(8,128)S(1)} collective-permute-done((f32[72,128]{1,0:T(8,128)S(1)}, f32[72,128]{1,0:T(8,128)S(1)}, u32[]{:S(2)}, u32[]{:S(2)}) %collective-permute-start.4) | collective-permute-done | bytes 36896 | tf_op jit(solution)/shard_map/ppermute | solution.py:227
  14.0 1.6 %collective-permute-done.3.rest_2_ = f32[72,128]{1,0:T(8,128)S(1)} collective-permute-done((f32[72,128]{1,0:T(8,128)S(1)}, f32[72,128]{1,0:T(8,128)S(1)}, u32[]{:S(2)}, u32[]{:S(2)}) %collective-permute-start.3) | collective-permute-done | bytes 36896 | tf_op jit(solution)/shard_map/ppermute | solution.py:227
  15.9 1.5 %collective-permute-start.5 = (f32[1,128,256]{2,1,0:T(8,128)S(1)}, f32[1,128,256]{2,1,0:T(8,128)S(1)}, u32[]{:S(2)}, u32[]{:S(2)}) collective-permute-start(f32[1,128,256]{2,1,0:T(8,128)S(1)} %shard_map.79.rest_0_), channel_id=1, source_target_pairs={{0,4},{4,0},{1,5},{5,1},{2,6},{6,2},{3,7},{7,3},{8,12},{12,8},{9,1... | collective-permute-start | bytes 393224 | tf_op jit(solution)/shard_map/ppermute | solution.py:234
  17.4 1.0 %collective-permute-done.5.rest_1_ = f32[1,128,256]{2,1,0:T(8,128)S(1)} collective-permute-done((f32[1,128,256]{2,1,0:T(8,128)S(1)}, f32[1,128,256]{2,1,0:T(8,128)S(1)}, u32[]{:S(2)}, u32[]{:S(2)}) %collective-permute-start.5) | collective-permute-done | bytes 131104 | tf_op jit(solution)/shard_map/ppermute | solution.py:234
  18.4 0.7 %shard_map.80 = (f32[72,128]{1,0:T(8,128)S(1)}, bf16[128,256]{1,0:T(8,128)(2,1)S(1)}, f32[128,256]{1,0:T(8,128)S(1)}) custom-call(bf16[32,256,256]{2,1,0:T(8,128)(2,1)S(1)} %get-tuple-element.23.turned, bf16[32,128]{1,0:T(8,128)(2,1)S(1)} %get-tuple-element.24.pick, f32[8,128]{1,0:T(8,128)S(1)} %get-tuple-element.25.marks, ...), custom_call_target="tpu_custom_call" | custom-call | tf_op jit(solution)/shard_map/pallas_call | solution.py:293
  19.1 1.5 %collective-permute-start.6 = (bf16[128,256]{1,0:T(8,128)(2,1)S(1)}, bf16[128,256]{1,0:T(8,128)(2,1)S(1)}, u32[]{:S(2)}, u32[]{:S(2)}) collective-permute-start(bf16[128,256]{1,0:T(8,128)(2,1)S(1)} %get-tuple-element.33), channel_id=1, source_target_pairs={{0,4},{4,12},{8,0},{12,20},{16,8},{20,28},{24,16},{28,24},{1,5},{5... | collective-permute-start | bytes 196616 | tf_op jit(solution)/shard_map/ppermute | solution.py:246
  20.6 0.8 %collective-permute-start.9 = (f32[72,128]{1,0:T(8,128)S(1)}, f32[72,128]{1,0:T(8,128)S(1)}, u32[]{:S(2)}, u32[]{:S(2)}) collective-permute-start(f32[72,128]{1,0:T(8,128)S(1)} %get-tuple-element.34.rest_0_), channel_id=1, source_target_pairs={{0,7},{1,6},{2,5},{3,4},{4,3},{5,2},{6,1},{7,0},{8,15},{9,14},{10,... | collective-permute-start | bytes 110600 | tf_op jit(solution)/shard_map/ppermute | solution.py:227
  21.5 0.7 %collective-permute-start.8 = (f32[72,128]{1,0:T(8,128)S(1)}, f32[72,128]{1,0:T(8,128)S(1)}, u32[]{:S(2)}, u32[]{:S(2)}) collective-permute-start(f32[72,128]{1,0:T(8,128)S(1)} %get-tuple-element.34.rest_0_), channel_id=1, source_target_pairs={{0,6},{1,7},{2,4},{3,5},{4,2},{5,3},{6,0},{7,1},{8,14},{9,15},{10,... | collective-permute-start | bytes 110600 | tf_op jit(solution)/shard_map/ppermute | solution.py:227
  22.1 2.3 %collective-permute-start.7 = (f32[72,128]{1,0:T(8,128)S(1)}, f32[72,128]{1,0:T(8,128)S(1)}, u32[]{:S(2)}, u32[]{:S(2)}) collective-permute-start(f32[72,128]{1,0:T(8,128)S(1)} %get-tuple-element.34.rest_0_), channel_id=1, source_target_pairs={{0,1},{1,0},{2,3},{3,2},{4,5},{5,4},{6,7},{7,6},{8,9},{9,8},{10,11... | collective-permute-start | bytes 110600 | tf_op jit(solution)/shard_map/ppermute | solution.py:227
  24.5 1.7 %collective-permute-done.9.rest_3_ = f32[72,128]{1,0:T(8,128)S(1)} collective-permute-done((f32[72,128]{1,0:T(8,128)S(1)}, f32[72,128]{1,0:T(8,128)S(1)}, u32[]{:S(2)}, u32[]{:S(2)}) %collective-permute-start.9) | collective-permute-done | bytes 36896 | tf_op jit(solution)/shard_map/ppermute | solution.py:227
  26.1 1.4 %collective-permute-done.8.rest_2_ = f32[72,128]{1,0:T(8,128)S(1)} collective-permute-done((f32[72,128]{1,0:T(8,128)S(1)}, f32[72,128]{1,0:T(8,128)S(1)}, u32[]{:S(2)}, u32[]{:S(2)}) %collective-permute-start.8) | collective-permute-done | bytes 36896 | tf_op jit(solution)/shard_map/ppermute | solution.py:227
  27.7 0.6 %collective-permute-start.10 = (f32[1,128,256]{2,1,0:T(8,128)S(1)}, f32[1,128,256]{2,1,0:T(8,128)S(1)}, u32[]{:S(2)}, u32[]{:S(2)}) collective-permute-start(f32[1,128,256]{2,1,0:T(8,128)S(1)} %get-tuple-element.35.rest_0_), channel_id=1, source_target_pairs={{0,4},{4,0},{1,5},{5,1},{2,6},{6,2},{3,7},{7,3},{8,12},{12,8},{9,1... | collective-permute-start | bytes 393224 | tf_op jit(solution)/shard_map/ppermute | solution.py:234
  28.3 1.0 %collective-permute-done.10.rest_1_ = f32[1,128,256]{2,1,0:T(8,128)S(1)} collective-permute-done((f32[1,128,256]{2,1,0:T(8,128)S(1)}, f32[1,128,256]{2,1,0:T(8,128)S(1)}, u32[]{:S(2)}, u32[]{:S(2)}) %collective-permute-start.10) | collective-permute-done | bytes 131104 | tf_op jit(solution)/shard_map/ppermute | solution.py:234
  29.3 0.7 %shard_map.82 = (f32[72,128]{1,0:T(8,128)S(1)}, bf16[128,256]{1,0:T(8,128)(2,1)S(1)}, f32[128,256]{1,0:T(8,128)S(1)}) custom-call(bf16[32,256,256]{2,1,0:T(8,128)(2,1)S(1)} %get-tuple-element.23.turned, bf16[32,128]{1,0:T(8,128)(2,1)S(1)} %get-tuple-element.24.pick, f32[8,128]{1,0:T(8,128)S(1)} %get-tuple-element.25.marks, ...), custom_call_target="tpu_custom_call" | custom-call | tf_op jit(solution)/shard_map/pallas_call | solution.py:293
  30.1 1.3 %collective-permute-start.11 = (bf16[128,256]{1,0:T(8,128)(2,1)S(1)}, bf16[128,256]{1,0:T(8,128)(2,1)S(1)}, u32[]{:S(2)}, u32[]{:S(2)}) collective-permute-start(bf16[128,256]{1,0:T(8,128)(2,1)S(1)} %get-tuple-element.37), channel_id=1, source_target_pairs={{0,4},{4,12},{8,0},{12,20},{16,8},{20,28},{24,16},{28,24},{1,5},{5... | collective-permute-start | bytes 196616 | tf_op jit(solution)/shard_map/ppermute | solution.py:246
  31.4 0.7 %collective-permute-start.14 = (f32[72,128]{1,0:T(8,128)S(1)}, f32[72,128]{1,0:T(8,128)S(1)}, u32[]{:S(2)}, u32[]{:S(2)}) collective-permute-start(f32[72,128]{1,0:T(8,128)S(1)} %get-tuple-element.38.rest_0_), channel_id=1, source_target_pairs={{0,7},{1,6},{2,5},{3,4},{4,3},{5,2},{6,1},{7,0},{8,15},{9,14},{10,... | collective-permute-start | bytes 110600 | tf_op jit(solution)/shard_map/ppermute | solution.py:227
  32.0 1.0 %collective-permute-start.13 = (f32[72,128]{1,0:T(8,128)S(1)}, f32[72,128]{1,0:T(8,128)S(1)}, u32[]{:S(2)}, u32[]{:S(2)}) collective-permute-start(f32[72,128]{1,0:T(8,128)S(1)} %get-tuple-element.38.rest_0_), channel_id=1, source_target_pairs={{0,6},{1,7},{2,4},{3,5},{4,2},{5,3},{6,0},{7,1},{8,14},{9,15},{10,... | collective-permute-start | bytes 110600 | tf_op jit(solution)/shard_map/ppermute | solution.py:227
  33.0 2.2 %collective-permute-start.12 = (f32[72,128]{1,0:T(8,128)S(1)}, f32[72,128]{1,0:T(8,128)S(1)}, u32[]{:S(2)}, u32[]{:S(2)}) collective-permute-start(f32[72,128]{1,0:T(8,128)S(1)} %get-tuple-element.38.rest_0_), channel_id=1, source_target_pairs={{0,1},{1,0},{2,3},{3,2},{4,5},{5,4},{6,7},{7,6},{8,9},{9,8},{10,11... | collective-permute-start | bytes 110600 | tf_op jit(solution)/shard_map/ppermute | solution.py:227
  35.2 1.5 %collective-permute-done.14.rest_3_ = f32[72,128]{1,0:T(8,128)S(1)} collective-permute-done((f32[72,128]{1,0:T(8,128)S(1)}, f32[72,128]{1,0:T(8,128)S(1)}, u32[]{:S(2)}, u32[]{:S(2)}) %collective-permute-start.14) | collective-permute-done | bytes 36896 | tf_op jit(solution)/shard_map/ppermute | solution.py:227
  36.7 1.3 %collective-permute-done.13.rest_2_ = f32[72,128]{1,0:T(8,128)S(1)} collective-permute-done((f32[72,128]{1,0:T(8,128)S(1)}, f32[72,128]{1,0:T(8,128)S(1)}, u32[]{:S(2)}, u32[]{:S(2)}) %collective-permute-start.13) | collective-permute-done | bytes 36896 | tf_op jit(solution)/shard_map/ppermute | solution.py:227
  38.5 0.6 %collective-permute-start.15 = (f32[1,128,256]{2,1,0:T(8,128)S(1)}, f32[1,128,256]{2,1,0:T(8,128)S(1)}, u32[]{:S(2)}, u32[]{:S(2)}) collective-permute-start(f32[1,128,256]{2,1,0:T(8,128)S(1)} %get-tuple-element.39.rest_0_), channel_id=1, source_target_pairs={{0,4},{4,0},{1,5},{5,1},{2,6},{6,2},{3,7},{7,3},{8,12},{12,8},{9,1... | collective-permute-start | bytes 393224 | tf_op jit(solution)/shard_map/ppermute | solution.py:234
  39.1 1.0 %collective-permute-done.15.rest_1_ = f32[1,128,256]{2,1,0:T(8,128)S(1)} collective-permute-done((f32[1,128,256]{2,1,0:T(8,128)S(1)}, f32[1,128,256]{2,1,0:T(8,128)S(1)}, u32[]{:S(2)}, u32[]{:S(2)}) %collective-permute-start.15) | collective-permute-done | bytes 131104 | tf_op jit(solution)/shard_map/ppermute | solution.py:234
  40.1 1.9 %collective-permute-start.18 = (f32[8,128]{1,0:T(8,128)S(1)}, f32[8,128]{1,0:T(8,128)S(1)}, u32[]{:S(2)}, u32[]{:S(2)}) collective-permute-start(f32[8,128]{1,0:T(8,128)S(1)} %get-tuple-element.43.refs_2_), channel_id=1, source_target_pairs={{0,7},{1,6},{2,5},{3,4},{4,3},{5,2},{6,1},{7,0},{8,15},{9,14},{10,... | collective-permute-start | bytes 12296 | tf_op jit(solution)/shard_map/ppermute | solution.py:227
  42.0 2.0 %collective-permute-start.16 = (f32[8,128]{1,0:T(8,128)S(1)}, f32[8,128]{1,0:T(8,128)S(1)}, u32[]{:S(2)}, u32[]{:S(2)}) collective-permute-start(f32[8,128]{1,0:T(8,128)S(1)} %get-tuple-element.43.refs_2_), channel_id=1, source_target_pairs={{0,1},{1,0},{2,3},{3,2},{4,5},{5,4},{6,7},{7,6},{8,9},{9,8},{10,11... | collective-permute-start | bytes 12296 | tf_op jit(solution)/shard_map/ppermute | solution.py:227
  44.0 0.6 %shard_map.85 = f32[128,128]{1,0:T(8,128)} custom-call(f32[128,256]{1,0:T(8,128)S(1)} %get-tuple-element.40.xnew), custom_call_target="tpu_custom_call" | custom-call | tf_op jit(solution)/shard_map/pallas_call | solution.py:306
  45.0 0.9 %collective-permute-done.17.refs_4_ = f32[8,128]{1,0:T(8,128)S(1)} collective-permute-done((f32[8,128]{1,0:T(8,128)S(1)}, f32[8,128]{1,0:T(8,128)S(1)}, u32[]{:S(2)}, u32[]{:S(2)}) %collective-permute-start.17) | collective-permute-done | bytes 4128 | tf_op jit(solution)/shard_map/ppermute | solution.py:227
  (16 shorter events, 2.3 us)
Async XLA Ops:
  4.0 1.5 %collective-permute-start = (f32[1,168,256]{2,1,0:T(8,128)S(1)}, f32[1,168,256]{2,1,0:T(8,128)S(1)}, u32[]{:S(2)}, u32[]{:S(2)}) collective-permute-start(f32[1,168,256]{2,1,0:T(8,128)S(1)} %get-tuple-element.26.rest_0_), channel_id=1, source_target_pairs={{0,4},{4,0},{1,5},{5,1},{2,6},{6,2},{3,7},{7,3},{8,12},{12,8},{9,1... | collective-permute-start | bytes 516104 | tf_op jit(solution)/shard_map/ppermute | solution.py:234
  6.4 9.2 %collective-permute-start.1 = (bf16[128,256]{1,0:T(8,128)(2,1)S(1)}, bf16[128,256]{1,0:T(8,128)(2,1)S(1)}, u32[]{:S(2)}, u32[]{:S(2)}) collective-permute-start(bf16[128,256]{1,0:T(8,128)(2,1)S(1)} %get-tuple-element.30), channel_id=1, source_target_pairs={{0,4},{4,12},{8,0},{12,20},{16,8},{20,28},{24,16},{28,24},{1,5},{5... | collective-permute-start | bytes 196616 | tf_op jit(solution)/shard_map/ppermute | solution.py:246
  8.9 5.2 %collective-permute-start.4 = (f32[72,128]{1,0:T(8,128)S(1)}, f32[72,128]{1,0:T(8,128)S(1)}, u32[]{:S(2)}, u32[]{:S(2)}) collective-permute-start(f32[72,128]{1,0:T(8,128)S(1)} %get-tuple-element.31.rest_0_), channel_id=1, source_target_pairs={{0,7},{1,6},{2,5},{3,4},{4,3},{5,2},{6,1},{7,0},{8,15},{9,14},{10,... | collective-permute-start | bytes 110600 | tf_op jit(solution)/shard_map/ppermute | solution.py:227
  11.4 4.3 %collective-permute-start.3 = (f32[72,128]{1,0:T(8,128)S(1)}, f32[72,128]{1,0:T(8,128)S(1)}, u32[]{:S(2)}, u32[]{:S(2)}) collective-permute-start(f32[72,128]{1,0:T(8,128)S(1)} %get-tuple-element.31.rest_0_), channel_id=1, source_target_pairs={{0,6},{1,7},{2,4},{3,5},{4,2},{5,3},{6,0},{7,1},{8,14},{9,15},{10,... | collective-permute-start | bytes 110600 | tf_op jit(solution)/shard_map/ppermute | solution.py:227
  11.6 4.0 %collective-permute-start.2 = (f32[72,128]{1,0:T(8,128)S(1)}, f32[72,128]{1,0:T(8,128)S(1)}, u32[]{:S(2)}, u32[]{:S(2)}) collective-permute-start(f32[72,128]{1,0:T(8,128)S(1)} %get-tuple-element.31.rest_0_), channel_id=1, source_target_pairs={{0,1},{1,0},{2,3},{3,2},{4,5},{5,4},{6,7},{7,6},{8,9},{9,8},{10,11... | collective-permute-start | bytes 110600 | tf_op jit(solution)/shard_map/ppermute | solution.py:227
  15.9 2.5 %collective-permute-start.5 = (f32[1,128,256]{2,1,0:T(8,128)S(1)}, f32[1,128,256]{2,1,0:T(8,128)S(1)}, u32[]{:S(2)}, u32[]{:S(2)}) collective-permute-start(f32[1,128,256]{2,1,0:T(8,128)S(1)} %shard_map.79.rest_0_), channel_id=1, source_target_pairs={{0,4},{4,0},{1,5},{5,1},{2,6},{6,2},{3,7},{7,3},{8,12},{12,8},{9,1... | collective-permute-start | bytes 393224 | tf_op jit(solution)/shard_map/ppermute | solution.py:234
  19.1 8.3 %collective-permute-start.6 = (bf16[128,256]{1,0:T(8,128)(2,1)S(1)}, bf16[128,256]{1,0:T(8,128)(2,1)S(1)}, u32[]{:S(2)}, u32[]{:S(2)}) collective-permute-start(bf16[128,256]{1,0:T(8,128)(2,1)S(1)} %get-tuple-element.33), channel_id=1, source_target_pairs={{0,4},{4,12},{8,0},{12,20},{16,8},{20,28},{24,16},{28,24},{1,5},{5... | collective-permute-start | bytes 196616 | tf_op jit(solution)/shard_map/ppermute | solution.py:246
  20.6 5.5 %collective-permute-start.9 = (f32[72,128]{1,0:T(8,128)S(1)}, f32[72,128]{1,0:T(8,128)S(1)}, u32[]{:S(2)}, u32[]{:S(2)}) collective-permute-start(f32[72,128]{1,0:T(8,128)S(1)} %get-tuple-element.34.rest_0_), channel_id=1, source_target_pairs={{0,7},{1,6},{2,5},{3,4},{4,3},{5,2},{6,1},{7,0},{8,15},{9,14},{10,... | collective-permute-start | bytes 110600 | tf_op jit(solution)/shard_map/ppermute | solution.py:227
  21.5 6.0 %collective-permute-start.8 = (f32[72,128]{1,0:T(8,128)S(1)}, f32[72,128]{1,0:T(8,128)S(1)}, u32[]{:S(2)}, u32[]{:S(2)}) collective-permute-start(f32[72,128]{1,0:T(8,128)S(1)} %get-tuple-element.34.rest_0_), channel_id=1, source_target_pairs={{0,6},{1,7},{2,4},{3,5},{4,2},{5,3},{6,0},{7,1},{8,14},{9,15},{10,... | collective-permute-start | bytes 110600 | tf_op jit(solution)/shard_map/ppermute | solution.py:227
  22.1 5.3 %collective-permute-start.7 = (f32[72,128]{1,0:T(8,128)S(1)}, f32[72,128]{1,0:T(8,128)S(1)}, u32[]{:S(2)}, u32[]{:S(2)}) collective-permute-start(f32[72,128]{1,0:T(8,128)S(1)} %get-tuple-element.34.rest_0_), channel_id=1, source_target_pairs={{0,1},{1,0},{2,3},{3,2},{4,5},{5,4},{6,7},{7,6},{8,9},{9,8},{10,11... | collective-permute-start | bytes 110600 | tf_op jit(solution)/shard_map/ppermute | solution.py:227
  27.7 1.6 %collective-permute-start.10 = (f32[1,128,256]{2,1,0:T(8,128)S(1)}, f32[1,128,256]{2,1,0:T(8,128)S(1)}, u32[]{:S(2)}, u32[]{:S(2)}) collective-permute-start(f32[1,128,256]{2,1,0:T(8,128)S(1)} %get-tuple-element.35.rest_0_), channel_id=1, source_target_pairs={{0,4},{4,0},{1,5},{5,1},{2,6},{6,2},{3,7},{7,3},{8,12},{12,8},{9,1... | collective-permute-start | bytes 393224 | tf_op jit(solution)/shard_map/ppermute | solution.py:234
  30.1 8.2 %collective-permute-start.11 = (bf16[128,256]{1,0:T(8,128)(2,1)S(1)}, bf16[128,256]{1,0:T(8,128)(2,1)S(1)}, u32[]{:S(2)}, u32[]{:S(2)}) collective-permute-start(bf16[128,256]{1,0:T(8,128)(2,1)S(1)} %get-tuple-element.37), channel_id=1, source_target_pairs={{0,4},{4,12},{8,0},{12,20},{16,8},{20,28},{24,16},{28,24},{1,5},{5... | collective-permute-start | bytes 196616 | tf_op jit(solution)/shard_map/ppermute | solution.py:246
  31.4 5.4 %collective-permute-start.14 = (f32[72,128]{1,0:T(8,128)S(1)}, f32[72,128]{1,0:T(8,128)S(1)}, u32[]{:S(2)}, u32[]{:S(2)}) collective-permute-start(f32[72,128]{1,0:T(8,128)S(1)} %get-tuple-element.38.rest_0_), channel_id=1, source_target_pairs={{0,7},{1,6},{2,5},{3,4},{4,3},{5,2},{6,1},{7,0},{8,15},{9,14},{10,... | collective-permute-start | bytes 110600 | tf_op jit(solution)/shard_map/ppermute | solution.py:227
  32.0 6.0 %collective-permute-start.13 = (f32[72,128]{1,0:T(8,128)S(1)}, f32[72,128]{1,0:T(8,128)S(1)}, u32[]{:S(2)}, u32[]{:S(2)}) collective-permute-start(f32[72,128]{1,0:T(8,128)S(1)} %get-tuple-element.38.rest_0_), channel_id=1, source_target_pairs={{0,6},{1,7},{2,4},{3,5},{4,2},{5,3},{6,0},{7,1},{8,14},{9,15},{10,... | collective-permute-start | bytes 110600 | tf_op jit(solution)/shard_map/ppermute | solution.py:227
  33.0 5.2 %collective-permute-start.12 = (f32[72,128]{1,0:T(8,128)S(1)}, f32[72,128]{1,0:T(8,128)S(1)}, u32[]{:S(2)}, u32[]{:S(2)}) collective-permute-start(f32[72,128]{1,0:T(8,128)S(1)} %get-tuple-element.38.rest_0_), channel_id=1, source_target_pairs={{0,1},{1,0},{2,3},{3,2},{4,5},{5,4},{6,7},{7,6},{8,9},{9,8},{10,11... | collective-permute-start | bytes 110600 | tf_op jit(solution)/shard_map/ppermute | solution.py:227
  38.5 1.6 %collective-permute-start.15 = (f32[1,128,256]{2,1,0:T(8,128)S(1)}, f32[1,128,256]{2,1,0:T(8,128)S(1)}, u32[]{:S(2)}, u32[]{:S(2)}) collective-permute-start(f32[1,128,256]{2,1,0:T(8,128)S(1)} %get-tuple-element.39.rest_0_), channel_id=1, source_target_pairs={{0,4},{4,0},{1,5},{5,1},{2,6},{6,2},{3,7},{7,3},{8,12},{12,8},{9,1... | collective-permute-start | bytes 393224 | tf_op jit(solution)/shard_map/ppermute | solution.py:234
  40.1 4.9 %collective-permute-start.18 = (f32[8,128]{1,0:T(8,128)S(1)}, f32[8,128]{1,0:T(8,128)S(1)}, u32[]{:S(2)}, u32[]{:S(2)}) collective-permute-start(f32[8,128]{1,0:T(8,128)S(1)} %get-tuple-element.43.refs_2_), channel_id=1, source_target_pairs={{0,7},{1,6},{2,5},{3,4},{4,3},{5,2},{6,1},{7,0},{8,15},{9,14},{10,... | collective-permute-start | bytes 12296 | tf_op jit(solution)/shard_map/ppermute | solution.py:227
  42.0 3.9 %collective-permute-start.17 = (f32[8,128]{1,0:T(8,128)S(1)}, f32[8,128]{1,0:T(8,128)S(1)}, u32[]{:S(2)}, u32[]{:S(2)}) collective-permute-start(f32[8,128]{1,0:T(8,128)S(1)} %get-tuple-element.43.refs_2_), channel_id=1, source_target_pairs={{0,6},{1,7},{2,4},{3,5},{4,2},{5,3},{6,0},{7,1},{8,14},{9,15},{10,... | collective-permute-start | bytes 12296 | tf_op jit(solution)/shard_map/ppermute | solution.py:227
  42.0 3.9 %collective-permute-start.16 = (f32[8,128]{1,0:T(8,128)S(1)}, f32[8,128]{1,0:T(8,128)S(1)}, u32[]{:S(2)}, u32[]{:S(2)}) collective-permute-start(f32[8,128]{1,0:T(8,128)S(1)} %get-tuple-element.43.refs_2_), channel_id=1, source_target_pairs={{0,1},{1,0},{2,3},{3,2},{4,5},{5,4},{6,7},{7,6},{8,9},{9,8},{10,11... | collective-permute-start | bytes 12296 | tf_op jit(solution)/shard_map/ppermute | solution.py:227

commit v3 on v2

--- a/solution.py
+++ b/solution.py
@@ -49,8 +49,8 @@
     return jnp.concatenate([ref[pl.ds(w, count, wide), :] for w in range(wide)], axis=1)
 
 
-def opening(values_h, cols_h, rows_h, count_h, x_h, dangling_h, packed, turned, pick, marks,
-            values, cols, rows, count, x, dangling, sems):
+def opening(values_h, cols_h, rows_h, count_h, x_h, dangling_h, packed, values, pick, marks,
+            cols, rows, count, x, dangling, sems):
     slots, edge, _ = values.shape
     blocks = x.shape[0] * 128 // edge
     step = slots // CHUNKS
@@ -84,9 +84,13 @@
         large[k].wait()
         for s in range(k * step, (k + 1) * step):
             block = values[s]
-            turned[s] = block.T
             got = jnp.dot(ones, block, preferred_element_type=F32)
             packed[0, s : s + 1, :] = got[0:1, :]
+
+
+def turn(values, turned):
+    for s in range(values.shape[0]):
+        turned[s] = values[s].T
 
 
 def send_out(layers, pair_rows, x, inv, kinv, turned, pick, marks, payload, spill, xcur):
@@ -270,16 +274,17 @@
     def lead(n):
         return jax.ShapeDtypeStruct((1, n, edge), F32)
 
-    packed, turned, pick, marks = call(
+    packed, values, pick, marks = call(
         opening,
         (lead(slots + META + 2 * blocks), pltpu.VMEM((slots, edge, edge), BF16),
          pltpu.VMEM((slots, col_blk), BF16), pltpu.VMEM((META, LANES), F32)),
         (HBM, HBM, HBM, pl.BlockSpec(memory_space=pl.ANY), HBM, HBM),
-        [pltpu.VMEM((slots, edge, edge), BF16), pltpu.VMEM((1, slots), jnp.int32),
+        [pltpu.VMEM((1, slots), jnp.int32),
          pltpu.VMEM((1, slots), jnp.int32), pltpu.VMEM((1, 1), jnp.int32), pltpu.VMEM(flat, F32),
          pltpu.VMEM(flat, jnp.int32), pltpu.SemaphoreType.DMA((5 + CHUNKS,))],
     )(*arguments)
     shared = to_rows(packed)
+    turned = call(turn, pltpu.VMEM((slots, edge, edge), BF16), (VMEM,))(values)
     lanes = jax.ShapeDtypeStruct((META, LANES), F32)
     products = jax.ShapeDtypeStruct((slots * edge // LANES + META, LANES), F32)
     sent = (products, shape(2 * blocks, BF16), shape(col_blk))

time: 47 us -> 46.9 us (level)
  waiting for transfers between devices: 14.7 us -> 13.6 us
  Pallas kernels: 7 us -> 8.02 us
    ppermute x4, waiting for transfers between devices: 4.35 us -> 3.21 us  [to_rows(): return (x, lax.ppermute(x, 'row', [(0, 1), (1, 0)]))]
    pallas_call x0 -> x1, Pallas kernels: none -> 1.13 us  [local(): turned = call(turn, pltpu.VMEM((slots, edge, edge), BF16), (VMEM,))(values)]
  transfers between devices with their start and end apart: 19 -> 19, of which waited for: 13 -> 13; matrix products, arithmetic and copies ran while one was open for 0% -> 0% of each run, Pallas kernels for 1% -> 4%
where the time goes in v3:
time: 46.9 us; the launch traced here: 46.5 us
  starting transfers between devices  23.4 us (50%)
  waiting for transfers between devices  13.6 us (29%)
  Pallas kernels  8.02 us (17%)
  between operations  1.4 us (3%)
    ppermute x12, starting transfers between devices, to_others(): got.append(lax.ppermute(x, ('row', 'col'), pairs))  15.4 us
    ppermute x12, waiting for transfers between devices, to_others(): got.append(lax.ppermute(x, ('row', 'col'), pairs))  10.4 us
    ppermute x3, starting transfers between devices, to_layers(): return lax.ppermute(spill, ('layer', 'row'), pairs)  5.24 us
    ppermute x4, waiting for transfers between devices, to_rows(): return (x, lax.ppermute(x, 'row', [(0, 1), (1, 0)]))  3.21 us
    ppermute x4, starting transfers between devices, to_rows(): return (x, lax.ppermute(x, 'row', [(0, 1), (1, 0)]))  2.81 us
    pallas_call x1, Pallas kernels, local(): call(opening, (lead(slots + META + 2 * blocks), pltpu.VMEM((slots, edge,...  2.61 us
    pallas_call x2, Pallas kernels, local(): call(functools.partial(middle, layers), sent, (VMEM,) * (6 + len(shared)))  1.41 us
    pallas_call x1, Pallas kernels, local(): turned = call(turn, pltpu.VMEM((slots, edge, edge), BF16), (VMEM,))(values)  1.13 us
  transfers between devices with their start and end apart: 19, of which 13 were waited for; matrix products, arithmetic and copies ran while one was open for 0% of the time, Pallas kernels for 4%

profile of v3, /device:TPU:1, one launch (start us, length us, event | category | flops | bytes accessed | tf_op | source)
XLA Modules:
  0.0 46.5 jit_solution(6667656839106344113)
XLA Ops:
  1.3 2.6 %shard_map.77 = (f32[1,168,256]{2,1,0:T(8,128)S(1)}, bf16[32,256,256]{2,1,0:T(8,128)(2,1)S(1)}, bf16[32,128]{1,0:T(8,128)(2,1)S(1)}, f32[8,128]{1,0:T(8,128)S(1)}) custom-call(bf16[32,256,256]{2,1,0:T(8,128)(2,1)} %bitcast.9, s32[1,32]{1,0:T(1,128)} %bitcast.13, s32[1,32]{1,0:T(1,128)} %bitcast.14, s32[1,1]{1,0:T(1,128)} %bitcast.8.count_h, ...), custom_call_target="tpu_custom_call" | custom-call | tf_op jit(solution)/shard_map/pallas_call | solution.py:277
  4.0 1.1 %shard_map.78.turned = bf16[32,256,256]{2,1,0:T(8,128)(2,1)S(1)} custom-call(bf16[32,256,256]{2,1,0:T(8,128)(2,1)S(1)} %get-tuple-element.23.values), custom_call_target="tpu_custom_call" | custom-call | tf_op jit(solution)/shard_map/pallas_call | solution.py:287
  5.4 0.9 %shard_map.79 = (f32[72,128]{1,0:T(8,128)S(1)}, bf16[128,256]{1,0:T(8,128)(2,1)S(1)}, f32[128,256]{1,0:T(8,128)S(1)}, f32[128,256]{1,0:T(8,128)S(1)}, f32[128,256]{1,0:T(8,128)S(1)}) custom-call(bf16[32,256,256]{2,1,0:T(8,128)(2,1)S(1)} %shard_map.78.turned, bf16[32,128]{1,0:T(8,128)(2,1)S(1)} %get-tuple-element.24.pick, ...), custom_call_target="tpu_custom_call" | custom-call | tf_op jit(solution)/shard_map/pallas_call | solution.py:291
  6.3 2.5 %collective-permute-start.1 = (bf16[128,256]{1,0:T(8,128)(2,1)S(1)}, bf16[128,256]{1,0:T(8,128)(2,1)S(1)}, u32[]{:S(2)}, u32[]{:S(2)}) collective-permute-start(bf16[128,256]{1,0:T(8,128)(2,1)S(1)} %get-tuple-element.30), channel_id=1, source_target_pairs={{0,4},{4,12},{8,0},{12,20},{16,8},{20,28},{24,16},{28,24},{1,5},{5... | collective-permute-start | bytes 196616 | tf_op jit(solution)/shard_map/ppermute | solution.py:250
  8.9 2.5 %collective-permute-start.4 = (f32[72,128]{1,0:T(8,128)S(1)}, f32[72,128]{1,0:T(8,128)S(1)}, u32[]{:S(2)}, u32[]{:S(2)}) collective-permute-start(f32[72,128]{1,0:T(8,128)S(1)} %get-tuple-element.31.rest_0_), channel_id=1, source_target_pairs={{0,7},{1,6},{2,5},{3,4},{4,3},{5,2},{6,1},{7,0},{8,15},{9,14},{10,... | collective-permute-start | bytes 110600 | tf_op jit(solution)/shard_map/ppermute | solution.py:231
  11.6 1.1 %collective-permute-start.2 = (f32[72,128]{1,0:T(8,128)S(1)}, f32[72,128]{1,0:T(8,128)S(1)}, u32[]{:S(2)}, u32[]{:S(2)}) collective-permute-start(f32[72,128]{1,0:T(8,128)S(1)} %get-tuple-element.31.rest_0_), channel_id=1, source_target_pairs={{0,1},{1,0},{2,3},{3,2},{4,5},{5,4},{6,7},{7,6},{8,9},{9,8},{10,11... | collective-permute-start | bytes 110600 | tf_op jit(solution)/shard_map/ppermute | solution.py:231
  12.7 1.4 %collective-permute-done.4.rest_3_ = f32[72,128]{1,0:T(8,128)S(1)} collective-permute-done((f32[72,128]{1,0:T(8,128)S(1)}, f32[72,128]{1,0:T(8,128)S(1)}, u32[]{:S(2)}, u32[]{:S(2)}) %collective-permute-start.4) | collective-permute-done | bytes 36896 | tf_op jit(solution)/shard_map/ppermute | solution.py:231
  14.0 1.6 %collective-permute-done.3.rest_2_ = f32[72,128]{1,0:T(8,128)S(1)} collective-permute-done((f32[72,128]{1,0:T(8,128)S(1)}, f32[72,128]{1,0:T(8,128)S(1)}, u32[]{:S(2)}, u32[]{:S(2)}) %collective-permute-start.3) | collective-permute-done | bytes 36896 | tf_op jit(solution)/shard_map/ppermute | solution.py:231
  15.9 1.5 %collective-permute-start.5 = (f32[1,128,256]{2,1,0:T(8,128)S(1)}, f32[1,128,256]{2,1,0:T(8,128)S(1)}, u32[]{:S(2)}, u32[]{:S(2)}) collective-permute-start(f32[1,128,256]{2,1,0:T(8,128)S(1)} %shard_map.80.rest_0_), channel_id=1, source_target_pairs={{0,4},{4,0},{1,5},{5,1},{2,6},{6,2},{3,7},{7,3},{8,12},{12,8},{9,1... | collective-permute-start | bytes 393224 | tf_op jit(solution)/shard_map/ppermute | solution.py:238
  17.4 1.0 %collective-permute-done.5.rest_1_ = f32[1,128,256]{2,1,0:T(8,128)S(1)} collective-permute-done((f32[1,128,256]{2,1,0:T(8,128)S(1)}, f32[1,128,256]{2,1,0:T(8,128)S(1)}, u32[]{:S(2)}, u32[]{:S(2)}) %collective-permute-start.5) | collective-permute-done | bytes 131104 | tf_op jit(solution)/shard_map/ppermute | solution.py:238
  18.4 0.7 %shard_map.81 = (f32[72,128]{1,0:T(8,128)S(1)}, bf16[128,256]{1,0:T(8,128)(2,1)S(1)}, f32[128,256]{1,0:T(8,128)S(1)}) custom-call(bf16[32,256,256]{2,1,0:T(8,128)(2,1)S(1)} %shard_map.78.turned, bf16[32,128]{1,0:T(8,128)(2,1)S(1)} %get-tuple-element.24.pick, f32[8,128]{1,0:T(8,128)S(1)} %get-tuple-element.25.marks, f32[128,256]{1,0:T(8,128)S(1)} %get-tuple-element.27.inv_i, ...), custom_call_target="tpu_custom_call" | custom-call | tf_op jit(solution)/shard_map/pallas_call | solution.py:298
  19.1 1.5 %collective-permute-start.6 = (bf16[128,256]{1,0:T(8,128)(2,1)S(1)}, bf16[128,256]{1,0:T(8,128)(2,1)S(1)}, u32[]{:S(2)}, u32[]{:S(2)}) collective-permute-start(bf16[128,256]{1,0:T(8,128)(2,1)S(1)} %get-tuple-element.33), channel_id=1, source_target_pairs={{0,4},{4,12},{8,0},{12,20},{16,8},{20,28},{24,16},{28,24},{1,5},{5... | collective-permute-start | bytes 196616 | tf_op jit(solution)/shard_map/ppermute | solution.py:250
  20.6 0.8 %collective-permute-start.9 = (f32[72,128]{1,0:T(8,128)S(1)}, f32[72,128]{1,0:T(8,128)S(1)}, u32[]{:S(2)}, u32[]{:S(2)}) collective-permute-start(f32[72,128]{1,0:T(8,128)S(1)} %get-tuple-element.34.rest_0_), channel_id=1, source_target_pairs={{0,7},{1,6},{2,5},{3,4},{4,3},{5,2},{6,1},{7,0},{8,15},{9,14},{10,... | collective-permute-start | bytes 110600 | tf_op jit(solution)/shard_map/ppermute | solution.py:231
  21.5 0.7 %collective-permute-start.8 = (f32[72,128]{1,0:T(8,128)S(1)}, f32[72,128]{1,0:T(8,128)S(1)}, u32[]{:S(2)}, u32[]{:S(2)}) collective-permute-start(f32[72,128]{1,0:T(8,128)S(1)} %get-tuple-element.34.rest_0_), channel_id=1, source_target_pairs={{0,6},{1,7},{2,4},{3,5},{4,2},{5,3},{6,0},{7,1},{8,14},{9,15},{10,... | collective-permute-start | bytes 110600 | tf_op jit(solution)/shard_map/ppermute | solution.py:231
  22.1 2.3 %collective-permute-start.7 = (f32[72,128]{1,0:T(8,128)S(1)}, f32[72,128]{1,0:T(8,128)S(1)}, u32[]{:S(2)}, u32[]{:S(2)}) collective-permute-start(f32[72,128]{1,0:T(8,128)S(1)} %get-tuple-element.34.rest_0_), channel_id=1, source_target_pairs={{0,1},{1,0},{2,3},{3,2},{4,5},{5,4},{6,7},{7,6},{8,9},{9,8},{10,11... | collective-permute-start | bytes 110600 | tf_op jit(solution)/shard_map/ppermute | solution.py:231
  24.4 1.6 %collective-permute-done.9.rest_3_ = f32[72,128]{1,0:T(8,128)S(1)} collective-permute-done((f32[72,128]{1,0:T(8,128)S(1)}, f32[72,128]{1,0:T(8,128)S(1)}, u32[]{:S(2)}, u32[]{:S(2)}) %collective-permute-start.9) | collective-permute-done | bytes 36896 | tf_op jit(solution)/shard_map/ppermute | solution.py:231
  26.1 1.4 %collective-permute-done.8.rest_2_ = f32[72,128]{1,0:T(8,128)S(1)} collective-permute-done((f32[72,128]{1,0:T(8,128)S(1)}, f32[72,128]{1,0:T(8,128)S(1)}, u32[]{:S(2)}, u32[]{:S(2)}) %collective-permute-start.8) | collective-permute-done | bytes 36896 | tf_op jit(solution)/shard_map/ppermute | solution.py:231
  27.7 0.6 %collective-permute-start.10 = (f32[1,128,256]{2,1,0:T(8,128)S(1)}, f32[1,128,256]{2,1,0:T(8,128)S(1)}, u32[]{:S(2)}, u32[]{:S(2)}) collective-permute-start(f32[1,128,256]{2,1,0:T(8,128)S(1)} %get-tuple-element.35.rest_0_), channel_id=1, source_target_pairs={{0,4},{4,0},{1,5},{5,1},{2,6},{6,2},{3,7},{7,3},{8,12},{12,8},{9,1... | collective-permute-start | bytes 393224 | tf_op jit(solution)/shard_map/ppermute | solution.py:238
  28.3 1.0 %collective-permute-done.10.rest_1_ = f32[1,128,256]{2,1,0:T(8,128)S(1)} collective-permute-done((f32[1,128,256]{2,1,0:T(8,128)S(1)}, f32[1,128,256]{2,1,0:T(8,128)S(1)}, u32[]{:S(2)}, u32[]{:S(2)}) %collective-permute-start.10) | collective-permute-done | bytes 131104 | tf_op jit(solution)/shard_map/ppermute | solution.py:238
  29.3 0.7 %shard_map.83 = (f32[72,128]{1,0:T(8,128)S(1)}, bf16[128,256]{1,0:T(8,128)(2,1)S(1)}, f32[128,256]{1,0:T(8,128)S(1)}) custom-call(bf16[32,256,256]{2,1,0:T(8,128)(2,1)S(1)} %shard_map.78.turned, bf16[32,128]{1,0:T(8,128)(2,1)S(1)} %get-tuple-element.24.pick, f32[8,128]{1,0:T(8,128)S(1)} %get-tuple-element.25.marks, f32[128,256]{1,0:T(8,128)S(1)} %get-tuple-element.27.inv_i, ...), custom_call_target="tpu_custom_call" | custom-call | tf_op jit(solution)/shard_map/pallas_call | solution.py:298
  30.0 1.2 %collective-permute-start.11 = (bf16[128,256]{1,0:T(8,128)(2,1)S(1)}, bf16[128,256]{1,0:T(8,128)(2,1)S(1)}, u32[]{:S(2)}, u32[]{:S(2)}) collective-permute-start(bf16[128,256]{1,0:T(8,128)(2,1)S(1)} %get-tuple-element.37), channel_id=1, source_target_pairs={{0,4},{4,12},{8,0},{12,20},{16,8},{20,28},{24,16},{28,24},{1,5},{5... | collective-permute-start | bytes 196616 | tf_op jit(solution)/shard_map/ppermute | solution.py:250
  31.3 0.8 %collective-permute-start.14 = (f32[72,128]{1,0:T(8,128)S(1)}, f32[72,128]{1,0:T(8,128)S(1)}, u32[]{:S(2)}, u32[]{:S(2)}) collective-permute-start(f32[72,128]{1,0:T(8,128)S(1)} %get-tuple-element.38.rest_0_), channel_id=1, source_target_pairs={{0,7},{1,6},{2,5},{3,4},{4,3},{5,2},{6,1},{7,0},{8,15},{9,14},{10,... | collective-permute-start | bytes 110600 | tf_op jit(solution)/shard_map/ppermute | solution.py:231
  32.0 1.0 %collective-permute-start.13 = (f32[72,128]{1,0:T(8,128)S(1)}, f32[72,128]{1,0:T(8,128)S(1)}, u32[]{:S(2)}, u32[]{:S(2)}) collective-permute-start(f32[72,128]{1,0:T(8,128)S(1)} %get-tuple-element.38.rest_0_), channel_id=1, source_target_pairs={{0,6},{1,7},{2,4},{3,5},{4,2},{5,3},{6,0},{7,1},{8,14},{9,15},{10,... | collective-permute-start | bytes 110600 | tf_op jit(solution)/shard_map/ppermute | solution.py:231
  33.0 2.1 %collective-permute-start.12 = (f32[72,128]{1,0:T(8,128)S(1)}, f32[72,128]{1,0:T(8,128)S(1)}, u32[]{:S(2)}, u32[]{:S(2)}) collective-permute-start(f32[72,128]{1,0:T(8,128)S(1)} %get-tuple-element.38.rest_0_), channel_id=1, source_target_pairs={{0,1},{1,0},{2,3},{3,2},{4,5},{5,4},{6,7},{7,6},{8,9},{9,8},{10,11... | collective-permute-start | bytes 110600 | tf_op jit(solution)/shard_map/ppermute | solution.py:231
  35.1 1.5 %collective-permute-done.14.rest_3_ = f32[72,128]{1,0:T(8,128)S(1)} collective-permute-done((f32[72,128]{1,0:T(8,128)S(1)}, f32[72,128]{1,0:T(8,128)S(1)}, u32[]{:S(2)}, u32[]{:S(2)}) %collective-permute-start.14) | collective-permute-done | bytes 36896 | tf_op jit(solution)/shard_map/ppermute | solution.py:231
  36.6 1.3 %collective-permute-done.13.rest_2_ = f32[72,128]{1,0:T(8,128)S(1)} collective-permute-done((f32[72,128]{1,0:T(8,128)S(1)}, f32[72,128]{1,0:T(8,128)S(1)}, u32[]{:S(2)}, u32[]{:S(2)}) %collective-permute-start.13) | collective-permute-done | bytes 36896 | tf_op jit(solution)/shard_map/ppermute | solution.py:231
  39.0 1.0 %collective-permute-done.15.rest_1_ = f32[1,128,256]{2,1,0:T(8,128)S(1)} collective-permute-done((f32[1,128,256]{2,1,0:T(8,128)S(1)}, f32[1,128,256]{2,1,0:T(8,128)S(1)}, u32[]{:S(2)}, u32[]{:S(2)}) %collective-permute-start.15) | collective-permute-done | bytes 131104 | tf_op jit(solution)/shard_map/ppermute | solution.py:238
  40.0 1.9 %collective-permute-start.18 = (f32[8,128]{1,0:T(8,128)S(1)}, f32[8,128]{1,0:T(8,128)S(1)}, u32[]{:S(2)}, u32[]{:S(2)}) collective-permute-start(f32[8,128]{1,0:T(8,128)S(1)} %get-tuple-element.43.refs_2_), channel_id=1, source_target_pairs={{0,7},{1,6},{2,5},{3,4},{4,3},{5,2},{6,1},{7,0},{8,15},{9,14},{10,... | collective-permute-start | bytes 12296 | tf_op jit(solution)/shard_map/ppermute | solution.py:231
  42.0 2.0 %collective-permute-start.16 = (f32[8,128]{1,0:T(8,128)S(1)}, f32[8,128]{1,0:T(8,128)S(1)}, u32[]{:S(2)}, u32[]{:S(2)}) collective-permute-start(f32[8,128]{1,0:T(8,128)S(1)} %get-tuple-element.43.refs_2_), channel_id=1, source_target_pairs={{0,1},{1,0},{2,3},{3,2},{4,5},{5,4},{6,7},{7,6},{8,9},{9,8},{10,11... | collective-permute-start | bytes 12296 | tf_op jit(solution)/shard_map/ppermute | solution.py:231
  43.9 0.6 %shard_map.86 = f32[128,128]{1,0:T(8,128)} custom-call(f32[128,256]{1,0:T(8,128)S(1)} %get-tuple-element.40.xnew), custom_call_target="tpu_custom_call" | custom-call | tf_op jit(solution)/shard_map/pallas_call | solution.py:311
  45.0 0.9 %collective-permute-done.17.refs_4_ = f32[8,128]{1,0:T(8,128)S(1)} collective-permute-done((f32[8,128]{1,0:T(8,128)S(1)}, f32[8,128]{1,0:T(8,128)S(1)}, u32[]{:S(2)}, u32[]{:S(2)}) %collective-permute-start.17) | collective-permute-done | bytes 4128 | tf_op jit(solution)/shard_map/ppermute | solution.py:231
  45.9 0.6 %shard_map.87 = f32[1,3]{1,0:T(1,128)} custom-call(f32[8,128]{1,0:T(8,128)S(1)} %get-tuple-element.41.refs_0_, f32[8,128]{1,0:T(8,128)S(1)} %get-tuple-element.42.refs_1_, f32[8,128]{1,0:T(8,128)S(1)} %get-tuple-element.43.refs_2_, f32[8,128]{1,0:T(8,128)S(1)} %collective-permute-done.16.refs_3_, f32[8,128]{1,0:T(8,128)S(1)} %collective-permute-done.17.refs_4_, ...), custom_call_target="tpu_custom_call" | custom-call | tf_op jit(solution)/shard_map/pallas_call | solution.py:312
  (17 shorter events, 2.5 us)
Async XLA Ops:
  3.9 1.5 %collective-permute-start = (f32[1,168,256]{2,1,0:T(8,128)S(1)}, f32[1,168,256]{2,1,0:T(8,128)S(1)}, u32[]{:S(2)}, u32[]{:S(2)}) collective-permute-start(f32[1,168,256]{2,1,0:T(8,128)S(1)} %get-tuple-element.26.rest_0_), channel_id=1, source_target_pairs={{0,4},{4,0},{1,5},{5,1},{2,6},{6,2},{3,7},{7,3},{8,12},{12,8},{9,1... | collective-permute-start | bytes 516104 | tf_op jit(solution)/shard_map/ppermute | solution.py:238
  6.3 9.3 %collective-permute-start.1 = (bf16[128,256]{1,0:T(8,128)(2,1)S(1)}, bf16[128,256]{1,0:T(8,128)(2,1)S(1)}, u32[]{:S(2)}, u32[]{:S(2)}) collective-permute-start(bf16[128,256]{1,0:T(8,128)(2,1)S(1)} %get-tuple-element.30), channel_id=1, source_target_pairs={{0,4},{4,12},{8,0},{12,20},{16,8},{20,28},{24,16},{28,24},{1,5},{5... | collective-permute-start | bytes 196616 | tf_op jit(solution)/shard_map/ppermute | solution.py:250
  8.9 5.2 %collective-permute-start.4 = (f32[72,128]{1,0:T(8,128)S(1)}, f32[72,128]{1,0:T(8,128)S(1)}, u32[]{:S(2)}, u32[]{:S(2)}) collective-permute-start(f32[72,128]{1,0:T(8,128)S(1)} %get-tuple-element.31.rest_0_), channel_id=1, source_target_pairs={{0,7},{1,6},{2,5},{3,4},{4,3},{5,2},{6,1},{7,0},{8,15},{9,14},{10,... | collective-permute-start | bytes 110600 | tf_op jit(solution)/shard_map/ppermute | solution.py:231
  11.4 4.3 %collective-permute-start.3 = (f32[72,128]{1,0:T(8,128)S(1)}, f32[72,128]{1,0:T(8,128)S(1)}, u32[]{:S(2)}, u32[]{:S(2)}) collective-permute-start(f32[72,128]{1,0:T(8,128)S(1)} %get-tuple-element.31.rest_0_), channel_id=1, source_target_pairs={{0,6},{1,7},{2,4},{3,5},{4,2},{5,3},{6,0},{7,1},{8,14},{9,15},{10,... | collective-permute-start | bytes 110600 | tf_op jit(solution)/shard_map/ppermute | solution.py:231
  11.6 4.0 %collective-permute-start.2 = (f32[72,128]{1,0:T(8,128)S(1)}, f32[72,128]{1,0:T(8,128)S(1)}, u32[]{:S(2)}, u32[]{:S(2)}) collective-permute-start(f32[72,128]{1,0:T(8,128)S(1)} %get-tuple-element.31.rest_0_), channel_id=1, source_target_pairs={{0,1},{1,0},{2,3},{3,2},{4,5},{5,4},{6,7},{7,6},{8,9},{9,8},{10,11... | collective-permute-start | bytes 110600 | tf_op jit(solution)/shard_map/ppermute | solution.py:231
  15.9 2.5 %collective-permute-start.5 = (f32[1,128,256]{2,1,0:T(8,128)S(1)}, f32[1,128,256]{2,1,0:T(8,128)S(1)}, u32[]{:S(2)}, u32[]{:S(2)}) collective-permute-start(f32[1,128,256]{2,1,0:T(8,128)S(1)} %shard_map.80.rest_0_), channel_id=1, source_target_pairs={{0,4},{4,0},{1,5},{5,1},{2,6},{6,2},{3,7},{7,3},{8,12},{12,8},{9,1... | collective-permute-start | bytes 393224 | tf_op jit(solution)/shard_map/ppermute | solution.py:238
  19.1 8.3 %collective-permute-start.6 = (bf16[128,256]{1,0:T(8,128)(2,1)S(1)}, bf16[128,256]{1,0:T(8,128)(2,1)S(1)}, u32[]{:S(2)}, u32[]{:S(2)}) collective-permute-start(bf16[128,256]{1,0:T(8,128)(2,1)S(1)} %get-tuple-element.33), channel_id=1, source_target_pairs={{0,4},{4,12},{8,0},{12,20},{16,8},{20,28},{24,16},{28,24},{1,5},{5... | collective-permute-start | bytes 196616 | tf_op jit(solution)/shard_map/ppermute | solution.py:250
  20.6 5.5 %collective-permute-start.9 = (f32[72,128]{1,0:T(8,128)S(1)}, f32[72,128]{1,0:T(8,128)S(1)}, u32[]{:S(2)}, u32[]{:S(2)}) collective-permute-start(f32[72,128]{1,0:T(8,128)S(1)} %get-tuple-element.34.rest_0_), channel_id=1, source_target_pairs={{0,7},{1,6},{2,5},{3,4},{4,3},{5,2},{6,1},{7,0},{8,15},{9,14},{10,... | collective-permute-start | bytes 110600 | tf_op jit(solution)/shard_map/ppermute | solution.py:231
  21.5 6.0 %collective-permute-start.8 = (f32[72,128]{1,0:T(8,128)S(1)}, f32[72,128]{1,0:T(8,128)S(1)}, u32[]{:S(2)}, u32[]{:S(2)}) collective-permute-start(f32[72,128]{1,0:T(8,128)S(1)} %get-tuple-element.34.rest_0_), channel_id=1, source_target_pairs={{0,6},{1,7},{2,4},{3,5},{4,2},{5,3},{6,0},{7,1},{8,14},{9,15},{10,... | collective-permute-start | bytes 110600 | tf_op jit(solution)/shard_map/ppermute | solution.py:231
  22.1 5.3 %collective-permute-start.7 = (f32[72,128]{1,0:T(8,128)S(1)}, f32[72,128]{1,0:T(8,128)S(1)}, u32[]{:S(2)}, u32[]{:S(2)}) collective-permute-start(f32[72,128]{1,0:T(8,128)S(1)} %get-tuple-element.34.rest_0_), channel_id=1, source_target_pairs={{0,1},{1,0},{2,3},{3,2},{4,5},{5,4},{6,7},{7,6},{8,9},{9,8},{10,11... | collective-permute-start | bytes 110600 | tf_op jit(solution)/shard_map/ppermute | solution.py:231
  27.7 1.6 %collective-permute-start.10 = (f32[1,128,256]{2,1,0:T(8,128)S(1)}, f32[1,128,256]{2,1,0:T(8,128)S(1)}, u32[]{:S(2)}, u32[]{:S(2)}) collective-permute-start(f32[1,128,256]{2,1,0:T(8,128)S(1)} %get-tuple-element.35.rest_0_), channel_id=1, source_target_pairs={{0,4},{4,0},{1,5},{5,1},{2,6},{6,2},{3,7},{7,3},{8,12},{12,8},{9,1... | collective-permute-start | bytes 393224 | tf_op jit(solution)/shard_map/ppermute | solution.py:238
  30.0 8.1 %collective-permute-start.11 = (bf16[128,256]{1,0:T(8,128)(2,1)S(1)}, bf16[128,256]{1,0:T(8,128)(2,1)S(1)}, u32[]{:S(2)}, u32[]{:S(2)}) collective-permute-start(bf16[128,256]{1,0:T(8,128)(2,1)S(1)} %get-tuple-element.37), channel_id=1, source_target_pairs={{0,4},{4,12},{8,0},{12,20},{16,8},{20,28},{24,16},{28,24},{1,5},{5... | collective-permute-start | bytes 196616 | tf_op jit(solution)/shard_map/ppermute | solution.py:250
  31.3 5.4 %collective-permute-start.14 = (f32[72,128]{1,0:T(8,128)S(1)}, f32[72,128]{1,0:T(8,128)S(1)}, u32[]{:S(2)}, u32[]{:S(2)}) collective-permute-start(f32[72,128]{1,0:T(8,128)S(1)} %get-tuple-element.38.rest_0_), channel_id=1, source_target_pairs={{0,7},{1,6},{2,5},{3,4},{4,3},{5,2},{6,1},{7,0},{8,15},{9,14},{10,... | collective-permute-start | bytes 110600 | tf_op jit(solution)/shard_map/ppermute | solution.py:231
  32.0 6.0 %collective-permute-start.13 = (f32[72,128]{1,0:T(8,128)S(1)}, f32[72,128]{1,0:T(8,128)S(1)}, u32[]{:S(2)}, u32[]{:S(2)}) collective-permute-start(f32[72,128]{1,0:T(8,128)S(1)} %get-tuple-element.38.rest_0_), channel_id=1, source_target_pairs={{0,6},{1,7},{2,4},{3,5},{4,2},{5,3},{6,0},{7,1},{8,14},{9,15},{10,... | collective-permute-start | bytes 110600 | tf_op jit(solution)/shard_map/ppermute | solution.py:231
  33.0 5.2 %collective-permute-start.12 = (f32[72,128]{1,0:T(8,128)S(1)}, f32[72,128]{1,0:T(8,128)S(1)}, u32[]{:S(2)}, u32[]{:S(2)}) collective-permute-start(f32[72,128]{1,0:T(8,128)S(1)} %get-tuple-element.38.rest_0_), channel_id=1, source_target_pairs={{0,1},{1,0},{2,3},{3,2},{4,5},{5,4},{6,7},{7,6},{8,9},{9,8},{10,11... | collective-permute-start | bytes 110600 | tf_op jit(solution)/shard_map/ppermute | solution.py:231
  38.4 1.6 %collective-permute-start.15 = (f32[1,128,256]{2,1,0:T(8,128)S(1)}, f32[1,128,256]{2,1,0:T(8,128)S(1)}, u32[]{:S(2)}, u32[]{:S(2)}) collective-permute-start(f32[1,128,256]{2,1,0:T(8,128)S(1)} %get-tuple-element.39.rest_0_), channel_id=1, source_target_pairs={{0,4},{4,0},{1,5},{5,1},{2,6},{6,2},{3,7},{7,3},{8,12},{12,8},{9,1... | collective-permute-start | bytes 393224 | tf_op jit(solution)/shard_map/ppermute | solution.py:238
  40.0 4.9 %collective-permute-start.18 = (f32[8,128]{1,0:T(8,128)S(1)}, f32[8,128]{1,0:T(8,128)S(1)}, u32[]{:S(2)}, u32[]{:S(2)}) collective-permute-start(f32[8,128]{1,0:T(8,128)S(1)} %get-tuple-element.43.refs_2_), channel_id=1, source_target_pairs={{0,7},{1,6},{2,5},{3,4},{4,3},{5,2},{6,1},{7,0},{8,15},{9,14},{10,... | collective-permute-start | bytes 12296 | tf_op jit(solution)/shard_map/ppermute | solution.py:231
  41.9 3.9 %collective-permute-start.17 = (f32[8,128]{1,0:T(8,128)S(1)}, f32[8,128]{1,0:T(8,128)S(1)}, u32[]{:S(2)}, u32[]{:S(2)}) collective-permute-start(f32[8,128]{1,0:T(8,128)S(1)} %get-tuple-element.43.refs_2_), channel_id=1, source_target_pairs={{0,6},{1,7},{2,4},{3,5},{4,2},{5,3},{6,0},{7,1},{8,14},{9,15},{10,... | collective-permute-start | bytes 12296 | tf_op jit(solution)/shard_map/ppermute | solution.py:231
  42.0 3.9 %collective-permute-start.16 = (f32[8,128]{1,0:T(8,128)S(1)}, f32[8,128]{1,0:T(8,128)S(1)}, u32[]{:S(2)}, u32[]{:S(2)}) collective-permute-start(f32[8,128]{1,0:T(8,128)S(1)} %get-tuple-element.43.refs_2_), channel_id=1, source_target_pairs={{0,1},{1,0},{2,3},{3,2},{4,5},{5,4},{6,7},{7,6},{8,9},{9,8},{10,11... | collective-permute-start | bytes 12296 | tf_op jit(solution)/shard_map/ppermute | solution.py:231

commit v4 on v3

--- a/solution.py
+++ b/solution.py
@@ -41,6 +41,12 @@
     return jnp.dot(onehot, hi, preferred_element_type=F32) + jnp.dot(
         onehot, lo, preferred_element_type=F32
     )
+
+
+def tree(terms):
+    while len(terms) > 1:
+        terms = [sum(terms[k + 1 : k + 2], terms[k]) for k in range(0, len(terms), 2)]
+    return terms[0]
 
 
 def to_blocks(ref, edge):
@@ -177,13 +183,13 @@
     odd = lax.axis_index("row") % 2
     first_block = (lax.axis_index("col") * blocks).astype(F32)
     block_ids = lax.broadcasted_iota(jnp.int32, (blocks, slots), 0).astype(F32) + first_block
-    walks, sums = [], None
+    walks, extras = [], []
     for pay in pays:
         onehot = (block_ids == pay[meta : meta + 1, 0:slots]).astype(BF16)
         terms = [pay[w * slots : (w + 1) * slots, :] for w in range(wide)]
         walks.append(place(onehot, jnp.concatenate(terms, axis=1)))
-        extra = pay[meta : meta + META, :]
-        sums = extra if sums is None else sums + extra
+        extras.append(pay[meta : meta + META, :])
+    sums = tree(extras)
     mass = jnp.sum(sums[1:2, :], axis=1, keepdims=True)
     if not early:
         outs[1][...] = sums
@@ -214,7 +220,7 @@
 
 def totals(*refs):
     early, late, out = refs[: ITERS - 1], refs[ITERS - 1 : -1], refs[-1]
-    rows = [ref[2:3, :] for ref in early] + [sum(ref[0:1, :] for ref in late)]
+    rows = [ref[2:3, :] for ref in early] + [tree([ref[0:1, :] for ref in late])]
     for t, row in enumerate(rows):
         out[0:1, t : t + 1] = jnp.sum(row, axis=1, keepdims=True)
 

time: 46.9 us -> 46.9 us (level)
  no operation moved by 1% of the time
where the time goes in v4:
time: 46.9 us; the launch traced here: 46.5 us
  starting transfers between devices  23.4 us (50%)
  waiting for transfers between devices  13.7 us (29%)
  Pallas kernels  8.02 us (17%)
  between operations  1.4 us (3%)
    ppermute x12, starting transfers between devices, to_others(): got.append(lax.ppermute(x, ('row', 'col'), pairs))  15.4 us
    ppermute x12, waiting for transfers between devices, to_others(): got.append(lax.ppermute(x, ('row', 'col'), pairs))  10.4 us
    ppermute x3, starting transfers between devices, to_layers(): return lax.ppermute(spill, ('layer', 'row'), pairs)  5.22 us
    ppermute x4, waiting for transfers between devices, to_rows(): return (x, lax.ppermute(x, 'row', [(0, 1), (1, 0)]))  3.21 us
    ppermute x4, starting transfers between devices, to_rows(): return (x, lax.ppermute(x, 'row', [(0, 1), (1, 0)]))  2.82 us
    pallas_call x1, Pallas kernels, local(): call(opening, (lead(slots + META + 2 * blocks), pltpu.VMEM((slots, edge,...  2.61 us
    pallas_call x2, Pallas kernels, local(): call(functools.partial(middle, layers), sent, (VMEM,) * (6 + len(shared)))  1.41 us
    pallas_call x1, Pallas kernels, local(): turned = call(turn, pltpu.VMEM((slots, edge, edge), BF16), (VMEM,))(values)  1.13 us
  transfers between devices with their start and end apart: 19, of which 13 were waited for; matrix products, arithmetic and copies ran while one was open for 0% of the time, Pallas kernels for 4%

profile of v4, /device:TPU:1, one launch (start us, length us, event | category | flops | bytes accessed | tf_op | source)
XLA Modules:
  0.0 46.5 jit_solution(6861396762437406187)
XLA Ops:
  1.3 2.6 %shard_map.77 = (f32[1,168,256]{2,1,0:T(8,128)S(1)}, bf16[32,256,256]{2,1,0:T(8,128)(2,1)S(1)}, bf16[32,128]{1,0:T(8,128)(2,1)S(1)}, f32[8,128]{1,0:T(8,128)S(1)}) custom-call(bf16[32,256,256]{2,1,0:T(8,128)(2,1)} %bitcast.9, s32[1,32]{1,0:T(1,128)} %bitcast.13, s32[1,32]{1,0:T(1,128)} %bitcast.14, s32[1,1]{1,0:T(1,128)} %bitcast.8.count_h, ...), custom_call_target="tpu_custom_call" | custom-call | tf_op jit(solution)/shard_map/pallas_call | solution.py:283
  4.0 1.1 %shard_map.78.turned = bf16[32,256,256]{2,1,0:T(8,128)(2,1)S(1)} custom-call(bf16[32,256,256]{2,1,0:T(8,128)(2,1)S(1)} %get-tuple-element.23.values), custom_call_target="tpu_custom_call" | custom-call | tf_op jit(solution)/shard_map/pallas_call | solution.py:293
  5.4 0.9 %shard_map.79 = (f32[72,128]{1,0:T(8,128)S(1)}, bf16[128,256]{1,0:T(8,128)(2,1)S(1)}, f32[128,256]{1,0:T(8,128)S(1)}, f32[128,256]{1,0:T(8,128)S(1)}, f32[128,256]{1,0:T(8,128)S(1)}) custom-call(bf16[32,256,256]{2,1,0:T(8,128)(2,1)S(1)} %shard_map.78.turned, bf16[32,128]{1,0:T(8,128)(2,1)S(1)} %get-tuple-element.24.pick, ...), custom_call_target="tpu_custom_call" | custom-call | tf_op jit(solution)/shard_map/pallas_call | solution.py:297
  6.3 2.5 %collective-permute-start.1 = (bf16[128,256]{1,0:T(8,128)(2,1)S(1)}, bf16[128,256]{1,0:T(8,128)(2,1)S(1)}, u32[]{:S(2)}, u32[]{:S(2)}) collective-permute-start(bf16[128,256]{1,0:T(8,128)(2,1)S(1)} %get-tuple-element.30), channel_id=1, source_target_pairs={{0,4},{4,12},{8,0},{12,20},{16,8},{20,28},{24,16},{28,24},{1,5},{5... | collective-permute-start | bytes 196616 | tf_op jit(solution)/shard_map/ppermute | solution.py:256
  8.9 2.5 %collective-permute-start.4 = (f32[72,128]{1,0:T(8,128)S(1)}, f32[72,128]{1,0:T(8,128)S(1)}, u32[]{:S(2)}, u32[]{:S(2)}) collective-permute-start(f32[72,128]{1,0:T(8,128)S(1)} %get-tuple-element.31.rest_0_), channel_id=1, source_target_pairs={{0,7},{1,6},{2,5},{3,4},{4,3},{5,2},{6,1},{7,0},{8,15},{9,14},{10,... | collective-permute-start | bytes 110600 | tf_op jit(solution)/shard_map/ppermute | solution.py:237
  11.6 1.1 %collective-permute-start.2 = (f32[72,128]{1,0:T(8,128)S(1)}, f32[72,128]{1,0:T(8,128)S(1)}, u32[]{:S(2)}, u32[]{:S(2)}) collective-permute-start(f32[72,128]{1,0:T(8,128)S(1)} %get-tuple-element.31.rest_0_), channel_id=1, source_target_pairs={{0,1},{1,0},{2,3},{3,2},{4,5},{5,4},{6,7},{7,6},{8,9},{9,8},{10,11... | collective-permute-start | bytes 110600 | tf_op jit(solution)/shard_map/ppermute | solution.py:237
  12.7 1.4 %collective-permute-done.4.rest_3_ = f32[72,128]{1,0:T(8,128)S(1)} collective-permute-done((f32[72,128]{1,0:T(8,128)S(1)}, f32[72,128]{1,0:T(8,128)S(1)}, u32[]{:S(2)}, u32[]{:S(2)}) %collective-permute-start.4) | collective-permute-done | bytes 36896 | tf_op jit(solution)/shard_map/ppermute | solution.py:237
  14.0 1.6 %collective-permute-done.3.rest_2_ = f32[72,128]{1,0:T(8,128)S(1)} collective-permute-done((f32[72,128]{1,0:T(8,128)S(1)}, f32[72,128]{1,0:T(8,128)S(1)}, u32[]{:S(2)}, u32[]{:S(2)}) %collective-permute-start.3) | collective-permute-done | bytes 36896 | tf_op jit(solution)/shard_map/ppermute | solution.py:237
  15.9 1.5 %collective-permute-start.5 = (f32[1,128,256]{2,1,0:T(8,128)S(1)}, f32[1,128,256]{2,1,0:T(8,128)S(1)}, u32[]{:S(2)}, u32[]{:S(2)}) collective-permute-start(f32[1,128,256]{2,1,0:T(8,128)S(1)} %shard_map.80.rest_0_), channel_id=1, source_target_pairs={{0,4},{4,0},{1,5},{5,1},{2,6},{6,2},{3,7},{7,3},{8,12},{12,8},{9,1... | collective-permute-start | bytes 393224 | tf_op jit(solution)/shard_map/ppermute | solution.py:244
  17.4 1.0 %collective-permute-done.5.rest_1_ = f32[1,128,256]{2,1,0:T(8,128)S(1)} collective-permute-done((f32[1,128,256]{2,1,0:T(8,128)S(1)}, f32[1,128,256]{2,1,0:T(8,128)S(1)}, u32[]{:S(2)}, u32[]{:S(2)}) %collective-permute-start.5) | collective-permute-done | bytes 131104 | tf_op jit(solution)/shard_map/ppermute | solution.py:244
  18.4 0.7 %shard_map.81 = (f32[72,128]{1,0:T(8,128)S(1)}, bf16[128,256]{1,0:T(8,128)(2,1)S(1)}, f32[128,256]{1,0:T(8,128)S(1)}) custom-call(bf16[32,256,256]{2,1,0:T(8,128)(2,1)S(1)} %shard_map.78.turned, bf16[32,128]{1,0:T(8,128)(2,1)S(1)} %get-tuple-element.24.pick, f32[8,128]{1,0:T(8,128)S(1)} %get-tuple-element.25.marks, f32[128,256]{1,0:T(8,128)S(1)} %get-tuple-element.27.inv_i, ...), custom_call_target="tpu_custom_call" | custom-call | tf_op jit(solution)/shard_map/pallas_call | solution.py:304
  19.1 1.5 %collective-permute-start.6 = (bf16[128,256]{1,0:T(8,128)(2,1)S(1)}, bf16[128,256]{1,0:T(8,128)(2,1)S(1)}, u32[]{:S(2)}, u32[]{:S(2)}) collective-permute-start(bf16[128,256]{1,0:T(8,128)(2,1)S(1)} %get-tuple-element.33), channel_id=1, source_target_pairs={{0,4},{4,12},{8,0},{12,20},{16,8},{20,28},{24,16},{28,24},{1,5},{5... | collective-permute-start | bytes 196616 | tf_op jit(solution)/shard_map/ppermute | solution.py:256
  20.6 0.8 %collective-permute-start.9 = (f32[72,128]{1,0:T(8,128)S(1)}, f32[72,128]{1,0:T(8,128)S(1)}, u32[]{:S(2)}, u32[]{:S(2)}) collective-permute-start(f32[72,128]{1,0:T(8,128)S(1)} %get-tuple-element.34.rest_0_), channel_id=1, source_target_pairs={{0,7},{1,6},{2,5},{3,4},{4,3},{5,2},{6,1},{7,0},{8,15},{9,14},{10,... | collective-permute-start | bytes 110600 | tf_op jit(solution)/shard_map/ppermute | solution.py:237
  21.5 0.7 %collective-permute-start.8 = (f32[72,128]{1,0:T(8,128)S(1)}, f32[72,128]{1,0:T(8,128)S(1)}, u32[]{:S(2)}, u32[]{:S(2)}) collective-permute-start(f32[72,128]{1,0:T(8,128)S(1)} %get-tuple-element.34.rest_0_), channel_id=1, source_target_pairs={{0,6},{1,7},{2,4},{3,5},{4,2},{5,3},{6,0},{7,1},{8,14},{9,15},{10,... | collective-permute-start | bytes 110600 | tf_op jit(solution)/shard_map/ppermute | solution.py:237
  22.1 2.3 %collective-permute-start.7 = (f32[72,128]{1,0:T(8,128)S(1)}, f32[72,128]{1,0:T(8,128)S(1)}, u32[]{:S(2)}, u32[]{:S(2)}) collective-permute-start(f32[72,128]{1,0:T(8,128)S(1)} %get-tuple-element.34.rest_0_), channel_id=1, source_target_pairs={{0,1},{1,0},{2,3},{3,2},{4,5},{5,4},{6,7},{7,6},{8,9},{9,8},{10,11... | collective-permute-start | bytes 110600 | tf_op jit(solution)/shard_map/ppermute | solution.py:237
  24.4 1.6 %collective-permute-done.9.rest_3_ = f32[72,128]{1,0:T(8,128)S(1)} collective-permute-done((f32[72,128]{1,0:T(8,128)S(1)}, f32[72,128]{1,0:T(8,128)S(1)}, u32[]{:S(2)}, u32[]{:S(2)}) %collective-permute-start.9) | collective-permute-done | bytes 36896 | tf_op jit(solution)/shard_map/ppermute | solution.py:237
  26.1 1.4 %collective-permute-done.8.rest_2_ = f32[72,128]{1,0:T(8,128)S(1)} collective-permute-done((f32[72,128]{1,0:T(8,128)S(1)}, f32[72,128]{1,0:T(8,128)S(1)}, u32[]{:S(2)}, u32[]{:S(2)}) %collective-permute-start.8) | collective-permute-done | bytes 36896 | tf_op jit(solution)/shard_map/ppermute | solution.py:237
  27.7 0.6 %collective-permute-start.10 = (f32[1,128,256]{2,1,0:T(8,128)S(1)}, f32[1,128,256]{2,1,0:T(8,128)S(1)}, u32[]{:S(2)}, u32[]{:S(2)}) collective-permute-start(f32[1,128,256]{2,1,0:T(8,128)S(1)} %get-tuple-element.35.rest_0_), channel_id=1, source_target_pairs={{0,4},{4,0},{1,5},{5,1},{2,6},{6,2},{3,7},{7,3},{8,12},{12,8},{9,1... | collective-permute-start | bytes 393224 | tf_op jit(solution)/shard_map/ppermute | solution.py:244
  28.3 1.0 %collective-permute-done.10.rest_1_ = f32[1,128,256]{2,1,0:T(8,128)S(1)} collective-permute-done((f32[1,128,256]{2,1,0:T(8,128)S(1)}, f32[1,128,256]{2,1,0:T(8,128)S(1)}, u32[]{:S(2)}, u32[]{:S(2)}) %collective-permute-start.10) | collective-permute-done | bytes 131104 | tf_op jit(solution)/shard_map/ppermute | solution.py:244
  29.3 0.7 %shard_map.83 = (f32[72,128]{1,0:T(8,128)S(1)}, bf16[128,256]{1,0:T(8,128)(2,1)S(1)}, f32[128,256]{1,0:T(8,128)S(1)}) custom-call(bf16[32,256,256]{2,1,0:T(8,128)(2,1)S(1)} %shard_map.78.turned, bf16[32,128]{1,0:T(8,128)(2,1)S(1)} %get-tuple-element.24.pick, f32[8,128]{1,0:T(8,128)S(1)} %get-tuple-element.25.marks, f32[128,256]{1,0:T(8,128)S(1)} %get-tuple-element.27.inv_i, ...), custom_call_target="tpu_custom_call" | custom-call | tf_op jit(solution)/shard_map/pallas_call | solution.py:304
  30.0 1.2 %collective-permute-start.11 = (bf16[128,256]{1,0:T(8,128)(2,1)S(1)}, bf16[128,256]{1,0:T(8,128)(2,1)S(1)}, u32[]{:S(2)}, u32[]{:S(2)}) collective-permute-start(bf16[128,256]{1,0:T(8,128)(2,1)S(1)} %get-tuple-element.37), channel_id=1, source_target_pairs={{0,4},{4,12},{8,0},{12,20},{16,8},{20,28},{24,16},{28,24},{1,5},{5... | collective-permute-start | bytes 196616 | tf_op jit(solution)/shard_map/ppermute | solution.py:256
  31.2 0.8 %collective-permute-start.14 = (f32[72,128]{1,0:T(8,128)S(1)}, f32[72,128]{1,0:T(8,128)S(1)}, u32[]{:S(2)}, u32[]{:S(2)}) collective-permute-start(f32[72,128]{1,0:T(8,128)S(1)} %get-tuple-element.38.rest_0_), channel_id=1, source_target_pairs={{0,7},{1,6},{2,5},{3,4},{4,3},{5,2},{6,1},{7,0},{8,15},{9,14},{10,... | collective-permute-start | bytes 110600 | tf_op jit(solution)/shard_map/ppermute | solution.py:237
  32.0 1.0 %collective-permute-start.13 = (f32[72,128]{1,0:T(8,128)S(1)}, f32[72,128]{1,0:T(8,128)S(1)}, u32[]{:S(2)}, u32[]{:S(2)}) collective-permute-start(f32[72,128]{1,0:T(8,128)S(1)} %get-tuple-element.38.rest_0_), channel_id=1, source_target_pairs={{0,6},{1,7},{2,4},{3,5},{4,2},{5,3},{6,0},{7,1},{8,14},{9,15},{10,... | collective-permute-start | bytes 110600 | tf_op jit(solution)/shard_map/ppermute | solution.py:237
  33.0 2.1 %collective-permute-start.12 = (f32[72,128]{1,0:T(8,128)S(1)}, f32[72,128]{1,0:T(8,128)S(1)}, u32[]{:S(2)}, u32[]{:S(2)}) collective-permute-start(f32[72,128]{1,0:T(8,128)S(1)} %get-tuple-element.38.rest_0_), channel_id=1, source_target_pairs={{0,1},{1,0},{2,3},{3,2},{4,5},{5,4},{6,7},{7,6},{8,9},{9,8},{10,11... | collective-permute-start | bytes 110600 | tf_op jit(solution)/shard_map/ppermute | solution.py:237
  35.1 1.6 %collective-permute-done.14.rest_3_ = f32[72,128]{1,0:T(8,128)S(1)} collective-permute-done((f32[72,128]{1,0:T(8,128)S(1)}, f32[72,128]{1,0:T(8,128)S(1)}, u32[]{:S(2)}, u32[]{:S(2)}) %collective-permute-start.14) | collective-permute-done | bytes 36896 | tf_op jit(solution)/shard_map/ppermute | solution.py:237
  36.6 1.3 %collective-permute-done.13.rest_2_ = f32[72,128]{1,0:T(8,128)S(1)} collective-permute-done((f32[72,128]{1,0:T(8,128)S(1)}, f32[72,128]{1,0:T(8,128)S(1)}, u32[]{:S(2)}, u32[]{:S(2)}) %collective-permute-start.13) | collective-permute-done | bytes 36896 | tf_op jit(solution)/shard_map/ppermute | solution.py:237
  39.0 1.0 %collective-permute-done.15.rest_1_ = f32[1,128,256]{2,1,0:T(8,128)S(1)} collective-permute-done((f32[1,128,256]{2,1,0:T(8,128)S(1)}, f32[1,128,256]{2,1,0:T(8,128)S(1)}, u32[]{:S(2)}, u32[]{:S(2)}) %collective-permute-start.15) | collective-permute-done | bytes 131104 | tf_op jit(solution)/shard_map/ppermute | solution.py:244
  40.0 2.0 %collective-permute-start.18 = (f32[8,128]{1,0:T(8,128)S(1)}, f32[8,128]{1,0:T(8,128)S(1)}, u32[]{:S(2)}, u32[]{:S(2)}) collective-permute-start(f32[8,128]{1,0:T(8,128)S(1)} %get-tuple-element.43.refs_2_), channel_id=1, source_target_pairs={{0,7},{1,6},{2,5},{3,4},{4,3},{5,2},{6,1},{7,0},{8,15},{9,14},{10,... | collective-permute-start | bytes 12296 | tf_op jit(solution)/shard_map/ppermute | solution.py:237
  42.0 1.9 %collective-permute-start.16 = (f32[8,128]{1,0:T(8,128)S(1)}, f32[8,128]{1,0:T(8,128)S(1)}, u32[]{:S(2)}, u32[]{:S(2)}) collective-permute-start(f32[8,128]{1,0:T(8,128)S(1)} %get-tuple-element.43.refs_2_), channel_id=1, source_target_pairs={{0,1},{1,0},{2,3},{3,2},{4,5},{5,4},{6,7},{7,6},{8,9},{9,8},{10,11... | collective-permute-start | bytes 12296 | tf_op jit(solution)/shard_map/ppermute | solution.py:237
  43.9 0.6 %shard_map.86 = f32[128,128]{1,0:T(8,128)} custom-call(f32[128,256]{1,0:T(8,128)S(1)} %get-tuple-element.40.xnew), custom_call_target="tpu_custom_call" | custom-call | tf_op jit(solution)/shard_map/pallas_call | solution.py:317
  44.9 1.0 %collective-permute-done.17.refs_4_ = f32[8,128]{1,0:T(8,128)S(1)} collective-permute-done((f32[8,128]{1,0:T(8,128)S(1)}, f32[8,128]{1,0:T(8,128)S(1)}, u32[]{:S(2)}, u32[]{:S(2)}) %collective-permute-start.17) | collective-permute-done | bytes 4128 | tf_op jit(solution)/shard_map/ppermute | solution.py:237
  45.9 0.6 %shard_map.87 = f32[1,3]{1,0:T(1,128)} custom-call(f32[8,128]{1,0:T(8,128)S(1)} %get-tuple-element.41.refs_0_, f32[8,128]{1,0:T(8,128)S(1)} %get-tuple-element.42.refs_1_, f32[8,128]{1,0:T(8,128)S(1)} %get-tuple-element.43.refs_2_, f32[8,128]{1,0:T(8,128)S(1)} %collective-permute-done.16.refs_3_, f32[8,128]{1,0:T(8,128)S(1)} %collective-permute-done.17.refs_4_, ...), custom_call_target="tpu_custom_call" | custom-call | tf_op jit(solution)/shard_map/pallas_call | solution.py:318
  (17 shorter events, 2.5 us)
Async XLA Ops:
  3.9 1.5 %collective-permute-start = (f32[1,168,256]{2,1,0:T(8,128)S(1)}, f32[1,168,256]{2,1,0:T(8,128)S(1)}, u32[]{:S(2)}, u32[]{:S(2)}) collective-permute-start(f32[1,168,256]{2,1,0:T(8,128)S(1)} %get-tuple-element.26.rest_0_), channel_id=1, source_target_pairs={{0,4},{4,0},{1,5},{5,1},{2,6},{6,2},{3,7},{7,3},{8,12},{12,8},{9,1... | collective-permute-start | bytes 516104 | tf_op jit(solution)/shard_map/ppermute | solution.py:244
  6.3 9.3 %collective-permute-start.1 = (bf16[128,256]{1,0:T(8,128)(2,1)S(1)}, bf16[128,256]{1,0:T(8,128)(2,1)S(1)}, u32[]{:S(2)}, u32[]{:S(2)}) collective-permute-start(bf16[128,256]{1,0:T(8,128)(2,1)S(1)} %get-tuple-element.30), channel_id=1, source_target_pairs={{0,4},{4,12},{8,0},{12,20},{16,8},{20,28},{24,16},{28,24},{1,5},{5... | collective-permute-start | bytes 196616 | tf_op jit(solution)/shard_map/ppermute | solution.py:256
  8.9 5.2 %collective-permute-start.4 = (f32[72,128]{1,0:T(8,128)S(1)}, f32[72,128]{1,0:T(8,128)S(1)}, u32[]{:S(2)}, u32[]{:S(2)}) collective-permute-start(f32[72,128]{1,0:T(8,128)S(1)} %get-tuple-element.31.rest_0_), channel_id=1, source_target_pairs={{0,7},{1,6},{2,5},{3,4},{4,3},{5,2},{6,1},{7,0},{8,15},{9,14},{10,... | collective-permute-start | bytes 110600 | tf_op jit(solution)/shard_map/ppermute | solution.py:237
  11.4 4.3 %collective-permute-start.3 = (f32[72,128]{1,0:T(8,128)S(1)}, f32[72,128]{1,0:T(8,128)S(1)}, u32[]{:S(2)}, u32[]{:S(2)}) collective-permute-start(f32[72,128]{1,0:T(8,128)S(1)} %get-tuple-element.31.rest_0_), channel_id=1, source_target_pairs={{0,6},{1,7},{2,4},{3,5},{4,2},{5,3},{6,0},{7,1},{8,14},{9,15},{10,... | collective-permute-start | bytes 110600 | tf_op jit(solution)/shard_map/ppermute | solution.py:237
  11.6 4.0 %collective-permute-start.2 = (f32[72,128]{1,0:T(8,128)S(1)}, f32[72,128]{1,0:T(8,128)S(1)}, u32[]{:S(2)}, u32[]{:S(2)}) collective-permute-start(f32[72,128]{1,0:T(8,128)S(1)} %get-tuple-element.31.rest_0_), channel_id=1, source_target_pairs={{0,1},{1,0},{2,3},{3,2},{4,5},{5,4},{6,7},{7,6},{8,9},{9,8},{10,11... | collective-permute-start | bytes 110600 | tf_op jit(solution)/shard_map/ppermute | solution.py:237
  15.9 2.5 %collective-permute-start.5 = (f32[1,128,256]{2,1,0:T(8,128)S(1)}, f32[1,128,256]{2,1,0:T(8,128)S(1)}, u32[]{:S(2)}, u32[]{:S(2)}) collective-permute-start(f32[1,128,256]{2,1,0:T(8,128)S(1)} %shard_map.80.rest_0_), channel_id=1, source_target_pairs={{0,4},{4,0},{1,5},{5,1},{2,6},{6,2},{3,7},{7,3},{8,12},{12,8},{9,1... | collective-permute-start | bytes 393224 | tf_op jit(solution)/shard_map/ppermute | solution.py:244
  19.1 8.3 %collective-permute-start.6 = (bf16[128,256]{1,0:T(8,128)(2,1)S(1)}, bf16[128,256]{1,0:T(8,128)(2,1)S(1)}, u32[]{:S(2)}, u32[]{:S(2)}) collective-permute-start(bf16[128,256]{1,0:T(8,128)(2,1)S(1)} %get-tuple-element.33), channel_id=1, source_target_pairs={{0,4},{4,12},{8,0},{12,20},{16,8},{20,28},{24,16},{28,24},{1,5},{5... | collective-permute-start | bytes 196616 | tf_op jit(solution)/shard_map/ppermute | solution.py:256
  20.6 5.5 %collective-permute-start.9 = (f32[72,128]{1,0:T(8,128)S(1)}, f32[72,128]{1,0:T(8,128)S(1)}, u32[]{:S(2)}, u32[]{:S(2)}) collective-permute-start(f32[72,128]{1,0:T(8,128)S(1)} %get-tuple-element.34.rest_0_), channel_id=1, source_target_pairs={{0,7},{1,6},{2,5},{3,4},{4,3},{5,2},{6,1},{7,0},{8,15},{9,14},{10,... | collective-permute-start | bytes 110600 | tf_op jit(solution)/shard_map/ppermute | solution.py:237
  21.5 6.0 %collective-permute-start.8 = (f32[72,128]{1,0:T(8,128)S(1)}, f32[72,128]{1,0:T(8,128)S(1)}, u32[]{:S(2)}, u32[]{:S(2)}) collective-permute-start(f32[72,128]{1,0:T(8,128)S(1)} %get-tuple-element.34.rest_0_), channel_id=1, source_target_pairs={{0,6},{1,7},{2,4},{3,5},{4,2},{5,3},{6,0},{7,1},{8,14},{9,15},{10,... | collective-permute-start | bytes 110600 | tf_op jit(solution)/shard_map/ppermute | solution.py:237
  22.1 5.3 %collective-permute-start.7 = (f32[72,128]{1,0:T(8,128)S(1)}, f32[72,128]{1,0:T(8,128)S(1)}, u32[]{:S(2)}, u32[]{:S(2)}) collective-permute-start(f32[72,128]{1,0:T(8,128)S(1)} %get-tuple-element.34.rest_0_), channel_id=1, source_target_pairs={{0,1},{1,0},{2,3},{3,2},{4,5},{5,4},{6,7},{7,6},{8,9},{9,8},{10,11... | collective-permute-start | bytes 110600 | tf_op jit(solution)/shard_map/ppermute | solution.py:237
  27.7 1.6 %collective-permute-start.10 = (f32[1,128,256]{2,1,0:T(8,128)S(1)}, f32[1,128,256]{2,1,0:T(8,128)S(1)}, u32[]{:S(2)}, u32[]{:S(2)}) collective-permute-start(f32[1,128,256]{2,1,0:T(8,128)S(1)} %get-tuple-element.35.rest_0_), channel_id=1, source_target_pairs={{0,4},{4,0},{1,5},{5,1},{2,6},{6,2},{3,7},{7,3},{8,12},{12,8},{9,1... | collective-permute-start | bytes 393224 | tf_op jit(solution)/shard_map/ppermute | solution.py:244
  30.0 8.1 %collective-permute-start.11 = (bf16[128,256]{1,0:T(8,128)(2,1)S(1)}, bf16[128,256]{1,0:T(8,128)(2,1)S(1)}, u32[]{:S(2)}, u32[]{:S(2)}) collective-permute-start(bf16[128,256]{1,0:T(8,128)(2,1)S(1)} %get-tuple-element.37), channel_id=1, source_target_pairs={{0,4},{4,12},{8,0},{12,20},{16,8},{20,28},{24,16},{28,24},{1,5},{5... | collective-permute-start | bytes 196616 | tf_op jit(solution)/shard_map/ppermute | solution.py:256
  31.2 5.4 %collective-permute-start.14 = (f32[72,128]{1,0:T(8,128)S(1)}, f32[72,128]{1,0:T(8,128)S(1)}, u32[]{:S(2)}, u32[]{:S(2)}) collective-permute-start(f32[72,128]{1,0:T(8,128)S(1)} %get-tuple-element.38.rest_0_), channel_id=1, source_target_pairs={{0,7},{1,6},{2,5},{3,4},{4,3},{5,2},{6,1},{7,0},{8,15},{9,14},{10,... | collective-permute-start | bytes 110600 | tf_op jit(solution)/shard_map/ppermute | solution.py:237
  32.0 6.0 %collective-permute-start.13 = (f32[72,128]{1,0:T(8,128)S(1)}, f32[72,128]{1,0:T(8,128)S(1)}, u32[]{:S(2)}, u32[]{:S(2)}) collective-permute-start(f32[72,128]{1,0:T(8,128)S(1)} %get-tuple-element.38.rest_0_), channel_id=1, source_target_pairs={{0,6},{1,7},{2,4},{3,5},{4,2},{5,3},{6,0},{7,1},{8,14},{9,15},{10,... | collective-permute-start | bytes 110600 | tf_op jit(solution)/shard_map/ppermute | solution.py:237
  33.0 5.2 %collective-permute-start.12 = (f32[72,128]{1,0:T(8,128)S(1)}, f32[72,128]{1,0:T(8,128)S(1)}, u32[]{:S(2)}, u32[]{:S(2)}) collective-permute-start(f32[72,128]{1,0:T(8,128)S(1)} %get-tuple-element.38.rest_0_), channel_id=1, source_target_pairs={{0,1},{1,0},{2,3},{3,2},{4,5},{5,4},{6,7},{7,6},{8,9},{9,8},{10,11... | collective-permute-start | bytes 110600 | tf_op jit(solution)/shard_map/ppermute | solution.py:237
  38.4 1.6 %collective-permute-start.15 = (f32[1,128,256]{2,1,0:T(8,128)S(1)}, f32[1,128,256]{2,1,0:T(8,128)S(1)}, u32[]{:S(2)}, u32[]{:S(2)}) collective-permute-start(f32[1,128,256]{2,1,0:T(8,128)S(1)} %get-tuple-element.39.rest_0_), channel_id=1, source_target_pairs={{0,4},{4,0},{1,5},{5,1},{2,6},{6,2},{3,7},{7,3},{8,12},{12,8},{9,1... | collective-permute-start | bytes 393224 | tf_op jit(solution)/shard_map/ppermute | solution.py:244
  40.0 4.9 %collective-permute-start.18 = (f32[8,128]{1,0:T(8,128)S(1)}, f32[8,128]{1,0:T(8,128)S(1)}, u32[]{:S(2)}, u32[]{:S(2)}) collective-permute-start(f32[8,128]{1,0:T(8,128)S(1)} %get-tuple-element.43.refs_2_), channel_id=1, source_target_pairs={{0,7},{1,6},{2,5},{3,4},{4,3},{5,2},{6,1},{7,0},{8,15},{9,14},{10,... | collective-permute-start | bytes 12296 | tf_op jit(solution)/shard_map/ppermute | solution.py:237
  42.0 3.9 %collective-permute-start.17 = (f32[8,128]{1,0:T(8,128)S(1)}, f32[8,128]{1,0:T(8,128)S(1)}, u32[]{:S(2)}, u32[]{:S(2)}) collective-permute-start(f32[8,128]{1,0:T(8,128)S(1)} %get-tuple-element.43.refs_2_), channel_id=1, source_target_pairs={{0,6},{1,7},{2,4},{3,5},{4,2},{5,3},{6,0},{7,1},{8,14},{9,15},{10,... | collective-permute-start | bytes 12296 | tf_op jit(solution)/shard_map/ppermute | solution.py:237
  42.0 3.9 %collective-permute-start.16 = (f32[8,128]{1,0:T(8,128)S(1)}, f32[8,128]{1,0:T(8,128)S(1)}, u32[]{:S(2)}, u32[]{:S(2)}) collective-permute-start(f32[8,128]{1,0:T(8,128)S(1)} %get-tuple-element.43.refs_2_), channel_id=1, source_target_pairs={{0,1},{1,0},{2,3},{3,2},{4,5},{5,4},{6,7},{7,6},{8,9},{9,8},{10,11... | collective-permute-start | bytes 12296 | tf_op jit(solution)/shard_map/ppermute | solution.py:237

commit v5 on v4

--- a/solution.py
+++ b/solution.py
@@ -196,8 +196,8 @@
     end = jnp.where(odd == 0, layers - 1, 0)
     arrive = jnp.where(lax.axis_index("layer") == end, 0.0, damping * spill[...].astype(F32))
     walk = damping * (1.0 - coupling)
-    own = walk * (sum(walks[:2]) + mass / node_total) + (1.0 - damping)
-    peer = walk * sum(walks[2:])
+    own = walk * (walks[0] + sum(walks[1::2]) + mass / node_total) + (1.0 - damping)
+    peer = walk * sum(walks[2::2])
     part[0, 0:blocks, :] = arrive[0:blocks] + jnp.where(odd == 0, own, peer)
     part[0, blocks:, :] = arrive[blocks:] + jnp.where(odd == 0, peer, own)
 
@@ -233,7 +233,7 @@
         for row in range(rows):
             for col in range(cols):
                 other = (col + step) % cols if cols & (cols - 1) else col ^ step
-                pairs.append((row * cols + col, (row ^ (step > 1)) * cols + other))
+                pairs.append((row * cols + col, (row ^ (step % 2 == 0)) * cols + other))
         got.append(lax.ppermute(x, ("row", "col"), pairs))
     return got
 

time: 46.9 us -> 46.4 us (0.989)
  starting transfers between devices: 23.4 us -> 19.5 us
  waiting for transfers between devices: 13.7 us -> 16.9 us
    ppermute x12, waiting for transfers between devices: 10.4 us -> 13.2 us  [to_others(): got.append(lax.ppermute(x, ('row', 'col'), pairs))]
    ppermute x12, starting transfers between devices: 15.4 us -> 12.9 us  [to_others(): got.append(lax.ppermute(x, ('row', 'col'), pairs))]
    ppermute x4, starting transfers between devices: 2.82 us -> 1.05 us  [to_rows(): return (x, lax.ppermute(x, 'row', [(0, 1), (1, 0)]))]
  transfers between devices with their start and end apart: 19 -> 19, of which waited for: 13 -> 11; matrix products, arithmetic and copies ran while one was open for 0% -> 0% of each run, Pallas kernels for 4% -> 4%
where the time goes in v5:
time: 46.4 us; the launch traced here: 45.9 us
  starting transfers between devices  19.5 us (42%)
  waiting for transfers between devices  16.9 us (36%)
  Pallas kernels  8.04 us (17%)
  between operations  1.41 us (3%)
    ppermute x12, waiting for transfers between devices, to_others(): got.append(lax.ppermute(x, ('row', 'col'), pairs))  13.2 us
    ppermute x12, starting transfers between devices, to_others(): got.append(lax.ppermute(x, ('row', 'col'), pairs))  12.9 us
    ppermute x3, starting transfers between devices, to_layers(): return lax.ppermute(spill, ('layer', 'row'), pairs)  5.6 us
    ppermute x4, waiting for transfers between devices, to_rows(): return (x, lax.ppermute(x, 'row', [(0, 1), (1, 0)]))  3.67 us
    pallas_call x1, Pallas kernels, local(): call(opening, (lead(slots + META + 2 * blocks), pltpu.VMEM((slots, edge,...  2.61 us
    pallas_call x2, Pallas kernels, local(): call(functools.partial(middle, layers), sent, (VMEM,) * (6 + len(shared)))  1.41 us
    pallas_call x1, Pallas kernels, local(): turned = call(turn, pltpu.VMEM((slots, edge, edge), BF16), (VMEM,))(values)  1.13 us
    ppermute x4, starting transfers between devices, to_rows(): return (x, lax.ppermute(x, 'row', [(0, 1), (1, 0)]))  1.05 us
  transfers between devices with their start and end apart: 19, of which 11 were waited for; matrix products, arithmetic and copies ran while one was open for 0% of the time, Pallas kernels for 4%

profile of v5, /device:TPU:1, one launch (start us, length us, event | category | flops | bytes accessed | tf_op | source)
XLA Modules:
  0.0 45.9 jit_solution(2824432669301385640)
XLA Ops:
  1.3 2.6 %shard_map.77 = (f32[1,168,256]{2,1,0:T(8,128)S(1)}, bf16[32,256,256]{2,1,0:T(8,128)(2,1)S(1)}, bf16[32,128]{1,0:T(8,128)(2,1)S(1)}, f32[8,128]{1,0:T(8,128)S(1)}) custom-call(bf16[32,256,256]{2,1,0:T(8,128)(2,1)} %bitcast.9, s32[1,32]{1,0:T(1,128)} %bitcast.13, s32[1,32]{1,0:T(1,128)} %bitcast.14, s32[1,1]{1,0:T(1,128)} %bitcast.8.count_h, ...), custom_call_target="tpu_custom_call" | custom-call | tf_op jit(solution)/shard_map/pallas_call | solution.py:283
  4.0 1.1 %shard_map.78.turned = bf16[32,256,256]{2,1,0:T(8,128)(2,1)S(1)} custom-call(bf16[32,256,256]{2,1,0:T(8,128)(2,1)S(1)} %get-tuple-element.23.values), custom_call_target="tpu_custom_call" | custom-call | tf_op jit(solution)/shard_map/pallas_call | solution.py:293
  5.1 0.3 collective-permute-done.rest_1_
  5.4 0.9 %shard_map.79 = (f32[72,128]{1,0:T(8,128)S(1)}, bf16[128,256]{1,0:T(8,128)(2,1)S(1)}, f32[128,256]{1,0:T(8,128)S(1)}, f32[128,256]{1,0:T(8,128)S(1)}, f32[128,256]{1,0:T(8,128)S(1)}) custom-call(bf16[32,256,256]{2,1,0:T(8,128)(2,1)S(1)} %shard_map.78.turned, bf16[32,128]{1,0:T(8,128)(2,1)S(1)} %get-tuple-element.24.pick, ...), custom_call_target="tpu_custom_call" | custom-call | tf_op jit(solution)/shard_map/pallas_call | solution.py:297
  6.3 2.5 %collective-permute-start.1 = (bf16[128,256]{1,0:T(8,128)(2,1)S(1)}, bf16[128,256]{1,0:T(8,128)(2,1)S(1)}, u32[]{:S(2)}, u32[]{:S(2)}) collective-permute-start(bf16[128,256]{1,0:T(8,128)(2,1)S(1)} %get-tuple-element.30), channel_id=1, source_target_pairs={{0,4},{4,12},{8,0},{12,20},{16,8},{20,28},{24,16},{28,24},{1,5},{5... | collective-permute-start | bytes 196616 | tf_op jit(solution)/shard_map/ppermute | solution.py:256
  8.9 3.3 %collective-permute-start.4 = (f32[72,128]{1,0:T(8,128)S(1)}, f32[72,128]{1,0:T(8,128)S(1)}, u32[]{:S(2)}, u32[]{:S(2)}) collective-permute-start(f32[72,128]{1,0:T(8,128)S(1)} %get-tuple-element.31.rest_0_), channel_id=1, source_target_pairs={{0,3},{1,2},{2,1},{3,0},{4,7},{5,6},{6,5},{7,4},{8,11},{9,10},{10,... | collective-permute-start | bytes 110600 | tf_op jit(solution)/shard_map/ppermute | solution.py:237
  12.2 1.3 %collective-permute-done.4.rest_3_ = f32[72,128]{1,0:T(8,128)S(1)} collective-permute-done((f32[72,128]{1,0:T(8,128)S(1)}, f32[72,128]{1,0:T(8,128)S(1)}, u32[]{:S(2)}, u32[]{:S(2)}) %collective-permute-start.4) | collective-permute-done | bytes 36896 | tf_op jit(solution)/shard_map/ppermute | solution.py:237
  13.5 2.9 %collective-permute-done.3.rest_2_ = f32[72,128]{1,0:T(8,128)S(1)} collective-permute-done((f32[72,128]{1,0:T(8,128)S(1)}, f32[72,128]{1,0:T(8,128)S(1)}, u32[]{:S(2)}, u32[]{:S(2)}) %collective-permute-start.3) | collective-permute-done | bytes 36896 | tf_op jit(solution)/shard_map/ppermute | solution.py:237
  16.8 1.3 %collective-permute-done.5.rest_1_ = f32[1,128,256]{2,1,0:T(8,128)S(1)} collective-permute-done((f32[1,128,256]{2,1,0:T(8,128)S(1)}, f32[1,128,256]{2,1,0:T(8,128)S(1)}, u32[]{:S(2)}, u32[]{:S(2)}) %collective-permute-start.5) | collective-permute-done | bytes 131104 | tf_op jit(solution)/shard_map/ppermute | solution.py:244
  18.1 0.7 %shard_map.81 = (f32[72,128]{1,0:T(8,128)S(1)}, bf16[128,256]{1,0:T(8,128)(2,1)S(1)}, f32[128,256]{1,0:T(8,128)S(1)}) custom-call(bf16[32,256,256]{2,1,0:T(8,128)(2,1)S(1)} %shard_map.78.turned, bf16[32,128]{1,0:T(8,128)(2,1)S(1)} %get-tuple-element.24.pick, f32[8,128]{1,0:T(8,128)S(1)} %get-tuple-element.25.marks, f32[128,256]{1,0:T(8,128)S(1)} %get-tuple-element.27.inv_i, ...), custom_call_target="tpu_custom_call" | custom-call | tf_op jit(solution)/shard_map/pallas_call | solution.py:304
  18.8 1.3 %collective-permute-start.6 = (bf16[128,256]{1,0:T(8,128)(2,1)S(1)}, bf16[128,256]{1,0:T(8,128)(2,1)S(1)}, u32[]{:S(2)}, u32[]{:S(2)}) collective-permute-start(bf16[128,256]{1,0:T(8,128)(2,1)S(1)} %get-tuple-element.33), channel_id=1, source_target_pairs={{0,4},{4,12},{8,0},{12,20},{16,8},{20,28},{24,16},{28,24},{1,5},{5... | collective-permute-start | bytes 196616 | tf_op jit(solution)/shard_map/ppermute | solution.py:256
  20.1 1.9 %collective-permute-start.9 = (f32[72,128]{1,0:T(8,128)S(1)}, f32[72,128]{1,0:T(8,128)S(1)}, u32[]{:S(2)}, u32[]{:S(2)}) collective-permute-start(f32[72,128]{1,0:T(8,128)S(1)} %get-tuple-element.34.rest_0_), channel_id=1, source_target_pairs={{0,3},{1,2},{2,1},{3,0},{4,7},{5,6},{6,5},{7,4},{8,11},{9,10},{10,... | collective-permute-start | bytes 110600 | tf_op jit(solution)/shard_map/ppermute | solution.py:237
  22.0 1.1 %collective-permute-start.7 = (f32[72,128]{1,0:T(8,128)S(1)}, f32[72,128]{1,0:T(8,128)S(1)}, u32[]{:S(2)}, u32[]{:S(2)}) collective-permute-start(f32[72,128]{1,0:T(8,128)S(1)} %get-tuple-element.34.rest_0_), channel_id=1, source_target_pairs={{0,1},{1,0},{2,3},{3,2},{4,5},{5,4},{6,7},{7,6},{8,9},{9,8},{10,11... | collective-permute-start | bytes 110600 | tf_op jit(solution)/shard_map/ppermute | solution.py:237
  23.1 1.8 %collective-permute-done.9.rest_3_ = f32[72,128]{1,0:T(8,128)S(1)} collective-permute-done((f32[72,128]{1,0:T(8,128)S(1)}, f32[72,128]{1,0:T(8,128)S(1)}, u32[]{:S(2)}, u32[]{:S(2)}) %collective-permute-start.9) | collective-permute-done | bytes 36896 | tf_op jit(solution)/shard_map/ppermute | solution.py:237
  24.9 1.6 %collective-permute-done.8.rest_2_ = f32[72,128]{1,0:T(8,128)S(1)} collective-permute-done((f32[72,128]{1,0:T(8,128)S(1)}, f32[72,128]{1,0:T(8,128)S(1)}, u32[]{:S(2)}, u32[]{:S(2)}) %collective-permute-start.8) | collective-permute-done | bytes 36896 | tf_op jit(solution)/shard_map/ppermute | solution.py:237
  26.8 0.6 %collective-permute-start.10 = (f32[1,128,256]{2,1,0:T(8,128)S(1)}, f32[1,128,256]{2,1,0:T(8,128)S(1)}, u32[]{:S(2)}, u32[]{:S(2)}) collective-permute-start(f32[1,128,256]{2,1,0:T(8,128)S(1)} %get-tuple-element.35.rest_0_), channel_id=1, source_target_pairs={{0,4},{4,0},{1,5},{5,1},{2,6},{6,2},{3,7},{7,3},{8,12},{12,8},{9,1... | collective-permute-start | bytes 393224 | tf_op jit(solution)/shard_map/ppermute | solution.py:244
  27.4 1.0 %collective-permute-done.10.rest_1_ = f32[1,128,256]{2,1,0:T(8,128)S(1)} collective-permute-done((f32[1,128,256]{2,1,0:T(8,128)S(1)}, f32[1,128,256]{2,1,0:T(8,128)S(1)}, u32[]{:S(2)}, u32[]{:S(2)}) %collective-permute-start.10) | collective-permute-done | bytes 131104 | tf_op jit(solution)/shard_map/ppermute | solution.py:244
  28.4 0.7 %shard_map.83 = (f32[72,128]{1,0:T(8,128)S(1)}, bf16[128,256]{1,0:T(8,128)(2,1)S(1)}, f32[128,256]{1,0:T(8,128)S(1)}) custom-call(bf16[32,256,256]{2,1,0:T(8,128)(2,1)S(1)} %shard_map.78.turned, bf16[32,128]{1,0:T(8,128)(2,1)S(1)} %get-tuple-element.24.pick, f32[8,128]{1,0:T(8,128)S(1)} %get-tuple-element.25.marks, f32[128,256]{1,0:T(8,128)S(1)} %get-tuple-element.27.inv_i, ...), custom_call_target="tpu_custom_call" | custom-call | tf_op jit(solution)/shard_map/pallas_call | solution.py:304
  29.1 1.8 %collective-permute-start.11 = (bf16[128,256]{1,0:T(8,128)(2,1)S(1)}, bf16[128,256]{1,0:T(8,128)(2,1)S(1)}, u32[]{:S(2)}, u32[]{:S(2)}) collective-permute-start(bf16[128,256]{1,0:T(8,128)(2,1)S(1)} %get-tuple-element.37), channel_id=1, source_target_pairs={{0,4},{4,12},{8,0},{12,20},{16,8},{20,28},{24,16},{28,24},{1,5},{5... | collective-permute-start | bytes 196616 | tf_op jit(solution)/shard_map/ppermute | solution.py:256
  30.9 2.2 %collective-permute-start.14 = (f32[72,128]{1,0:T(8,128)S(1)}, f32[72,128]{1,0:T(8,128)S(1)}, u32[]{:S(2)}, u32[]{:S(2)}) collective-permute-start(f32[72,128]{1,0:T(8,128)S(1)} %get-tuple-element.38.rest_0_), channel_id=1, source_target_pairs={{0,3},{1,2},{2,1},{3,0},{4,7},{5,6},{6,5},{7,4},{8,11},{9,10},{10,... | collective-permute-start | bytes 110600 | tf_op jit(solution)/shard_map/ppermute | solution.py:237
  33.1 0.3 collective-permute-start.12
  33.4 2.1 %collective-permute-done.14.rest_3_ = f32[72,128]{1,0:T(8,128)S(1)} collective-permute-done((f32[72,128]{1,0:T(8,128)S(1)}, f32[72,128]{1,0:T(8,128)S(1)}, u32[]{:S(2)}, u32[]{:S(2)}) %collective-permute-start.14) | collective-permute-done | bytes 36896 | tf_op jit(solution)/shard_map/ppermute | solution.py:237
  35.5 2.0 %collective-permute-done.13.rest_2_ = f32[72,128]{1,0:T(8,128)S(1)} collective-permute-done((f32[72,128]{1,0:T(8,128)S(1)}, f32[72,128]{1,0:T(8,128)S(1)}, u32[]{:S(2)}, u32[]{:S(2)}) %collective-permute-start.13) | collective-permute-done | bytes 36896 | tf_op jit(solution)/shard_map/ppermute | solution.py:237
  37.5 0.2 shard_map.84
  37.8 0.3 collective-permute-start.15
  38.1 1.1 %collective-permute-done.15.rest_1_ = f32[1,128,256]{2,1,0:T(8,128)S(1)} collective-permute-done((f32[1,128,256]{2,1,0:T(8,128)S(1)}, f32[1,128,256]{2,1,0:T(8,128)S(1)}, u32[]{:S(2)}, u32[]{:S(2)}) %collective-permute-start.15) | collective-permute-done | bytes 131104 | tf_op jit(solution)/shard_map/ppermute | solution.py:244
  39.2 1.9 %collective-permute-start.18 = (f32[8,128]{1,0:T(8,128)S(1)}, f32[8,128]{1,0:T(8,128)S(1)}, u32[]{:S(2)}, u32[]{:S(2)}) collective-permute-start(f32[8,128]{1,0:T(8,128)S(1)} %get-tuple-element.43.refs_2_), channel_id=1, source_target_pairs={{0,3},{1,2},{2,1},{3,0},{4,7},{5,6},{6,5},{7,4},{8,11},{9,10},{10,... | collective-permute-start | bytes 12296 | tf_op jit(solution)/shard_map/ppermute | solution.py:237
  41.1 0.8 %collective-permute-start.17 = (f32[8,128]{1,0:T(8,128)S(1)}, f32[8,128]{1,0:T(8,128)S(1)}, u32[]{:S(2)}, u32[]{:S(2)}) collective-permute-start(f32[8,128]{1,0:T(8,128)S(1)} %get-tuple-element.43.refs_2_), channel_id=1, source_target_pairs={{0,6},{1,7},{2,4},{3,5},{4,2},{5,3},{6,0},{7,1},{8,14},{9,15},{10,... | collective-permute-start | bytes 12296 | tf_op jit(solution)/shard_map/ppermute | solution.py:237
  41.9 1.4 %collective-permute-start.16 = (f32[8,128]{1,0:T(8,128)S(1)}, f32[8,128]{1,0:T(8,128)S(1)}, u32[]{:S(2)}, u32[]{:S(2)}) collective-permute-start(f32[8,128]{1,0:T(8,128)S(1)} %get-tuple-element.43.refs_2_), channel_id=1, source_target_pairs={{0,1},{1,0},{2,3},{3,2},{4,5},{5,4},{6,7},{7,6},{8,9},{9,8},{10,11... | collective-permute-start | bytes 12296 | tf_op jit(solution)/shard_map/ppermute | solution.py:237
  43.3 0.6 %shard_map.86 = f32[128,128]{1,0:T(8,128)} custom-call(f32[128,256]{1,0:T(8,128)S(1)} %get-tuple-element.40.xnew), custom_call_target="tpu_custom_call" | custom-call | tf_op jit(solution)/shard_map/pallas_call | solution.py:317
  43.9 1.4 %collective-permute-done.17.refs_4_ = f32[8,128]{1,0:T(8,128)S(1)} collective-permute-done((f32[8,128]{1,0:T(8,128)S(1)}, f32[8,128]{1,0:T(8,128)S(1)}, u32[]{:S(2)}, u32[]{:S(2)}) %collective-permute-start.17) | collective-permute-done | bytes 4128 | tf_op jit(solution)/shard_map/ppermute | solution.py:237
  45.3 0.6 %shard_map.87 = f32[1,3]{1,0:T(1,128)} custom-call(f32[8,128]{1,0:T(8,128)S(1)} %get-tuple-element.41.refs_0_, f32[8,128]{1,0:T(8,128)S(1)} %get-tuple-element.42.refs_1_, f32[8,128]{1,0:T(8,128)S(1)} %get-tuple-element.43.refs_2_, f32[8,128]{1,0:T(8,128)S(1)} %collective-permute-done.16.refs_3_, f32[8,128]{1,0:T(8,128)S(1)} %collective-permute-done.17.refs_4_, ...), custom_call_target="tpu_custom_call" | custom-call | tf_op jit(solution)/shard_map/pallas_call | solution.py:318
  (17 shorter events, 0.7 us)
Async XLA Ops:
  3.9 1.5 %collective-permute-start = (f32[1,168,256]{2,1,0:T(8,128)S(1)}, f32[1,168,256]{2,1,0:T(8,128)S(1)}, u32[]{:S(2)}, u32[]{:S(2)}) collective-permute-start(f32[1,168,256]{2,1,0:T(8,128)S(1)} %get-tuple-element.26.rest_0_), channel_id=1, source_target_pairs={{0,4},{4,0},{1,5},{5,1},{2,6},{6,2},{3,7},{7,3},{8,12},{12,8},{9,1... | collective-permute-start | bytes 516104 | tf_op jit(solution)/shard_map/ppermute | solution.py:244
  6.3 10.1 %collective-permute-start.1 = (bf16[128,256]{1,0:T(8,128)(2,1)S(1)}, bf16[128,256]{1,0:T(8,128)(2,1)S(1)}, u32[]{:S(2)}, u32[]{:S(2)}) collective-permute-start(bf16[128,256]{1,0:T(8,128)(2,1)S(1)} %get-tuple-element.30), channel_id=1, source_target_pairs={{0,4},{4,12},{8,0},{12,20},{16,8},{20,28},{24,16},{28,24},{1,5},{5... | collective-permute-start | bytes 196616 | tf_op jit(solution)/shard_map/ppermute | solution.py:256
  8.9 4.7 %collective-permute-start.4 = (f32[72,128]{1,0:T(8,128)S(1)}, f32[72,128]{1,0:T(8,128)S(1)}, u32[]{:S(2)}, u32[]{:S(2)}) collective-permute-start(f32[72,128]{1,0:T(8,128)S(1)} %get-tuple-element.31.rest_0_), channel_id=1, source_target_pairs={{0,3},{1,2},{2,1},{3,0},{4,7},{5,6},{6,5},{7,4},{8,11},{9,10},{10,... | collective-permute-start | bytes 110600 | tf_op jit(solution)/shard_map/ppermute | solution.py:237
  12.2 4.3 %collective-permute-start.3 = (f32[72,128]{1,0:T(8,128)S(1)}, f32[72,128]{1,0:T(8,128)S(1)}, u32[]{:S(2)}, u32[]{:S(2)}) collective-permute-start(f32[72,128]{1,0:T(8,128)S(1)} %get-tuple-element.31.rest_0_), channel_id=1, source_target_pairs={{0,6},{1,7},{2,4},{3,5},{4,2},{5,3},{6,0},{7,1},{8,14},{9,15},{10,... | collective-permute-start | bytes 110600 | tf_op jit(solution)/shard_map/ppermute | solution.py:237
  12.2 4.3 %collective-permute-start.2 = (f32[72,128]{1,0:T(8,128)S(1)}, f32[72,128]{1,0:T(8,128)S(1)}, u32[]{:S(2)}, u32[]{:S(2)}) collective-permute-start(f32[72,128]{1,0:T(8,128)S(1)} %get-tuple-element.31.rest_0_), channel_id=1, source_target_pairs={{0,1},{1,0},{2,3},{3,2},{4,5},{5,4},{6,7},{7,6},{8,9},{9,8},{10,11... | collective-permute-start | bytes 110600 | tf_op jit(solution)/shard_map/ppermute | solution.py:237
  16.7 1.4 %collective-permute-start.5 = (f32[1,128,256]{2,1,0:T(8,128)S(1)}, f32[1,128,256]{2,1,0:T(8,128)S(1)}, u32[]{:S(2)}, u32[]{:S(2)}) collective-permute-start(f32[1,128,256]{2,1,0:T(8,128)S(1)} %shard_map.80.rest_0_), channel_id=1, source_target_pairs={{0,4},{4,0},{1,5},{5,1},{2,6},{6,2},{3,7},{7,3},{8,12},{12,8},{9,1... | collective-permute-start | bytes 393224 | tf_op jit(solution)/shard_map/ppermute | solution.py:244
  18.8 7.7 %collective-permute-start.6 = (bf16[128,256]{1,0:T(8,128)(2,1)S(1)}, bf16[128,256]{1,0:T(8,128)(2,1)S(1)}, u32[]{:S(2)}, u32[]{:S(2)}) collective-permute-start(bf16[128,256]{1,0:T(8,128)(2,1)S(1)} %get-tuple-element.33), channel_id=1, source_target_pairs={{0,4},{4,12},{8,0},{12,20},{16,8},{20,28},{24,16},{28,24},{1,5},{5... | collective-permute-start | bytes 196616 | tf_op jit(solution)/shard_map/ppermute | solution.py:256
  20.1 4.8 %collective-permute-start.9 = (f32[72,128]{1,0:T(8,128)S(1)}, f32[72,128]{1,0:T(8,128)S(1)}, u32[]{:S(2)}, u32[]{:S(2)}) collective-permute-start(f32[72,128]{1,0:T(8,128)S(1)} %get-tuple-element.34.rest_0_), channel_id=1, source_target_pairs={{0,3},{1,2},{2,1},{3,0},{4,7},{5,6},{6,5},{7,4},{8,11},{9,10},{10,... | collective-permute-start | bytes 110600 | tf_op jit(solution)/shard_map/ppermute | solution.py:237
  22.0 4.5 %collective-permute-start.8 = (f32[72,128]{1,0:T(8,128)S(1)}, f32[72,128]{1,0:T(8,128)S(1)}, u32[]{:S(2)}, u32[]{:S(2)}) collective-permute-start(f32[72,128]{1,0:T(8,128)S(1)} %get-tuple-element.34.rest_0_), channel_id=1, source_target_pairs={{0,6},{1,7},{2,4},{3,5},{4,2},{5,3},{6,0},{7,1},{8,14},{9,15},{10,... | collective-permute-start | bytes 110600 | tf_op jit(solution)/shard_map/ppermute | solution.py:237
  22.0 4.5 %collective-permute-start.7 = (f32[72,128]{1,0:T(8,128)S(1)}, f32[72,128]{1,0:T(8,128)S(1)}, u32[]{:S(2)}, u32[]{:S(2)}) collective-permute-start(f32[72,128]{1,0:T(8,128)S(1)} %get-tuple-element.34.rest_0_), channel_id=1, source_target_pairs={{0,1},{1,0},{2,3},{3,2},{4,5},{5,4},{6,7},{7,6},{8,9},{9,8},{10,11... | collective-permute-start | bytes 110600 | tf_op jit(solution)/shard_map/ppermute | solution.py:237
  26.8 1.6 %collective-permute-start.10 = (f32[1,128,256]{2,1,0:T(8,128)S(1)}, f32[1,128,256]{2,1,0:T(8,128)S(1)}, u32[]{:S(2)}, u32[]{:S(2)}) collective-permute-start(f32[1,128,256]{2,1,0:T(8,128)S(1)} %get-tuple-element.35.rest_0_), channel_id=1, source_target_pairs={{0,4},{4,0},{1,5},{5,1},{2,6},{6,2},{3,7},{7,3},{8,12},{12,8},{9,1... | collective-permute-start | bytes 393224 | tf_op jit(solution)/shard_map/ppermute | solution.py:244
  29.1 8.4 %collective-permute-start.11 = (bf16[128,256]{1,0:T(8,128)(2,1)S(1)}, bf16[128,256]{1,0:T(8,128)(2,1)S(1)}, u32[]{:S(2)}, u32[]{:S(2)}) collective-permute-start(bf16[128,256]{1,0:T(8,128)(2,1)S(1)} %get-tuple-element.37), channel_id=1, source_target_pairs={{0,4},{4,12},{8,0},{12,20},{16,8},{20,28},{24,16},{28,24},{1,5},{5... | collective-permute-start | bytes 196616 | tf_op jit(solution)/shard_map/ppermute | solution.py:256
  30.9 4.6 %collective-permute-start.14 = (f32[72,128]{1,0:T(8,128)S(1)}, f32[72,128]{1,0:T(8,128)S(1)}, u32[]{:S(2)}, u32[]{:S(2)}) collective-permute-start(f32[72,128]{1,0:T(8,128)S(1)} %get-tuple-element.38.rest_0_), channel_id=1, source_target_pairs={{0,3},{1,2},{2,1},{3,0},{4,7},{5,6},{6,5},{7,4},{8,11},{9,10},{10,... | collective-permute-start | bytes 110600 | tf_op jit(solution)/shard_map/ppermute | solution.py:237
  33.1 4.4 %collective-permute-start.13 = (f32[72,128]{1,0:T(8,128)S(1)}, f32[72,128]{1,0:T(8,128)S(1)}, u32[]{:S(2)}, u32[]{:S(2)}) collective-permute-start(f32[72,128]{1,0:T(8,128)S(1)} %get-tuple-element.38.rest_0_), channel_id=1, source_target_pairs={{0,6},{1,7},{2,4},{3,5},{4,2},{5,3},{6,0},{7,1},{8,14},{9,15},{10,... | collective-permute-start | bytes 110600 | tf_op jit(solution)/shard_map/ppermute | solution.py:237
  33.1 4.4 %collective-permute-start.12 = (f32[72,128]{1,0:T(8,128)S(1)}, f32[72,128]{1,0:T(8,128)S(1)}, u32[]{:S(2)}, u32[]{:S(2)}) collective-permute-start(f32[72,128]{1,0:T(8,128)S(1)} %get-tuple-element.38.rest_0_), channel_id=1, source_target_pairs={{0,1},{1,0},{2,3},{3,2},{4,5},{5,4},{6,7},{7,6},{8,9},{9,8},{10,11... | collective-permute-start | bytes 110600 | tf_op jit(solution)/shard_map/ppermute | solution.py:237
  37.8 1.4 %collective-permute-start.15 = (f32[1,128,256]{2,1,0:T(8,128)S(1)}, f32[1,128,256]{2,1,0:T(8,128)S(1)}, u32[]{:S(2)}, u32[]{:S(2)}) collective-permute-start(f32[1,128,256]{2,1,0:T(8,128)S(1)} %get-tuple-element.39.rest_0_), channel_id=1, source_target_pairs={{0,4},{4,0},{1,5},{5,1},{2,6},{6,2},{3,7},{7,3},{8,12},{12,8},{9,1... | collective-permute-start | bytes 393224 | tf_op jit(solution)/shard_map/ppermute | solution.py:244
  39.2 4.7 %collective-permute-start.18 = (f32[8,128]{1,0:T(8,128)S(1)}, f32[8,128]{1,0:T(8,128)S(1)}, u32[]{:S(2)}, u32[]{:S(2)}) collective-permute-start(f32[8,128]{1,0:T(8,128)S(1)} %get-tuple-element.43.refs_2_), channel_id=1, source_target_pairs={{0,3},{1,2},{2,1},{3,0},{4,7},{5,6},{6,5},{7,4},{8,11},{9,10},{10,... | collective-permute-start | bytes 12296 | tf_op jit(solution)/shard_map/ppermute | solution.py:237
  41.1 4.2 %collective-permute-start.17 = (f32[8,128]{1,0:T(8,128)S(1)}, f32[8,128]{1,0:T(8,128)S(1)}, u32[]{:S(2)}, u32[]{:S(2)}) collective-permute-start(f32[8,128]{1,0:T(8,128)S(1)} %get-tuple-element.43.refs_2_), channel_id=1, source_target_pairs={{0,6},{1,7},{2,4},{3,5},{4,2},{5,3},{6,0},{7,1},{8,14},{9,15},{10,... | collective-permute-start | bytes 12296 | tf_op jit(solution)/shard_map/ppermute | solution.py:237
  41.9 3.4 %collective-permute-start.16 = (f32[8,128]{1,0:T(8,128)S(1)}, f32[8,128]{1,0:T(8,128)S(1)}, u32[]{:S(2)}, u32[]{:S(2)}) collective-permute-start(f32[8,128]{1,0:T(8,128)S(1)} %get-tuple-element.43.refs_2_), channel_id=1, source_target_pairs={{0,1},{1,0},{2,3},{3,2},{4,5},{5,4},{6,7},{7,6},{8,9},{9,8},{10,11... | collective-permute-start | bytes 12296 | tf_op jit(solution)/shard_map/ppermute | solution.py:237
